TPU v7x, 256 devices: a whole 4x4x8 slice. The times are simulated.
256 devices in a mesh: row: 16 (over x_hi, z), col: 8 (over x_lo, y), rep: 2 (over core).
Axes of the slice: x: 4 (x_hi: 2, x_lo: 2; x = x_hi * 2 + x_lo), y: 4, z: 8, core: 2. Of those that a mesh axis runs over, the one named last changes fastest.
Arguments:
- matrix: float32 [16384, 16384], P('row', 'col'), may hold values from -0.125 to 0.125
- vectors: float32 [64, 16384], P('rep', 'row'), may hold values from -0.3 to 0.3
Outputs:
- result: float32 [64, 16384], P('rep', 'row')
All inputs are finite; a program needn't handle non-finite values.
Results may differ from a plain program's by a relative error of at most 0.00011.
Values sent between devices are 32-bit elements; how exact they have to be, the bound alone decides.
No kernel may reach another device: no remote copies, remote signals or barrier semaphores. Data moves between devices by JAX's collectives and lax.ppermute only.
A program may use at most 64 MiB of HBM per device.

v0:
```python
import jax
import jax.numpy as jnp
from jax import lax
from jax.sharding import PartitionSpec as P

TERMS = 6
STEPS = 1


def from_root(shard, axis, root):
    return lax.dynamic_index_in_dim(lax.all_gather(shard, axis), root, 0, keepdims=False)


def copy_for_each(shard, axis):
    count = lax.axis_size(axis)
    return lax.all_to_all(
        jnp.broadcast_to(shard[None], (count, *shard.shape)), axis, 0, 0, tiled=True
    )


def over_copies(shard, axis):
    return copy_for_each(shard, axis).sum(axis=0)


def apply_matrix(current, matrix):
    fanout = lax.axis_size("row") // lax.axis_size("col")
    column_index = lax.axis_index("col")
    pieces = [from_root(current, "row", column_index * fanout + which) for which in range(fanout)]
    operand = jnp.concatenate(pieces, axis=1)
    partial_value = lax.dot_general(
        operand,
        matrix,
        (((1,), (1,)), ((), ())),
        precision=lax.Precision.HIGHEST,
        preferred_element_type=jnp.float32,
    )
    return over_copies(partial_value, "col")


def local(matrix, vectors):
    summand = vectors
    running = vectors
    for degree in range(1, TERMS + 1):
        summand = apply_matrix(summand, matrix) / float(degree * STEPS)
        running = running + summand
    return running


def solution(mesh):
    placed = (P("row", "col"), P("rep", "row"))
    return jax.shard_map(
        local, mesh=mesh, in_specs=placed, out_specs=P("rep", "row"), check_vma=False
    )
```

profile of v0, /device:TPU:2, one launch (start us, length us, event | category | flops | bytes accessed | tf_op | source)
XLA Modules:
  0.0 676.9 jit_solution(11237662189762884529)
XLA Ops:
  7.3 90.0 %all-gather.13.cloned.1.call-done = f32[512,1024]{1,0:T(8,128)} async-done(((f32[32,1024]{1,0:T(8,128)}), f32[512,1024]{1,0:T(8,128)}) %all-gather.13.cloned.1.call-update) | async-done | bytes 2097168 | tf_op jit(solution)/shard_map/all_gather | solution.py:11
  97.3 1.0 dynamic-slice_bitcast_fusion.11
  98.3 10.0 %fusion = f32[32,1024]{1,0:T(8,128)S(1)} fusion(f32[1024,2048]{1,0:T(8,128)} %param.2, f32[32,1024]{1,0:T(8,128)S(1)} %get-tuple-element.16, f32[32,1024]{1,0:T(8,128)S(1)} %get-tuple-element.15), kind=kOutput, calls=%fused_computation | convolution fusion | flops 805371904 | bytes 8781824 | tf_op jit(solution)/shard_map/dot_general | solution.py:30
  108.4 16.2 %all_to_all.30 = f32[8,32,1024]{2,1,0:T(8,128)S(1)} all-to-all(f32[8,32,1024]{2,1,0:T(8,128)S(1)} %broadcast_in_dim.12), channel_id=1, replica_groups=mesh['row'=16,'col'=8,'rep'=2] {'col'}, dimensions={0} | all-to-all | bytes 2097152 | tf_op jit(solution)/shard_map/all_to_all | solution.py:16
  125.4 80.8 %all-gather.15.cloned.1.call-done = f32[512,1024]{1,0:T(8,128)} async-done(((f32[32,1024]{1,0:T(8,128)}), f32[512,1024]{1,0:T(8,128)}) %all-gather.15.cloned.1.call-update) | async-done | bytes 2097168 | tf_op jit(solution)/shard_map/all_gather | solution.py:11
  206.2 1.0 dynamic-slice_bitcast_fusion.9
  207.2 10.0 %fusion.4 = f32[32,1024]{1,0:T(8,128)S(1)} fusion(f32[1024,2048]{1,0:T(8,128)} %param.2, f32[32,1024]{1,0:T(8,128)S(1)} %get-tuple-element.14, f32[32,1024]{1,0:T(8,128)S(1)} %get-tuple-element.13), kind=kOutput, calls=%fused_computation.4 | convolution fusion | flops 805371904 | bytes 8781824 | tf_op jit(solution)/shard_map/dot_general | solution.py:30
  217.3 16.2 %all_to_all.31 = f32[8,32,1024]{2,1,0:T(8,128)S(1)} all-to-all(f32[8,32,1024]{2,1,0:T(8,128)S(1)} %broadcast_in_dim.13), channel_id=1, replica_groups=mesh['row'=16,'col'=8,'rep'=2] {'col'}, dimensions={0} | all-to-all | bytes 2097152 | tf_op jit(solution)/shard_map/all_to_all | solution.py:16
  234.3 80.8 %all-gather.17.cloned.1.call-done = f32[512,1024]{1,0:T(8,128)} async-done(((f32[32,1024]{1,0:T(8,128)}), f32[512,1024]{1,0:T(8,128)}) %all-gather.17.cloned.1.call-update) | async-done | bytes 2097168 | tf_op jit(solution)/shard_map/all_gather | solution.py:11
  315.1 1.0 dynamic-slice_bitcast_fusion.7
  316.1 10.0 %fusion.8 = f32[32,1024]{1,0:T(8,128)S(1)} fusion(f32[1024,2048]{1,0:T(8,128)} %param.2, f32[32,1024]{1,0:T(8,128)S(1)} %get-tuple-element.12, f32[32,1024]{1,0:T(8,128)S(1)} %get-tuple-element.11), kind=kOutput, calls=%fused_computation.8 | convolution fusion | flops 805371904 | bytes 8781824 | tf_op jit(solution)/shard_map/dot_general | solution.py:30
  326.2 16.2 %all_to_all.32 = f32[8,32,1024]{2,1,0:T(8,128)S(1)} all-to-all(f32[8,32,1024]{2,1,0:T(8,128)S(1)} %broadcast_in_dim.14), channel_id=1, replica_groups=mesh['row'=16,'col'=8,'rep'=2] {'col'}, dimensions={0} | all-to-all | bytes 2097152 | tf_op jit(solution)/shard_map/all_to_all | solution.py:16
  343.4 80.7 %all-gather.19.cloned.1.call-done = f32[512,1024]{1,0:T(8,128)} async-done(((f32[32,1024]{1,0:T(8,128)}), f32[512,1024]{1,0:T(8,128)}) %all-gather.19.cloned.1.call-update) | async-done | bytes 2097168 | tf_op jit(solution)/shard_map/all_gather | solution.py:11
  424.0 1.0 dynamic-slice_bitcast_fusion.5
  425.0 10.0 %fusion.12 = f32[32,1024]{1,0:T(8,128)S(1)} fusion(f32[1024,2048]{1,0:T(8,128)} %param.2, f32[32,1024]{1,0:T(8,128)S(1)} %get-tuple-element.10, f32[32,1024]{1,0:T(8,128)S(1)} %get-tuple-element.9), kind=kOutput, calls=%fused_computation.12 | convolution fusion | flops 805371904 | bytes 8781824 | tf_op jit(solution)/shard_map/dot_general | solution.py:30
  435.1 16.2 %all_to_all.33 = f32[8,32,1024]{2,1,0:T(8,128)S(1)} all-to-all(f32[8,32,1024]{2,1,0:T(8,128)S(1)} %broadcast_in_dim.15), channel_id=1, replica_groups=mesh['row'=16,'col'=8,'rep'=2] {'col'}, dimensions={0} | all-to-all | bytes 2097152 | tf_op jit(solution)/shard_map/all_to_all | solution.py:16
  452.1 80.8 %all-gather.21.cloned.1.call-done = f32[512,1024]{1,0:T(8,128)} async-done(((f32[32,1024]{1,0:T(8,128)}), f32[512,1024]{1,0:T(8,128)}) %all-gather.21.cloned.1.call-update) | async-done | bytes 2097168 | tf_op jit(solution)/shard_map/all_gather | solution.py:11
  532.9 1.0 dynamic-slice_bitcast_fusion.3
  533.9 10.0 %fusion.16 = f32[32,1024]{1,0:T(8,128)S(1)} fusion(f32[1024,2048]{1,0:T(8,128)} %param.2, f32[32,1024]{1,0:T(8,128)S(1)} %get-tuple-element.8, f32[32,1024]{1,0:T(8,128)S(1)} %get-tuple-element.7), kind=kOutput, calls=%fused_computation.16 | convolution fusion | flops 805371904 | bytes 8781824 | tf_op jit(solution)/shard_map/dot_general | solution.py:30
  544.0 16.3 %all_to_all.34 = f32[8,32,1024]{2,1,0:T(8,128)S(1)} all-to-all(f32[8,32,1024]{2,1,0:T(8,128)S(1)} %broadcast_in_dim.16), channel_id=1, replica_groups=mesh['row'=16,'col'=8,'rep'=2] {'col'}, dimensions={0} | all-to-all | bytes 2097152 | tf_op jit(solution)/shard_map/all_to_all | solution.py:16
  561.1 80.9 %all-gather.23.cloned.1.call-done = f32[512,1024]{1,0:T(8,128)} async-done(((f32[32,1024]{1,0:T(8,128)}), f32[512,1024]{1,0:T(8,128)}) %all-gather.23.cloned.1.call-update) | async-done | bytes 2097168 | tf_op jit(solution)/shard_map/all_gather | solution.py:11
  642.0 1.0 dynamic-slice_bitcast_fusion.1
  643.0 10.0 %fusion.20 = f32[32,1024]{1,0:T(8,128)S(1)} fusion(f32[1024,2048]{1,0:T(8,128)} %param.2, f32[32,1024]{1,0:T(8,128)S(1)} %get-tuple-element.6, f32[32,1024]{1,0:T(8,128)S(1)} %get-tuple-element.5), kind=kOutput, calls=%fused_computation.20 | convolution fusion | flops 805371904 | bytes 8781824 | tf_op jit(solution)/shard_map/dot_general | solution.py:30
  653.1 16.2 %all_to_all.35 = f32[8,32,1024]{2,1,0:T(8,128)S(1)} all-to-all(f32[8,32,1024]{2,1,0:T(8,128)S(1)} %broadcast_in_dim.17), channel_id=1, replica_groups=mesh['row'=16,'col'=8,'rep'=2] {'col'}, dimensions={0} | all-to-all | bytes 2097152 | tf_op jit(solution)/shard_map/all_to_all | solution.py:16
  (33 shorter events, 6.3 us)
Async XLA Ops:
  6.5 90.8 %all-gather.13.cloned.1.call-start = ((), (), s32[]{:S(2)}) async-start(), calls=%async_computation.6 | async-start | bytes 2228224 | tf_op jit(solution)/shard_map/all_gather | solution.py:11
  7.3 199.0 %all-gather.15.cloned.1.call-start = ((), (), s32[]{:S(2)}) async-start(), calls=%async_computation.7 | async-start | bytes 2228224 | tf_op jit(solution)/shard_map/all_gather | solution.py:11
  125.3 189.8 %all-gather.17.cloned.1.call-start = ((), (), s32[]{:S(2)}) async-start(), calls=%async_computation.8 | async-start | bytes 2228224 | tf_op jit(solution)/shard_map/all_gather | solution.py:11
  234.2 189.8 %all-gather.19.cloned.1.call-start = ((), (), s32[]{:S(2)}) async-start(), calls=%async_computation.9 | async-start | bytes 2228224 | tf_op jit(solution)/shard_map/all_gather | solution.py:11
  343.1 189.8 %all-gather.21.cloned.1.call-start = ((), (), s32[]{:S(2)}) async-start(), calls=%async_computation.10 | async-start | bytes 2228224 | tf_op jit(solution)/shard_map/all_gather | solution.py:11
  452.0 190.0 %all-gather.23.cloned.1.call-start = ((), (), s32[]{:S(2)}) async-start(), calls=%async_computation.11 | async-start | bytes 2228224 | tf_op jit(solution)/shard_map/all_gather | solution.py:11
  544.0 125.3 %copy-start = (f32[32,1024]{1,0:T(8,128)S(1)}, f32[32,1024]{1,0:T(8,128)}, u32[]{:S(2)}) copy-start(f32[32,1024]{1,0:T(8,128)} %reduce_sum.54) | copy-start | bytes 393220
  544.0 125.3 %copy-start.1 = (f32[32,1024]{1,0:T(8,128)S(1)}, f32[32,1024]{1,0:T(8,128)}, u32[]{:S(2)}) copy-start(f32[32,1024]{1,0:T(8,128)} %param.3) | copy-start | bytes 393220
Sparse Core Ops, SparseCore 0:
  9.9 87.3 all-gather.12
  125.4 80.7 all-gather.14
  234.3 80.7 all-gather.16
  343.3 80.7 all-gather.18
  452.2 80.7 all-gather.20
  561.2 80.7 all-gather.22
where the time goes:
time: 677 us
  waiting for transfers between devices  495 us (73%)
  blocking collectives  97.1 us (14%)
  matrix products  59.8 us (9%)
  between operations  13.6 us (2%)
    all_gather x6, waiting for transfers between devices, from_root(): lax.all_gather(shard, axis)  494 us
    all_to_all x6, blocking collectives, copy_for_each(): lax.all_to_all(jnp.broadcast_to(shard[None], (count, *shard.shape)), axis...  97.1 us
    dot_general x6, matrix products, apply_matrix(): lax.dot_general(operand, matrix, (((1,), (1,)), ((), ())), precision=lax....  59.8 us
  transfers between devices with their start and end apart: 6, of which 6 were waited for; matrix products, arithmetic and copies ran while one was open for 0% of the time, Pallas kernels for 0%

commit v1 on v0

v1 whole, which is shorter than its diff:
```python
import functools

import jax
import jax.numpy as jnp
from jax import lax
from jax.experimental import pallas as pl
from jax.experimental.pallas import tpu as pltpu
from jax.sharding import Mesh, PartitionSpec as P

TERMS = 6
STEPS = 1

ROW = ("xh", "zh", "zl")
COL = ("xl", "y")
SIZES = {"xh": 2, "zh": 4, "zl": 2, "xl": 2, "y": 4, "rep": 2}


def owner_moves():
    def place(xh, zh, zl, xl, y):
        return (((xh * 4 + zh) * 2 + zl) * 2 + xl) * 4 + y

    return [
        (place(xh, zh, zl, xl, y), place(xl, (y + 2) % 4, zl, xh, zh))
        for xh in range(2)
        for zh in range(4)
        for zl in range(2)
        for xl in range(2)
        for y in range(4)
    ]


def split(value):
    high = value.astype(jnp.bfloat16)
    low = (value - high.astype(jnp.float32)).astype(jnp.bfloat16)
    return high, low


def prepare_kernel(a_ref, high_ref, low_ref, held, sems):
    blocks = held.shape[0]
    width = held.shape[2]

    def copy(block):
        return pltpu.make_async_copy(
            a_ref.at[:, pl.ds(pl.multiple_of(block * width, width), width)], held.at[block], sems.at[block]
        )

    for block in range(blocks):
        copy(block).start()

    def step(block, carry):
        copy(block).wait()
        high, low = split(held[block].T)
        rows = pl.ds(pl.multiple_of(block * width, width), width)
        high_ref[rows, :] = high
        low_ref[rows, :] = low
        return carry

    lax.fori_loop(0, blocks, step, 0)


def prepare(matrix):
    rows, columns = matrix.shape
    width = 256
    half = pltpu.VMEM((columns, rows), jnp.bfloat16)
    return pl.pallas_call(
        prepare_kernel,
        out_shape=(half, half),
        in_specs=[pl.BlockSpec(memory_space=pltpu.HBM)],
        out_specs=(pl.BlockSpec(memory_space=pltpu.VMEM),) * 2,
        scratch_shapes=[
            pltpu.VMEM((columns // width, rows, width), jnp.float32),
            pltpu.SemaphoreType.DMA((columns // width,)),
        ],
        cost_estimate=pl.CostEstimate(flops=4_000_000_000, bytes_accessed=8 << 20, transcendentals=0),
        compiler_params=pltpu.CompilerParams(vmem_limit_bytes=24 << 20),
    )(pltpu.with_memory_space_constraint(matrix, pltpu.HBM))


def product_tiles(x_ref, high_ref, low_ref, tile):
    pieces = [split(x_ref[piece]) for piece in range(x_ref.shape[0])]
    x_high = jnp.concatenate([high for high, _ in pieces], axis=1)
    x_low = jnp.concatenate([low for _, low in pieces], axis=1)
    both = jnp.concatenate([x_high, x_low], axis=0)
    vectors = x_high.shape[0]
    for start in range(0, high_ref.shape[1], tile):
        columns = slice(start, start + tile)
        first = jnp.dot(both, high_ref[:, columns], preferred_element_type=jnp.float32)
        second = jnp.dot(x_high, low_ref[:, columns], preferred_element_type=jnp.float32)
        yield start, first[:vectors] + (first[vectors:] + second)


def product_kernel(x_ref, high_ref, low_ref, out_ref):
    width = out_ref.shape[2]
    for start, total in product_tiles(x_ref, high_ref, low_ref, 256):
        side, within = divmod(start, width)
        for copy in range(4):
            out_ref[side * 4 + copy, :, within : within + 256] = total


def last_kernel(scale, x_ref, high_ref, low_ref, running_ref, out_ref):
    width = running_ref.shape[1]
    mine = lax.axis_index("xl")
    first = lax.axis_index("y") == 0
    for start, total in product_tiles(x_ref, high_ref, low_ref, 256):
        side, within = divmod(start, width)
        running = running_ref[:, within : within + 256]
        adds = jnp.logical_and(first, mine == side)
        total = total / scale + jnp.where(adds, running, jnp.zeros_like(running))
        for copy in range(8):
            out_ref[copy, :, start : start + 256] = total


def product(operand, halves, running=None, scale=None):
    vectors = operand.shape[1]
    rows = halves[0].shape[1]
    last = running is not None
    vmem = pl.BlockSpec(memory_space=pltpu.VMEM)
    operands = (operand, *halves) + ((running,) if last else ())
    return pl.pallas_call(
        functools.partial(last_kernel, scale) if last else product_kernel,
        out_shape=jax.ShapeDtypeStruct((8, vectors, rows if last else rows // 2), jnp.float32),
        in_specs=[vmem] * len(operands),
        out_specs=vmem,
        cost_estimate=pl.CostEstimate(flops=400_000_000, bytes_accessed=8 << 20, transcendentals=0),
        compiler_params=pltpu.CompilerParams(vmem_limit_bytes=8 << 20),
    )(*operands)


def combine_kernel(scale, parts_ref, running_ref, summand_ref, total_ref):
    summand = parts_ref[0]
    for part in range(1, parts_ref.shape[0]):
        summand = summand + parts_ref[part]
    summand = summand / scale
    summand_ref[...] = summand
    total_ref[...] = running_ref[...] + summand


def combine(parts, running, scale):
    vmem = pl.BlockSpec(memory_space=pltpu.VMEM)
    out = jax.ShapeDtypeStruct(running.shape, jnp.float32)
    return pl.pallas_call(
        functools.partial(combine_kernel, scale),
        out_shape=(out, out),
        in_specs=[vmem, vmem],
        out_specs=(vmem, vmem),
        cost_estimate=pl.CostEstimate(flops=1_000_000, bytes_accessed=1 << 19, transcendentals=0),
        compiler_params=pltpu.CompilerParams(vmem_limit_bytes=2 << 20),
    )(parts, running)


def exchange(value, axes):
    return lax.all_to_all(value, axes, 0, 0, tiled=True)


def move(piece):
    return lax.ppermute(piece, ROW + COL, owner_moves())


def gather(moved):
    return exchange(jnp.broadcast_to(moved[None], (4, *moved.shape)), ("zl", "xh"))


def local(matrix, vectors):
    half = vectors.shape[1] // 2
    running = jnp.where(lax.axis_index("xl") == 0, vectors[:, :half], vectors[:, half:])
    moved = move(running)
    halves = prepare(matrix)
    moved, halves = lax.optimization_barrier((moved, halves))
    for degree in range(1, TERMS):
        parts = exchange(product(gather(moved), halves), COL)
        summand, running = combine(parts, running, float(degree * STEPS))
        moved = move(summand)
    parts = exchange(product(gather(moved), halves, running, float(TERMS * STEPS)), COL)
    return functools.reduce(jnp.add, [parts[part] for part in range(8)])


def solution(mesh):
    fine = Mesh(mesh.devices.reshape(tuple(SIZES.values())), tuple(SIZES))
    placed = (P(ROW, COL), P("rep", ROW))
    return jax.shard_map(local, mesh=fine, in_specs=placed, out_specs=P("rep", ROW), check_vma=False)
```

time: 677 us -> 206 us (0.30)
  waiting for transfers between devices: 495 us -> 18.1 us
  matrix products: 59.8 us -> 0 us
  blocking collectives: 97.1 us -> 141 us
  starting transfers between devices: 0.39 us -> 31.1 us
  Pallas kernels: 0 us -> 13.9 us
  between operations: 13.6 us -> 0.13 us
    all_gather x6 -> x0, waiting for transfers between devices: 494 us -> none  [from_root(): lax.all_gather(shard, axis)]
    dot_general x6 -> x0, matrix products: 59.8 us -> none  [apply_matrix(): lax.dot_general(operand, matrix, (((1,), (1,)), ((), ())), precision=lax....]
    all_to_all x6 -> x12, blocking collectives: 97.1 us -> 141 us  [exchange(): return lax.all_to_all(value, axes, 0, 0, tiled=True)]
    ppermute x0 -> x6, starting transfers between devices: none -> 31.1 us  [move(): return lax.ppermute(piece, ROW + COL, owner_moves())]
    ppermute x0 -> x6, waiting for transfers between devices: none -> 18.1 us  [move(): return lax.ppermute(piece, ROW + COL, owner_moves())]
    pallas_call x0 -> x12, Pallas kernels: none -> 13.9 us  [the longest x6 9.42 us: product(): pl.pallas_call(functools.partial(last_kernel, scale) if last else product...]
  transfers between devices with their start and end apart: 6 -> 6, of which waited for: 6 -> 5; matrix products, arithmetic and copies ran while one was open for 0% -> 0% of each run, Pallas kernels for 0% -> 2%
where the time goes in v1:
time: 206 us
  blocking collectives  141 us (68%)
  starting transfers between devices  31.1 us (15%)
  waiting for transfers between devices  18.1 us (9%)
  Pallas kernels  13.9 us (7%)
    all_to_all x12, blocking collectives, exchange(): return lax.all_to_all(value, axes, 0, 0, tiled=True)  141 us
    ppermute x6, starting transfers between devices, move(): return lax.ppermute(piece, ROW + COL, owner_moves())  31.1 us
    ppermute x6, waiting for transfers between devices, move(): return lax.ppermute(piece, ROW + COL, owner_moves())  18.1 us
    pallas_call x6, Pallas kernels, product(): pl.pallas_call(functools.partial(last_kernel, scale) if last else product...  9.42 us
    pallas_call x1, Pallas kernels, prepare(): pl.pallas_call(prepare_kernel, out_shape=(half, half), in_specs=[pl.Block...  4.29 us
  transfers between devices with their start and end apart: 6, of which 5 were waited for; matrix products, arithmetic and copies ran while one was open for 0% of the time, Pallas kernels for 2%

profile of v1, /device:TPU:2, one launch (start us, length us, event | category | flops | bytes accessed | tf_op | source)
XLA Modules:
  0.0 205.7 jit_solution(6495066752217360297)
XLA Ops:
  0.9 8.2 %collective-permute-start = (f32[32,512]{1,0:T(8,128)S(1)}, f32[32,512]{1,0:T(8,128)S(1)}, u32[]{:S(2)}, u32[]{:S(2)}) collective-permute-start(f32[32,512]{1,0:T(8,128)S(1)} %slice_select_fusion.running_ref), channel_id=1, source_target_pairs={{0,64},{2,96},{4,0},{6,32},{8,192},{10,224},{12,128},{14,160},{16,... | collective-permute-start | bytes 196616 | tf_op jit(solution)/shard_map/ppermute | solution.py:156
  9.1 4.3 %shard_map.28 = (bf16[2048,1024]{1,0:T(8,128)(2,1)S(1)}, bf16[2048,1024]{1,0:T(8,128)(2,1)S(1)}) custom-call(f32[1024,2048]{1,0:T(8,128)} %a_ref.1), custom_call_target="tpu_custom_call" | custom-call | flops 4000000000 | bytes 8388608 | tf_op jit(solution)/shard_map/pallas_call | solution.py:65
  13.4 9.9 %all_to_all.60.x_ref = f32[4,32,512]{2,1,0:T(8,128)S(1)} all-to-all(f32[4,32,512]{2,1,0:T(8,128)S(1)} %broadcast_in_dim.12), channel_id=1, replica_groups=mesh['xh'=2,'zh'=4,'zl'=2,'xl'=2,'y'=4,'rep'=2] {'zl','xh'}, dimensions={0} | all-to-all | bytes 524288 | tf_op jit(solution)/shard_map/all_to_all | solution.py:152
  24.9 12.7 %all_to_all.61.parts_ref = f32[8,32,512]{2,1,0:T(8,128)S(1)} all-to-all(f32[8,32,512]{2,1,0:T(8,128)S(1)} %shard_map.29), channel_id=1, replica_groups=mesh['xh'=2,'zh'=4,'zl'=2,'xl'=2,'y'=4,'rep'=2] {'xl','y'}, dimensions={0} | all-to-all | bytes 1048576 | tf_op jit(solution)/shard_map/all_to_all | solution.py:152
  37.7 6.6 %collective-permute-start.1 = (f32[32,512]{1,0:T(8,128)S(1)}, f32[32,512]{1,0:T(8,128)S(1)}, u32[]{:S(2)}, u32[]{:S(2)}) collective-permute-start(f32[32,512]{1,0:T(8,128)S(1)} %get-tuple-element.25), channel_id=1, source_target_pairs={{0,64},{2,96},{4,0},{6,32},{8,192},{10,224},{12,128},{14,160},{16,... | collective-permute-start | bytes 196616 | tf_op jit(solution)/shard_map/ppermute | solution.py:156
  44.2 2.3 %collective-permute-done.1 = f32[32,512]{1,0:T(8,128)S(1)} collective-permute-done((f32[32,512]{1,0:T(8,128)S(1)}, f32[32,512]{1,0:T(8,128)S(1)}, u32[]{:S(2)}, u32[]{:S(2)}) %collective-permute-start.1) | collective-permute-done | bytes 65568 | tf_op jit(solution)/shard_map/ppermute | solution.py:156
  46.6 9.6 %all_to_all.62.x_ref = f32[4,32,512]{2,1,0:T(8,128)S(1)} all-to-all(f32[4,32,512]{2,1,0:T(8,128)S(1)} %broadcast_in_dim.13), channel_id=1, replica_groups=mesh['xh'=2,'zh'=4,'zl'=2,'xl'=2,'y'=4,'rep'=2] {'zl','xh'}, dimensions={0} | all-to-all | bytes 524288 | tf_op jit(solution)/shard_map/all_to_all | solution.py:152
  57.8 13.7 %all_to_all.63.parts_ref = f32[8,32,512]{2,1,0:T(8,128)S(1)} all-to-all(f32[8,32,512]{2,1,0:T(8,128)S(1)} %shard_map.31), channel_id=1, replica_groups=mesh['xh'=2,'zh'=4,'zl'=2,'xl'=2,'y'=4,'rep'=2] {'xl','y'}, dimensions={0} | all-to-all | bytes 1048576 | tf_op jit(solution)/shard_map/all_to_all | solution.py:152
  71.6 5.0 %collective-permute-start.2 = (f32[32,512]{1,0:T(8,128)S(1)}, f32[32,512]{1,0:T(8,128)S(1)}, u32[]{:S(2)}, u32[]{:S(2)}) collective-permute-start(f32[32,512]{1,0:T(8,128)S(1)} %get-tuple-element.27), channel_id=1, source_target_pairs={{0,64},{2,96},{4,0},{6,32},{8,192},{10,224},{12,128},{14,160},{16,... | collective-permute-start | bytes 196616 | tf_op jit(solution)/shard_map/ppermute | solution.py:156
  76.5 5.3 %collective-permute-done.2 = f32[32,512]{1,0:T(8,128)S(1)} collective-permute-done((f32[32,512]{1,0:T(8,128)S(1)}, f32[32,512]{1,0:T(8,128)S(1)}, u32[]{:S(2)}, u32[]{:S(2)}) %collective-permute-start.2) | collective-permute-done | bytes 65568 | tf_op jit(solution)/shard_map/ppermute | solution.py:156
  81.8 9.6 %all_to_all.64.x_ref = f32[4,32,512]{2,1,0:T(8,128)S(1)} all-to-all(f32[4,32,512]{2,1,0:T(8,128)S(1)} %broadcast_in_dim.14), channel_id=1, replica_groups=mesh['xh'=2,'zh'=4,'zl'=2,'xl'=2,'y'=4,'rep'=2] {'zl','xh'}, dimensions={0} | all-to-all | bytes 524288 | tf_op jit(solution)/shard_map/all_to_all | solution.py:152
  93.0 10.3 %all_to_all.65.parts_ref = f32[8,32,512]{2,1,0:T(8,128)S(1)} all-to-all(f32[8,32,512]{2,1,0:T(8,128)S(1)} %shard_map.33), channel_id=1, replica_groups=mesh['xh'=2,'zh'=4,'zl'=2,'xl'=2,'y'=4,'rep'=2] {'xl','y'}, dimensions={0} | all-to-all | bytes 1048576 | tf_op jit(solution)/shard_map/all_to_all | solution.py:152
  103.4 4.8 %collective-permute-start.3 = (f32[32,512]{1,0:T(8,128)S(1)}, f32[32,512]{1,0:T(8,128)S(1)}, u32[]{:S(2)}, u32[]{:S(2)}) collective-permute-start(f32[32,512]{1,0:T(8,128)S(1)} %get-tuple-element.29), channel_id=1, source_target_pairs={{0,64},{2,96},{4,0},{6,32},{8,192},{10,224},{12,128},{14,160},{16,... | collective-permute-start | bytes 196616 | tf_op jit(solution)/shard_map/ppermute | solution.py:156
  108.2 1.9 collective-permute-done.3
  110.2 9.6 %all_to_all.66.x_ref = f32[4,32,512]{2,1,0:T(8,128)S(1)} all-to-all(f32[4,32,512]{2,1,0:T(8,128)S(1)} %broadcast_in_dim.15), channel_id=1, replica_groups=mesh['xh'=2,'zh'=4,'zl'=2,'xl'=2,'y'=4,'rep'=2] {'zl','xh'}, dimensions={0} | all-to-all | bytes 524288 | tf_op jit(solution)/shard_map/all_to_all | solution.py:152
  121.4 16.4 %all_to_all.67.parts_ref = f32[8,32,512]{2,1,0:T(8,128)S(1)} all-to-all(f32[8,32,512]{2,1,0:T(8,128)S(1)} %shard_map.35), channel_id=1, replica_groups=mesh['xh'=2,'zh'=4,'zl'=2,'xl'=2,'y'=4,'rep'=2] {'xl','y'}, dimensions={0} | all-to-all | bytes 1048576 | tf_op jit(solution)/shard_map/all_to_all | solution.py:152
  137.8 2.0 collective-permute-start.4
  139.8 5.4 %collective-permute-done.4 = f32[32,512]{1,0:T(8,128)S(1)} collective-permute-done((f32[32,512]{1,0:T(8,128)S(1)}, f32[32,512]{1,0:T(8,128)S(1)}, u32[]{:S(2)}, u32[]{:S(2)}) %collective-permute-start.4) | collective-permute-done | bytes 65568 | tf_op jit(solution)/shard_map/ppermute | solution.py:156
  145.3 9.6 %all_to_all.68.x_ref = f32[4,32,512]{2,1,0:T(8,128)S(1)} all-to-all(f32[4,32,512]{2,1,0:T(8,128)S(1)} %broadcast_in_dim.16), channel_id=1, replica_groups=mesh['xh'=2,'zh'=4,'zl'=2,'xl'=2,'y'=4,'rep'=2] {'zl','xh'}, dimensions={0} | all-to-all | bytes 524288 | tf_op jit(solution)/shard_map/all_to_all | solution.py:152
  156.5 13.3 %all_to_all.69.parts_ref = f32[8,32,512]{2,1,0:T(8,128)S(1)} all-to-all(f32[8,32,512]{2,1,0:T(8,128)S(1)} %shard_map.37), channel_id=1, replica_groups=mesh['xh'=2,'zh'=4,'zl'=2,'xl'=2,'y'=4,'rep'=2] {'xl','y'}, dimensions={0} | all-to-all | bytes 1048576 | tf_op jit(solution)/shard_map/all_to_all | solution.py:152
  169.8 4.6 %collective-permute-start.5 = (f32[32,512]{1,0:T(8,128)S(1)}, f32[32,512]{1,0:T(8,128)S(1)}, u32[]{:S(2)}, u32[]{:S(2)}) collective-permute-start(f32[32,512]{1,0:T(8,128)S(1)} %get-tuple-element.33), channel_id=1, source_target_pairs={{0,64},{2,96},{4,0},{6,32},{8,192},{10,224},{12,128},{14,160},{16,... | collective-permute-start | bytes 196616 | tf_op jit(solution)/shard_map/ppermute | solution.py:156
  174.3 3.1 %collective-permute-done.5 = f32[32,512]{1,0:T(8,128)S(1)} collective-permute-done((f32[32,512]{1,0:T(8,128)S(1)}, f32[32,512]{1,0:T(8,128)S(1)}, u32[]{:S(2)}, u32[]{:S(2)}) %collective-permute-start.5) | collective-permute-done | bytes 65568 | tf_op jit(solution)/shard_map/ppermute | solution.py:156
  177.4 9.8 %all_to_all.70.x_ref = f32[4,32,512]{2,1,0:T(8,128)S(1)} all-to-all(f32[4,32,512]{2,1,0:T(8,128)S(1)} %broadcast_in_dim.17), channel_id=1, replica_groups=mesh['xh'=2,'zh'=4,'zl'=2,'xl'=2,'y'=4,'rep'=2] {'zl','xh'}, dimensions={0} | all-to-all | bytes 524288 | tf_op jit(solution)/shard_map/all_to_all | solution.py:152
  188.8 16.2 %all_to_all.71 = f32[8,32,1024]{2,1,0:T(8,128)S(1)} all-to-all(f32[8,32,1024]{2,1,0:T(8,128)S(1)} %shard_map.39), channel_id=1, replica_groups=mesh['xh'=2,'zh'=4,'zl'=2,'xl'=2,'y'=4,'rep'=2] {'xl','y'}, dimensions={0} | all-to-all | bytes 2097152 | tf_op jit(solution)/shard_map/all_to_all | solution.py:152
  (20 shorter events, 11.3 us)
Async XLA Ops:
  0.9 12.5 %collective-permute-start = (f32[32,512]{1,0:T(8,128)S(1)}, f32[32,512]{1,0:T(8,128)S(1)}, u32[]{:S(2)}, u32[]{:S(2)}) collective-permute-start(f32[32,512]{1,0:T(8,128)S(1)} %slice_select_fusion.running_ref), channel_id=1, source_target_pairs={{0,64},{2,96},{4,0},{6,32},{8,192},{10,224},{12,128},{14,160},{16,... | collective-permute-start | bytes 196616 | tf_op jit(solution)/shard_map/ppermute | solution.py:156
  37.7 8.9 %collective-permute-start.1 = (f32[32,512]{1,0:T(8,128)S(1)}, f32[32,512]{1,0:T(8,128)S(1)}, u32[]{:S(2)}, u32[]{:S(2)}) collective-permute-start(f32[32,512]{1,0:T(8,128)S(1)} %get-tuple-element.25), channel_id=1, source_target_pairs={{0,64},{2,96},{4,0},{6,32},{8,192},{10,224},{12,128},{14,160},{16,... | collective-permute-start | bytes 196616 | tf_op jit(solution)/shard_map/ppermute | solution.py:156
  71.6 10.3 %collective-permute-start.2 = (f32[32,512]{1,0:T(8,128)S(1)}, f32[32,512]{1,0:T(8,128)S(1)}, u32[]{:S(2)}, u32[]{:S(2)}) collective-permute-start(f32[32,512]{1,0:T(8,128)S(1)} %get-tuple-element.27), channel_id=1, source_target_pairs={{0,64},{2,96},{4,0},{6,32},{8,192},{10,224},{12,128},{14,160},{16,... | collective-permute-start | bytes 196616 | tf_op jit(solution)/shard_map/ppermute | solution.py:156
  103.4 6.7 %collective-permute-start.3 = (f32[32,512]{1,0:T(8,128)S(1)}, f32[32,512]{1,0:T(8,128)S(1)}, u32[]{:S(2)}, u32[]{:S(2)}) collective-permute-start(f32[32,512]{1,0:T(8,128)S(1)} %get-tuple-element.29), channel_id=1, source_target_pairs={{0,64},{2,96},{4,0},{6,32},{8,192},{10,224},{12,128},{14,160},{16,... | collective-permute-start | bytes 196616 | tf_op jit(solution)/shard_map/ppermute | solution.py:156
  137.8 7.4 %collective-permute-start.4 = (f32[32,512]{1,0:T(8,128)S(1)}, f32[32,512]{1,0:T(8,128)S(1)}, u32[]{:S(2)}, u32[]{:S(2)}) collective-permute-start(f32[32,512]{1,0:T(8,128)S(1)} %get-tuple-element.31), channel_id=1, source_target_pairs={{0,64},{2,96},{4,0},{6,32},{8,192},{10,224},{12,128},{14,160},{16,... | collective-permute-start | bytes 196616 | tf_op jit(solution)/shard_map/ppermute | solution.py:156
  169.8 7.7 %collective-permute-start.5 = (f32[32,512]{1,0:T(8,128)S(1)}, f32[32,512]{1,0:T(8,128)S(1)}, u32[]{:S(2)}, u32[]{:S(2)}) collective-permute-start(f32[32,512]{1,0:T(8,128)S(1)} %get-tuple-element.33), channel_id=1, source_target_pairs={{0,64},{2,96},{4,0},{6,32},{8,192},{10,224},{12,128},{14,160},{16,... | collective-permute-start | bytes 196616 | tf_op jit(solution)/shard_map/ppermute | solution.py:156

commit v2 on v1

--- a/solution.py
+++ b/solution.py
@@ -160,7 +160,7 @@
     return exchange(jnp.broadcast_to(moved[None], (4, *moved.shape)), ("zl", "xh"))
 
 
-def local(matrix, vectors):
+def series(matrix, vectors):
     half = vectors.shape[1] // 2
     running = jnp.where(lax.axis_index("xl") == 0, vectors[:, :half], vectors[:, half:])
     moved = move(running)
@@ -174,6 +174,15 @@
     return functools.reduce(jnp.add, [parts[part] for part in range(8)])
 
 
+def local(matrix, vectors):
+    count = vectors.shape[0]
+    other = lax.ppermute(vectors, "rep", [(0, 1)])
+    both = jnp.concatenate([other, vectors], axis=0)
+    result = lax.cond(lax.axis_index("rep") == 1, series, lambda matrix, both: both, matrix, both)
+    back = lax.ppermute(result[:count], "rep", [(1, 0)])
+    return jnp.where(lax.axis_index("rep") == 1, result[count:], back)
+
+
 def solution(mesh):
     fine = Mesh(mesh.devices.reshape(tuple(SIZES.values())), tuple(SIZES))
     placed = (P(ROW, COL), P("rep", ROW))

time: 206 us -> 226 us (1.097); the launches traced: 206 us -> 223 us
  waiting for transfers between devices: 18.1 us -> 219 us
  blocking collectives: 141 us -> 0 us
  starting transfers between devices: 31.1 us -> 3.03 us
  Pallas kernels: 13.9 us -> 0 us
    ppermute x6 -> x2, waiting for transfers between devices: 18.1 us -> 219 us  [the longest x1 218 us: local(): back = lax.ppermute(result[:count], 'rep', [(1, 0)])]
    all_to_all x12 -> x0, blocking collectives: 141 us -> none  [exchange(): return lax.all_to_all(value, axes, 0, 0, tiled=True)]
    ppermute x6 -> x2, starting transfers between devices: 31.1 us -> 3.03 us  [the longest x1 1.74 us: local(): other = lax.ppermute(vectors, 'rep', [(0, 1)])]
    pallas_call x12 -> x0, Pallas kernels: 13.9 us -> none  [the longest x6 9.42 us: product(): pl.pallas_call(functools.partial(last_kernel, scale) if last else product...]
  transfers between devices with their start and end apart: 6 -> 2, of which waited for: 5 -> 2; matrix products, arithmetic and copies ran while one was open for 0% -> 0% of each run, Pallas kernels for 2% -> 0%
where the time goes in v2:
time: 226 us; the launch traced here: 223 us
  waiting for transfers between devices  219 us (97%)
  starting transfers between devices  3.03 us (1%)
    ppermute x1, waiting for transfers between devices, local(): back = lax.ppermute(result[:count], 'rep', [(1, 0)])  218 us
  transfers between devices with their start and end apart: 2, of which 2 were waited for; matrix products, arithmetic and copies ran while one was open for 0% of the time, Pallas kernels for 0%

profile of v2, /device:TPU:2, one launch (start us, length us, event | category | flops | bytes accessed | tf_op | source)
XLA Modules:
  0.0 223.4 jit_solution(2062142024616589778)
XLA Ops:
  0.0 1.7 collective-permute-start.6
  1.7 1.2 collective-permute-done.6
  2.9 0.9 constant_dynamic-update-slice_fusion
  3.9 1.3 collective-permute-start.7
  5.2 217.5 %collective-permute-done.7 = f32[32,1024]{1,0:T(8,128)S(1)} collective-permute-done((f32[32,1024]{1,0:T(8,128)S(1)}, f32[32,1024]{1,0:T(8,128)S(1)}, u32[]{:S(2)}, u32[]{:S(2)}) %collective-permute-start.7) | collective-permute-done | bytes 131104 | tf_op jit(solution)/shard_map/ppermute | solution.py:182
  222.7 0.7 slice_select_fusion.1
  (3 shorter events, 0.0 us)
Async XLA Ops:
  0.0 2.9 %collective-permute-start.6 = (f32[32,1024]{1,0:T(8,128)}, f32[32,1024]{1,0:T(8,128)S(1)}, u32[]{:S(2)}, u32[]{:S(2)}) collective-permute-start(f32[32,1024]{1,0:T(8,128)} %param.5), channel_id=1, source_target_pairs={{0,1},{2,3},{4,5},{6,7},{8,9},{10,11},{12,13},{14,15},{16,17},{18,... | collective-permute-start | bytes 393224 | tf_op jit(solution)/shard_map/ppermute | solution.py:179
  3.9 218.8 %collective-permute-start.7 = (f32[32,1024]{1,0:T(8,128)S(1)}, f32[32,1024]{1,0:T(8,128)S(1)}, u32[]{:S(2)}, u32[]{:S(2)}) collective-permute-start(f32[32,1024]{1,0:T(8,128)S(1)} %slice.47), channel_id=1, source_target_pairs={{1,0},{3,2},{5,4},{7,6},{9,8},{11,10},{13,12},{15,14},{17,16},{19,... | collective-permute-start | bytes 393224 | tf_op jit(solution)/shard_map/ppermute | solution.py:182

commit v3 on v1

v3 whole, which is shorter than its diff:
```python
import functools

import jax
import jax.numpy as jnp
from jax import lax
from jax.experimental import pallas as pl
from jax.experimental.pallas import tpu as pltpu
from jax.sharding import Mesh, PartitionSpec as P

TERMS = 6
STEPS = 1

ROW = ("xh", "zh", "zl")
COL = ("xl", "y")
SIZES = {"xh": 2, "zh": 4, "zl": 2, "xl": 2, "y": 4, "rep": 2}
PLACES = [
    (xh, zh, zl, xl, y)
    for xh in range(2)
    for zh in range(4)
    for zl in range(2)
    for xl in range(2)
    for y in range(4)
]
FAR = 2


def index(xh, zh, zl, xl, y):
    return (((xh * 4 + zh) * 2 + zl) * 2 + xl) * 4 + y


def owner_moves():
    return [
        (index(xh, zh, zl, xl, y), index(xl, (y + FAR) % 4, zl ^ int(y == zh), xh, zh))
        for xh, zh, zl, xl, y in PLACES
    ]


def neighbour_moves():
    return [(index(xh, zh, zl, xl, y), index(xh, zh, 1 - zl, xl, y)) for xh, zh, zl, xl, y in PLACES]


def split(value):
    high = value.astype(jnp.bfloat16)
    low = (value - high.astype(jnp.float32)).astype(jnp.bfloat16)
    return high, low


def prepare_kernel(a_ref, high_ref, low_ref, held, sems):
    blocks = held.shape[0]
    width = held.shape[2]
    swapped = lax.rem(lax.axis_index("y") + FAR, 4) == lax.axis_index("zh")
    mine = lax.axis_index("zl") ^ swapped.astype(jnp.int32)

    def copy(block):
        column = pl.multiple_of(block * width, width)
        return pltpu.make_async_copy(a_ref.at[:, pl.ds(column, width)], held.at[block], sems.at[block])

    for block in range(blocks):
        copy(block).start()

    def step(block, carry):
        copy(block).wait()
        high, low = split(held[block].T)
        place = lax.rem(block + mine * (blocks // 2), blocks)
        rows = pl.ds(pl.multiple_of(place * width, width), width)
        high_ref[rows, :] = high
        low_ref[rows, :] = low
        return carry

    lax.fori_loop(0, blocks, step, 0)


def prepare(matrix):
    rows, columns = matrix.shape
    width = 256
    half = pltpu.VMEM((columns, rows), jnp.bfloat16)
    return pl.pallas_call(
        prepare_kernel,
        out_shape=(half, half),
        in_specs=[pl.BlockSpec(memory_space=pltpu.HBM)],
        out_specs=(pl.BlockSpec(memory_space=pltpu.VMEM),) * 2,
        scratch_shapes=[
            pltpu.VMEM((columns // width, rows, width), jnp.float32),
            pltpu.SemaphoreType.DMA((columns // width,)),
        ],
        cost_estimate=pl.CostEstimate(flops=4_000_000_000, bytes_accessed=8 << 20, transcendentals=0),
        compiler_params=pltpu.CompilerParams(vmem_limit_bytes=24 << 20),
    )(pltpu.with_memory_space_constraint(matrix, pltpu.HBM))


def half_product(x_ref, high_ref, low_ref, which):
    x_high, x_low = split(x_ref[...])
    both = jnp.concatenate([x_high, x_low], axis=0)
    vectors, depth = x_high.shape
    rows = slice(which * depth, (which + 1) * depth)
    for start in range(0, high_ref.shape[1], 256):
        columns = slice(start, start + 256)
        first = jnp.dot(both, high_ref[rows, columns], preferred_element_type=jnp.float32)
        second = jnp.dot(x_high, low_ref[rows, columns], preferred_element_type=jnp.float32)
        yield columns, first[:vectors] + (first[vectors:] + second)


def first_kernel(x_ref, high_ref, low_ref, out_ref):
    for columns, total in half_product(x_ref, high_ref, low_ref, 0):
        out_ref[:, columns] = total


def second_kernel(x_ref, high_ref, low_ref, before_ref, out_ref):
    for columns, total in half_product(x_ref, high_ref, low_ref, 1):
        total = before_ref[:, columns] + total
        for copy in range(out_ref.shape[0]):
            out_ref[copy, :, columns] = total


def combine_kernel(scale, parts_ref, running_ref, summand_ref, total_ref):
    summand = parts_ref[0]
    for part in range(1, parts_ref.shape[0]):
        summand = summand + parts_ref[part]
    summand = summand / scale
    summand_ref[...] = summand
    total_ref[...] = running_ref[...] + summand


def call(kernel, out, flops, limit, *operands):
    vmem = pl.BlockSpec(memory_space=pltpu.VMEM)
    shapes = jax.tree.map(lambda shape: jax.ShapeDtypeStruct(shape, jnp.float32), out, is_leaf=lambda o: isinstance(o[0], int))
    return pl.pallas_call(
        kernel,
        out_shape=shapes,
        in_specs=[vmem] * len(operands),
        out_specs=jax.tree.map(lambda _: vmem, shapes),
        cost_estimate=pl.CostEstimate(flops=flops, bytes_accessed=4 << 20, transcendentals=0),
        compiler_params=pltpu.CompilerParams(vmem_limit_bytes=limit),
    )(*operands)


def product(block, halves):
    shape = block.shape
    other = lax.ppermute(block, ROW + COL, neighbour_moves())
    before = call(first_kernel, shape, 200_000_000, 4 << 20, block, *halves)
    return call(second_kernel, (8, *shape), 200_000_000, 4 << 20, other, *halves, before)


def local(matrix, vectors):
    shape = vectors.shape
    block = lax.ppermute(vectors, ROW + COL, owner_moves())
    halves = prepare(matrix)
    block, halves = lax.optimization_barrier((block, halves))
    running = vectors
    for degree in range(1, TERMS + 1):
        parts = lax.all_to_all(product(block, halves), COL, 0, 0, tiled=True)
        kernel = functools.partial(combine_kernel, float(degree * STEPS))
        summand, running = call(kernel, (shape, shape), 1_000_000, 2 << 20, parts, running)
        if degree < TERMS:
            block = lax.ppermute(summand, ROW + COL, owner_moves())
    return running


def solution(mesh):
    fine = Mesh(mesh.devices.reshape(tuple(SIZES.values())), tuple(SIZES))
    placed = (P(ROW, COL), P("rep", ROW))
    return jax.shard_map(local, mesh=fine, in_specs=placed, out_specs=P("rep", ROW), check_vma=False)
```

time: 206 us -> 219 us (1.063)
  the two profiles are of different devices: /device:TPU:2 before, /device:TPU:64 now
where the time goes in v3:
time: 219 us
  blocking collectives  116 us (53%)
  waiting for transfers between devices  60 us (27%)
  starting transfers between devices  27.2 us (12%)
  Pallas kernels  15.3 us (7%)
    all_to_all x6, blocking collectives, local(): parts = lax.all_to_all(product(block, halves), COL, 0, 0, tiled=True)  116 us
    ppermute x5, waiting for transfers between devices, local(): block = lax.ppermute(summand, ROW + COL, owner_moves())  43.7 us
    ppermute x6, waiting for transfers between devices, product(): other = lax.ppermute(block, ROW + COL, neighbour_moves())  14.8 us
    ppermute x6, starting transfers between devices, product(): other = lax.ppermute(block, ROW + COL, neighbour_moves())  13.7 us
    pallas_call x18, Pallas kernels, call(): pl.pallas_call(kernel, out_shape=shapes, in_specs=[vmem] * len(operands),...  11 us
    ppermute x5, starting transfers between devices, local(): block = lax.ppermute(summand, ROW + COL, owner_moves())  7.94 us
    ppermute x1, starting transfers between devices, local(): block = lax.ppermute(vectors, ROW + COL, owner_moves())  5.49 us
  transfers between devices with their start and end apart: 12, of which 12 were waited for; matrix products, arithmetic and copies ran while one was open for 0% of the time, Pallas kernels for 4%

profile of v3, /device:TPU:64, one launch (start us, length us, event | category | flops | bytes accessed | tf_op | source)
XLA Modules:
  0.0 219.1 jit_solution(7584092482801454565)
XLA Ops:
  0.0 5.5 %collective-permute-start = (f32[32,1024]{1,0:T(8,128)}, f32[32,1024]{1,0:T(8,128)S(1)}, u32[]{:S(2)}, u32[]{:S(2)}) collective-permute-start(f32[32,1024]{1,0:T(8,128)} %running_ref.1), channel_id=1, source_target_pairs={{0,80},{2,96},{4,0},{6,32},{8,208},{10,224},{12,128},{14,160},{16,... | collective-permute-start | bytes 393224 | tf_op jit(solution)/shard_map/ppermute | solution.py:146
  5.5 4.3 %shard_map.28 = (bf16[2048,1024]{1,0:T(8,128)(2,1)S(1)}, bf16[2048,1024]{1,0:T(8,128)(2,1)S(1)}) custom-call(f32[1024,2048]{1,0:T(8,128)} %a_ref.1), custom_call_target="tpu_custom_call" | custom-call | flops 4000000000 | bytes 8388608 | tf_op jit(solution)/shard_map/pallas_call | solution.py:77
  11.4 4.3 %collective-permute-start.1 = (f32[32,1024]{1,0:T(8,128)S(1)}, f32[32,1024]{1,0:T(8,128)S(1)}, u32[]{:S(2)}, u32[]{:S(2)}) collective-permute-start(f32[32,1024]{1,0:T(8,128)S(1)} %collective-permute-done.x_ref), channel_id=1, source_target_pairs={{0,16},{2,18},{4,20},{6,22},{8,24},{10,26},{12,28},{14,30},{16,0},... | collective-permute-start | bytes 393224 | tf_op jit(solution)/shard_map/ppermute | solution.py:139
  16.5 2.8 %collective-permute-done.1.x_ref = f32[32,1024]{1,0:T(8,128)S(1)} collective-permute-done((f32[32,1024]{1,0:T(8,128)S(1)}, f32[32,1024]{1,0:T(8,128)S(1)}, u32[]{:S(2)}, u32[]{:S(2)}) %collective-permute-start.1) | collective-permute-done | bytes 131104 | tf_op jit(solution)/shard_map/ppermute | solution.py:139
  20.1 20.3 %all_to_all.30.parts_ref = f32[8,32,1024]{2,1,0:T(8,128)S(1)} all-to-all(f32[8,32,1024]{2,1,0:T(8,128)S(1)} %shard_map.30), channel_id=1, replica_groups=mesh['xh'=2,'zh'=4,'zl'=2,'xl'=2,'y'=4,'rep'=2] {'xl','y'}, dimensions={0} | all-to-all | bytes 2097152 | tf_op jit(solution)/shard_map/all_to_all | solution.py:151
  40.5 4.8 %collective-permute-start.2 = (f32[32,1024]{1,0:T(8,128)S(1)}, f32[32,1024]{1,0:T(8,128)S(1)}, u32[]{:S(2)}, u32[]{:S(2)}) collective-permute-start(f32[32,1024]{1,0:T(8,128)S(1)} %get-tuple-element.26), channel_id=1, source_target_pairs={{0,80},{2,96},{4,0},{6,32},{8,208},{10,224},{12,128},{14,160},{16,... | collective-permute-start | bytes 393224 | tf_op jit(solution)/shard_map/ppermute | solution.py:155
  45.3 4.8 %collective-permute-done.2.x_ref = f32[32,1024]{1,0:T(8,128)S(1)} collective-permute-done((f32[32,1024]{1,0:T(8,128)S(1)}, f32[32,1024]{1,0:T(8,128)S(1)}, u32[]{:S(2)}, u32[]{:S(2)}) %collective-permute-start.2) | collective-permute-done | bytes 131104 | tf_op jit(solution)/shard_map/ppermute | solution.py:155
  50.0 2.8 %collective-permute-start.3 = (f32[32,1024]{1,0:T(8,128)S(1)}, f32[32,1024]{1,0:T(8,128)S(1)}, u32[]{:S(2)}, u32[]{:S(2)}) collective-permute-start(f32[32,1024]{1,0:T(8,128)S(1)} %collective-permute-done.2.x_ref), channel_id=1, source_target_pairs={{0,16},{2,18},{4,20},{6,22},{8,24},{10,26},{12,28},{14,30},{16,0},... | collective-permute-start | bytes 393224 | tf_op jit(solution)/shard_map/ppermute | solution.py:139
  53.6 2.1 collective-permute-done.3.x_ref
  56.6 19.6 %all_to_all.31.parts_ref = f32[8,32,1024]{2,1,0:T(8,128)S(1)} all-to-all(f32[8,32,1024]{2,1,0:T(8,128)S(1)} %shard_map.33), channel_id=1, replica_groups=mesh['xh'=2,'zh'=4,'zl'=2,'xl'=2,'y'=4,'rep'=2] {'xl','y'}, dimensions={0} | all-to-all | bytes 2097152 | tf_op jit(solution)/shard_map/all_to_all | solution.py:151
  76.2 2.9 %collective-permute-start.4 = (f32[32,1024]{1,0:T(8,128)S(1)}, f32[32,1024]{1,0:T(8,128)S(1)}, u32[]{:S(2)}, u32[]{:S(2)}) collective-permute-start(f32[32,1024]{1,0:T(8,128)S(1)} %get-tuple-element.28), channel_id=1, source_target_pairs={{0,80},{2,96},{4,0},{6,32},{8,208},{10,224},{12,128},{14,160},{16,... | collective-permute-start | bytes 393224 | tf_op jit(solution)/shard_map/ppermute | solution.py:155
  79.1 7.7 %collective-permute-done.4.x_ref = f32[32,1024]{1,0:T(8,128)S(1)} collective-permute-done((f32[32,1024]{1,0:T(8,128)S(1)}, f32[32,1024]{1,0:T(8,128)S(1)}, u32[]{:S(2)}, u32[]{:S(2)}) %collective-permute-start.4) | collective-permute-done | bytes 131104 | tf_op jit(solution)/shard_map/ppermute | solution.py:155
  89.1 2.7 %collective-permute-done.5.x_ref = f32[32,1024]{1,0:T(8,128)S(1)} collective-permute-done((f32[32,1024]{1,0:T(8,128)S(1)}, f32[32,1024]{1,0:T(8,128)S(1)}, u32[]{:S(2)}, u32[]{:S(2)}) %collective-permute-start.5) | collective-permute-done | bytes 131104 | tf_op jit(solution)/shard_map/ppermute | solution.py:139
  92.6 18.9 %all_to_all.32.parts_ref = f32[8,32,1024]{2,1,0:T(8,128)S(1)} all-to-all(f32[8,32,1024]{2,1,0:T(8,128)S(1)} %shard_map.36), channel_id=1, replica_groups=mesh['xh'=2,'zh'=4,'zl'=2,'xl'=2,'y'=4,'rep'=2] {'xl','y'}, dimensions={0} | all-to-all | bytes 2097152 | tf_op jit(solution)/shard_map/all_to_all | solution.py:151
  111.7 10.4 %collective-permute-done.6.x_ref = f32[32,1024]{1,0:T(8,128)S(1)} collective-permute-done((f32[32,1024]{1,0:T(8,128)S(1)}, f32[32,1024]{1,0:T(8,128)S(1)}, u32[]{:S(2)}, u32[]{:S(2)}) %collective-permute-start.6) | collective-permute-done | bytes 131104 | tf_op jit(solution)/shard_map/ppermute | solution.py:155
  122.0 1.8 collective-permute-start.7
  124.7 2.3 %collective-permute-done.7.x_ref = f32[32,1024]{1,0:T(8,128)S(1)} collective-permute-done((f32[32,1024]{1,0:T(8,128)S(1)}, f32[32,1024]{1,0:T(8,128)S(1)}, u32[]{:S(2)}, u32[]{:S(2)}) %collective-permute-start.7) | collective-permute-done | bytes 131104 | tf_op jit(solution)/shard_map/ppermute | solution.py:139
  127.9 19.4 %all_to_all.33.parts_ref = f32[8,32,1024]{2,1,0:T(8,128)S(1)} all-to-all(f32[8,32,1024]{2,1,0:T(8,128)S(1)} %shard_map.39), channel_id=1, replica_groups=mesh['xh'=2,'zh'=4,'zl'=2,'xl'=2,'y'=4,'rep'=2] {'xl','y'}, dimensions={0} | all-to-all | bytes 2097152 | tf_op jit(solution)/shard_map/all_to_all | solution.py:151
  147.4 10.5 %collective-permute-done.8.x_ref = f32[32,1024]{1,0:T(8,128)S(1)} collective-permute-done((f32[32,1024]{1,0:T(8,128)S(1)}, f32[32,1024]{1,0:T(8,128)S(1)}, u32[]{:S(2)}, u32[]{:S(2)}) %collective-permute-start.8) | collective-permute-done | bytes 131104 | tf_op jit(solution)/shard_map/ppermute | solution.py:155
  160.2 2.6 %collective-permute-done.9.x_ref = f32[32,1024]{1,0:T(8,128)S(1)} collective-permute-done((f32[32,1024]{1,0:T(8,128)S(1)}, f32[32,1024]{1,0:T(8,128)S(1)}, u32[]{:S(2)}, u32[]{:S(2)}) %collective-permute-start.9) | collective-permute-done | bytes 131104 | tf_op jit(solution)/shard_map/ppermute | solution.py:139
  163.7 18.9 %all_to_all.34.parts_ref = f32[8,32,1024]{2,1,0:T(8,128)S(1)} all-to-all(f32[8,32,1024]{2,1,0:T(8,128)S(1)} %shard_map.42), channel_id=1, replica_groups=mesh['xh'=2,'zh'=4,'zl'=2,'xl'=2,'y'=4,'rep'=2] {'xl','y'}, dimensions={0} | all-to-all | bytes 2097152 | tf_op jit(solution)/shard_map/all_to_all | solution.py:151
  182.7 10.4 %collective-permute-done.10.x_ref = f32[32,1024]{1,0:T(8,128)S(1)} collective-permute-done((f32[32,1024]{1,0:T(8,128)S(1)}, f32[32,1024]{1,0:T(8,128)S(1)}, u32[]{:S(2)}, u32[]{:S(2)}) %collective-permute-start.10) | collective-permute-done | bytes 131104 | tf_op jit(solution)/shard_map/ppermute | solution.py:155
  195.8 2.3 %collective-permute-done.11.x_ref = f32[32,1024]{1,0:T(8,128)S(1)} collective-permute-done((f32[32,1024]{1,0:T(8,128)S(1)}, f32[32,1024]{1,0:T(8,128)S(1)}, u32[]{:S(2)}, u32[]{:S(2)}) %collective-permute-start.11) | collective-permute-done | bytes 131104 | tf_op jit(solution)/shard_map/ppermute | solution.py:139
  199.0 19.4 %all_to_all.35.parts_ref = f32[8,32,1024]{2,1,0:T(8,128)S(1)} all-to-all(f32[8,32,1024]{2,1,0:T(8,128)S(1)} %shard_map.45), channel_id=1, replica_groups=mesh['xh'=2,'zh'=4,'zl'=2,'xl'=2,'y'=4,'rep'=2] {'xl','y'}, dimensions={0} | all-to-all | bytes 2097152 | tf_op jit(solution)/shard_map/all_to_all | solution.py:151
  (27 shorter events, 17.7 us)
Async XLA Ops:
  0.0 11.4 %collective-permute-start = (f32[32,1024]{1,0:T(8,128)}, f32[32,1024]{1,0:T(8,128)S(1)}, u32[]{:S(2)}, u32[]{:S(2)}) collective-permute-start(f32[32,1024]{1,0:T(8,128)} %running_ref.1), channel_id=1, source_target_pairs={{0,80},{2,96},{4,0},{6,32},{8,208},{10,224},{12,128},{14,160},{16,... | collective-permute-start | bytes 393224 | tf_op jit(solution)/shard_map/ppermute | solution.py:146
  11.4 7.8 %collective-permute-start.1 = (f32[32,1024]{1,0:T(8,128)S(1)}, f32[32,1024]{1,0:T(8,128)S(1)}, u32[]{:S(2)}, u32[]{:S(2)}) collective-permute-start(f32[32,1024]{1,0:T(8,128)S(1)} %collective-permute-done.x_ref), channel_id=1, source_target_pairs={{0,16},{2,18},{4,20},{6,22},{8,24},{10,26},{12,28},{14,30},{16,0},... | collective-permute-start | bytes 393224 | tf_op jit(solution)/shard_map/ppermute | solution.py:139
  16.5 23.9 %copy-start = (f32[32,1024]{1,0:T(8,128)S(1)}, f32[32,1024]{1,0:T(8,128)}, u32[]{:S(2)}) copy-start(f32[32,1024]{1,0:T(8,128)} %running_ref.1) | copy-start | bytes 393220
  40.5 9.6 %collective-permute-start.2 = (f32[32,1024]{1,0:T(8,128)S(1)}, f32[32,1024]{1,0:T(8,128)S(1)}, u32[]{:S(2)}, u32[]{:S(2)}) collective-permute-start(f32[32,1024]{1,0:T(8,128)S(1)} %get-tuple-element.26), channel_id=1, source_target_pairs={{0,80},{2,96},{4,0},{6,32},{8,208},{10,224},{12,128},{14,160},{16,... | collective-permute-start | bytes 393224 | tf_op jit(solution)/shard_map/ppermute | solution.py:155
  50.0 5.7 %collective-permute-start.3 = (f32[32,1024]{1,0:T(8,128)S(1)}, f32[32,1024]{1,0:T(8,128)S(1)}, u32[]{:S(2)}, u32[]{:S(2)}) collective-permute-start(f32[32,1024]{1,0:T(8,128)S(1)} %collective-permute-done.2.x_ref), channel_id=1, source_target_pairs={{0,16},{2,18},{4,20},{6,22},{8,24},{10,26},{12,28},{14,30},{16,0},... | collective-permute-start | bytes 393224 | tf_op jit(solution)/shard_map/ppermute | solution.py:139
  76.2 10.6 %collective-permute-start.4 = (f32[32,1024]{1,0:T(8,128)S(1)}, f32[32,1024]{1,0:T(8,128)S(1)}, u32[]{:S(2)}, u32[]{:S(2)}) collective-permute-start(f32[32,1024]{1,0:T(8,128)S(1)} %get-tuple-element.28), channel_id=1, source_target_pairs={{0,80},{2,96},{4,0},{6,32},{8,208},{10,224},{12,128},{14,160},{16,... | collective-permute-start | bytes 393224 | tf_op jit(solution)/shard_map/ppermute | solution.py:155
  86.8 5.0 %collective-permute-start.5 = (f32[32,1024]{1,0:T(8,128)S(1)}, f32[32,1024]{1,0:T(8,128)S(1)}, u32[]{:S(2)}, u32[]{:S(2)}) collective-permute-start(f32[32,1024]{1,0:T(8,128)S(1)} %collective-permute-done.4.x_ref), channel_id=1, source_target_pairs={{0,16},{2,18},{4,20},{6,22},{8,24},{10,26},{12,28},{14,30},{16,0},... | collective-permute-start | bytes 393224 | tf_op jit(solution)/shard_map/ppermute | solution.py:139
  111.6 10.5 %collective-permute-start.6 = (f32[32,1024]{1,0:T(8,128)S(1)}, f32[32,1024]{1,0:T(8,128)S(1)}, u32[]{:S(2)}, u32[]{:S(2)}) collective-permute-start(f32[32,1024]{1,0:T(8,128)S(1)} %get-tuple-element.30), channel_id=1, source_target_pairs={{0,80},{2,96},{4,0},{6,32},{8,208},{10,224},{12,128},{14,160},{16,... | collective-permute-start | bytes 393224 | tf_op jit(solution)/shard_map/ppermute | solution.py:155
  122.0 5.0 %collective-permute-start.7 = (f32[32,1024]{1,0:T(8,128)S(1)}, f32[32,1024]{1,0:T(8,128)S(1)}, u32[]{:S(2)}, u32[]{:S(2)}) collective-permute-start(f32[32,1024]{1,0:T(8,128)S(1)} %collective-permute-done.6.x_ref), channel_id=1, source_target_pairs={{0,16},{2,18},{4,20},{6,22},{8,24},{10,26},{12,28},{14,30},{16,0},... | collective-permute-start | bytes 393224 | tf_op jit(solution)/shard_map/ppermute | solution.py:139
  147.3 10.6 %collective-permute-start.8 = (f32[32,1024]{1,0:T(8,128)S(1)}, f32[32,1024]{1,0:T(8,128)S(1)}, u32[]{:S(2)}, u32[]{:S(2)}) collective-permute-start(f32[32,1024]{1,0:T(8,128)S(1)} %get-tuple-element.32), channel_id=1, source_target_pairs={{0,80},{2,96},{4,0},{6,32},{8,208},{10,224},{12,128},{14,160},{16,... | collective-permute-start | bytes 393224 | tf_op jit(solution)/shard_map/ppermute | solution.py:155
  157.9 5.0 %collective-permute-start.9 = (f32[32,1024]{1,0:T(8,128)S(1)}, f32[32,1024]{1,0:T(8,128)S(1)}, u32[]{:S(2)}, u32[]{:S(2)}) collective-permute-start(f32[32,1024]{1,0:T(8,128)S(1)} %collective-permute-done.8.x_ref), channel_id=1, source_target_pairs={{0,16},{2,18},{4,20},{6,22},{8,24},{10,26},{12,28},{14,30},{16,0},... | collective-permute-start | bytes 393224 | tf_op jit(solution)/shard_map/ppermute | solution.py:139
  182.6 10.5 %collective-permute-start.10 = (f32[32,1024]{1,0:T(8,128)S(1)}, f32[32,1024]{1,0:T(8,128)S(1)}, u32[]{:S(2)}, u32[]{:S(2)}) collective-permute-start(f32[32,1024]{1,0:T(8,128)S(1)} %get-tuple-element.34), channel_id=1, source_target_pairs={{0,80},{2,96},{4,0},{6,32},{8,208},{10,224},{12,128},{14,160},{16,... | collective-permute-start | bytes 393224 | tf_op jit(solution)/shard_map/ppermute | solution.py:155
  193.1 5.0 %collective-permute-start.11 = (f32[32,1024]{1,0:T(8,128)S(1)}, f32[32,1024]{1,0:T(8,128)S(1)}, u32[]{:S(2)}, u32[]{:S(2)}) collective-permute-start(f32[32,1024]{1,0:T(8,128)S(1)} %collective-permute-done.10.x_ref), channel_id=1, source_target_pairs={{0,16},{2,18},{4,20},{6,22},{8,24},{10,26},{12,28},{14,30},{16,0},... | collective-permute-start | bytes 393224 | tf_op jit(solution)/shard_map/ppermute | solution.py:139

commit v4 on v3

--- a/solution.py
+++ b/solution.py
@@ -29,8 +29,11 @@
 
 
 def owner_moves():
+    def across(zh, y):
+        return y if (y - zh) % 2 else (y + FAR) % 4
+
     return [
-        (index(xh, zh, zl, xl, y), index(xl, (y + FAR) % 4, zl ^ int(y == zh), xh, zh))
+        (index(xh, zh, zl, xl, y), index(xl, across(zh, y), zl ^ int(y == zh), xh, zh))
         for xh, zh, zl, xl, y in PLACES
     ]
 

time: 219 us -> 202 us (0.922)
  the two profiles are of different devices: /device:TPU:64 before, /device:TPU:2 now
where the time goes in v4:
time: 202 us; the launch traced here: 201 us
  blocking collectives  111 us (55%)
  waiting for transfers between devices  51.1 us (25%)
  starting transfers between devices  22.7 us (11%)
  Pallas kernels  15.3 us (8%)
    all_to_all x6, blocking collectives, local(): parts = lax.all_to_all(product(block, halves), COL, 0, 0, tiled=True)  111 us
    ppermute x5, waiting for transfers between devices, local(): block = lax.ppermute(summand, ROW + COL, owner_moves())  36.4 us
    ppermute x6, waiting for transfers between devices, product(): other = lax.ppermute(block, ROW + COL, neighbour_moves())  14.7 us
    pallas_call x18, Pallas kernels, call(): pl.pallas_call(kernel, out_shape=shapes, in_specs=[vmem] * len(operands),...  11 us
    ppermute x6, starting transfers between devices, product(): other = lax.ppermute(block, ROW + COL, neighbour_moves())  10.5 us
    ppermute x1, starting transfers between devices, local(): block = lax.ppermute(vectors, ROW + COL, owner_moves())  7.67 us
    ppermute x5, starting transfers between devices, local(): block = lax.ppermute(summand, ROW + COL, owner_moves())  4.51 us
    pallas_call x1, Pallas kernels, prepare(): pl.pallas_call(prepare_kernel, out_shape=(half, half), in_specs=[pl.Block...  4.29 us
  transfers between devices with their start and end apart: 12, of which 11 were waited for; matrix products, arithmetic and copies ran while one was open for 0% of the time, Pallas kernels for 5%

profile of v4, /device:TPU:2, one launch (start us, length us, event | category | flops | bytes accessed | tf_op | source)
XLA Modules:
  0.0 200.7 jit_solution(18078935786348049511)
XLA Ops:
  0.0 7.7 %collective-permute-start = (f32[32,1024]{1,0:T(8,128)}, f32[32,1024]{1,0:T(8,128)S(1)}, u32[]{:S(2)}, u32[]{:S(2)}) collective-permute-start(f32[32,1024]{1,0:T(8,128)} %running_ref.1), channel_id=1, source_target_pairs={{0,80},{2,32},{4,0},{6,96},{8,208},{10,160},{12,128},{14,224},{16,... | collective-permute-start | bytes 393224 | tf_op jit(solution)/shard_map/ppermute | solution.py:149
  7.7 4.3 %shard_map.28 = (bf16[2048,1024]{1,0:T(8,128)(2,1)S(1)}, bf16[2048,1024]{1,0:T(8,128)(2,1)S(1)}) custom-call(f32[1024,2048]{1,0:T(8,128)} %a_ref.1), custom_call_target="tpu_custom_call" | custom-call | flops 4000000000 | bytes 8388608 | tf_op jit(solution)/shard_map/pallas_call | solution.py:80
  13.9 3.1 %collective-permute-done.1.x_ref = f32[32,1024]{1,0:T(8,128)S(1)} collective-permute-done((f32[32,1024]{1,0:T(8,128)S(1)}, f32[32,1024]{1,0:T(8,128)S(1)}, u32[]{:S(2)}, u32[]{:S(2)}) %collective-permute-start.1) | collective-permute-done | bytes 131104 | tf_op jit(solution)/shard_map/ppermute | solution.py:142
  17.9 20.9 %all_to_all.30.parts_ref = f32[8,32,1024]{2,1,0:T(8,128)S(1)} all-to-all(f32[8,32,1024]{2,1,0:T(8,128)S(1)} %shard_map.30), channel_id=1, replica_groups=mesh['xh'=2,'zh'=4,'zl'=2,'xl'=2,'y'=4,'rep'=2] {'xl','y'}, dimensions={0} | all-to-all | bytes 2097152 | tf_op jit(solution)/shard_map/all_to_all | solution.py:154
  38.9 4.2 %collective-permute-start.2 = (f32[32,1024]{1,0:T(8,128)S(1)}, f32[32,1024]{1,0:T(8,128)S(1)}, u32[]{:S(2)}, u32[]{:S(2)}) collective-permute-start(f32[32,1024]{1,0:T(8,128)S(1)} %get-tuple-element.26), channel_id=1, source_target_pairs={{0,80},{2,32},{4,0},{6,96},{8,208},{10,160},{12,128},{14,224},{16,... | collective-permute-start | bytes 393224 | tf_op jit(solution)/shard_map/ppermute | solution.py:158
  43.1 5.6 %collective-permute-done.2.x_ref = f32[32,1024]{1,0:T(8,128)S(1)} collective-permute-done((f32[32,1024]{1,0:T(8,128)S(1)}, f32[32,1024]{1,0:T(8,128)S(1)}, u32[]{:S(2)}, u32[]{:S(2)}) %collective-permute-start.2) | collective-permute-done | bytes 131104 | tf_op jit(solution)/shard_map/ppermute | solution.py:158
  50.9 2.7 %collective-permute-done.3.x_ref = f32[32,1024]{1,0:T(8,128)S(1)} collective-permute-done((f32[32,1024]{1,0:T(8,128)S(1)}, f32[32,1024]{1,0:T(8,128)S(1)}, u32[]{:S(2)}, u32[]{:S(2)}) %collective-permute-start.3) | collective-permute-done | bytes 131104 | tf_op jit(solution)/shard_map/ppermute | solution.py:142
  54.5 18.4 %all_to_all.31.parts_ref = f32[8,32,1024]{2,1,0:T(8,128)S(1)} all-to-all(f32[8,32,1024]{2,1,0:T(8,128)S(1)} %shard_map.33), channel_id=1, replica_groups=mesh['xh'=2,'zh'=4,'zl'=2,'xl'=2,'y'=4,'rep'=2] {'xl','y'}, dimensions={0} | all-to-all | bytes 2097152 | tf_op jit(solution)/shard_map/all_to_all | solution.py:154
  73.1 7.4 %collective-permute-done.4.x_ref = f32[32,1024]{1,0:T(8,128)S(1)} collective-permute-done((f32[32,1024]{1,0:T(8,128)S(1)}, f32[32,1024]{1,0:T(8,128)S(1)}, u32[]{:S(2)}, u32[]{:S(2)}) %collective-permute-start.4) | collective-permute-done | bytes 131104 | tf_op jit(solution)/shard_map/ppermute | solution.py:158
  80.4 1.7 collective-permute-start.5
  82.9 2.5 %collective-permute-done.5.x_ref = f32[32,1024]{1,0:T(8,128)S(1)} collective-permute-done((f32[32,1024]{1,0:T(8,128)S(1)}, f32[32,1024]{1,0:T(8,128)S(1)}, u32[]{:S(2)}, u32[]{:S(2)}) %collective-permute-start.5) | collective-permute-done | bytes 131104 | tf_op jit(solution)/shard_map/ppermute | solution.py:142
  86.2 18.0 %all_to_all.32.parts_ref = f32[8,32,1024]{2,1,0:T(8,128)S(1)} all-to-all(f32[8,32,1024]{2,1,0:T(8,128)S(1)} %shard_map.36), channel_id=1, replica_groups=mesh['xh'=2,'zh'=4,'zl'=2,'xl'=2,'y'=4,'rep'=2] {'xl','y'}, dimensions={0} | all-to-all | bytes 2097152 | tf_op jit(solution)/shard_map/all_to_all | solution.py:154
  104.3 7.4 %collective-permute-done.6.x_ref = f32[32,1024]{1,0:T(8,128)S(1)} collective-permute-done((f32[32,1024]{1,0:T(8,128)S(1)}, f32[32,1024]{1,0:T(8,128)S(1)}, u32[]{:S(2)}, u32[]{:S(2)}) %collective-permute-start.6) | collective-permute-done | bytes 131104 | tf_op jit(solution)/shard_map/ppermute | solution.py:158
  111.7 2.2 %collective-permute-start.7 = (f32[32,1024]{1,0:T(8,128)S(1)}, f32[32,1024]{1,0:T(8,128)S(1)}, u32[]{:S(2)}, u32[]{:S(2)}) collective-permute-start(f32[32,1024]{1,0:T(8,128)S(1)} %collective-permute-done.6.x_ref), channel_id=1, source_target_pairs={{0,16},{2,18},{4,20},{6,22},{8,24},{10,26},{12,28},{14,30},{16,0},... | collective-permute-start | bytes 393224 | tf_op jit(solution)/shard_map/ppermute | solution.py:142
  114.7 2.1 %collective-permute-done.7.x_ref = f32[32,1024]{1,0:T(8,128)S(1)} collective-permute-done((f32[32,1024]{1,0:T(8,128)S(1)}, f32[32,1024]{1,0:T(8,128)S(1)}, u32[]{:S(2)}, u32[]{:S(2)}) %collective-permute-start.7) | collective-permute-done | bytes 131104 | tf_op jit(solution)/shard_map/ppermute | solution.py:142
  117.7 19.4 %all_to_all.33.parts_ref = f32[8,32,1024]{2,1,0:T(8,128)S(1)} all-to-all(f32[8,32,1024]{2,1,0:T(8,128)S(1)} %shard_map.39), channel_id=1, replica_groups=mesh['xh'=2,'zh'=4,'zl'=2,'xl'=2,'y'=4,'rep'=2] {'xl','y'}, dimensions={0} | all-to-all | bytes 2097152 | tf_op jit(solution)/shard_map/all_to_all | solution.py:154
  137.2 8.8 %collective-permute-done.8.x_ref = f32[32,1024]{1,0:T(8,128)S(1)} collective-permute-done((f32[32,1024]{1,0:T(8,128)S(1)}, f32[32,1024]{1,0:T(8,128)S(1)}, u32[]{:S(2)}, u32[]{:S(2)}) %collective-permute-start.8) | collective-permute-done | bytes 131104 | tf_op jit(solution)/shard_map/ppermute | solution.py:158
  146.0 2.0 %collective-permute-start.9 = (f32[32,1024]{1,0:T(8,128)S(1)}, f32[32,1024]{1,0:T(8,128)S(1)}, u32[]{:S(2)}, u32[]{:S(2)}) collective-permute-start(f32[32,1024]{1,0:T(8,128)S(1)} %collective-permute-done.8.x_ref), channel_id=1, source_target_pairs={{0,16},{2,18},{4,20},{6,22},{8,24},{10,26},{12,28},{14,30},{16,0},... | collective-permute-start | bytes 393224 | tf_op jit(solution)/shard_map/ppermute | solution.py:142
  148.8 2.1 %collective-permute-done.9.x_ref = f32[32,1024]{1,0:T(8,128)S(1)} collective-permute-done((f32[32,1024]{1,0:T(8,128)S(1)}, f32[32,1024]{1,0:T(8,128)S(1)}, u32[]{:S(2)}, u32[]{:S(2)}) %collective-permute-start.9) | collective-permute-done | bytes 131104 | tf_op jit(solution)/shard_map/ppermute | solution.py:142
  151.8 16.0 %all_to_all.34.parts_ref = f32[8,32,1024]{2,1,0:T(8,128)S(1)} all-to-all(f32[8,32,1024]{2,1,0:T(8,128)S(1)} %shard_map.42), channel_id=1, replica_groups=mesh['xh'=2,'zh'=4,'zl'=2,'xl'=2,'y'=4,'rep'=2] {'xl','y'}, dimensions={0} | all-to-all | bytes 2097152 | tf_op jit(solution)/shard_map/all_to_all | solution.py:154
  168.0 7.4 %collective-permute-done.10.x_ref = f32[32,1024]{1,0:T(8,128)S(1)} collective-permute-done((f32[32,1024]{1,0:T(8,128)S(1)}, f32[32,1024]{1,0:T(8,128)S(1)}, u32[]{:S(2)}, u32[]{:S(2)}) %collective-permute-start.10) | collective-permute-done | bytes 131104 | tf_op jit(solution)/shard_map/ppermute | solution.py:158
  175.3 2.0 %collective-permute-start.11 = (f32[32,1024]{1,0:T(8,128)S(1)}, f32[32,1024]{1,0:T(8,128)S(1)}, u32[]{:S(2)}, u32[]{:S(2)}) collective-permute-start(f32[32,1024]{1,0:T(8,128)S(1)} %collective-permute-done.10.x_ref), channel_id=1, source_target_pairs={{0,16},{2,18},{4,20},{6,22},{8,24},{10,26},{12,28},{14,30},{16,0},... | collective-permute-start | bytes 393224 | tf_op jit(solution)/shard_map/ppermute | solution.py:142
  178.2 2.1 %collective-permute-done.11.x_ref = f32[32,1024]{1,0:T(8,128)S(1)} collective-permute-done((f32[32,1024]{1,0:T(8,128)S(1)}, f32[32,1024]{1,0:T(8,128)S(1)}, u32[]{:S(2)}, u32[]{:S(2)}) %collective-permute-start.11) | collective-permute-done | bytes 131104 | tf_op jit(solution)/shard_map/ppermute | solution.py:142
  181.2 18.8 %all_to_all.35.parts_ref = f32[8,32,1024]{2,1,0:T(8,128)S(1)} all-to-all(f32[8,32,1024]{2,1,0:T(8,128)S(1)} %shard_map.45), channel_id=1, replica_groups=mesh['xh'=2,'zh'=4,'zl'=2,'xl'=2,'y'=4,'rep'=2] {'xl','y'}, dimensions={0} | all-to-all | bytes 2097152 | tf_op jit(solution)/shard_map/all_to_all | solution.py:154
  (27 shorter events, 13.9 us)
Async XLA Ops:
  0.0 12.0 %collective-permute-start = (f32[32,1024]{1,0:T(8,128)}, f32[32,1024]{1,0:T(8,128)S(1)}, u32[]{:S(2)}, u32[]{:S(2)}) collective-permute-start(f32[32,1024]{1,0:T(8,128)} %running_ref.1), channel_id=1, source_target_pairs={{0,80},{2,32},{4,0},{6,96},{8,208},{10,160},{12,128},{14,224},{16,... | collective-permute-start | bytes 393224 | tf_op jit(solution)/shard_map/ppermute | solution.py:149
  12.0 5.1 %collective-permute-start.1 = (f32[32,1024]{1,0:T(8,128)S(1)}, f32[32,1024]{1,0:T(8,128)S(1)}, u32[]{:S(2)}, u32[]{:S(2)}) collective-permute-start(f32[32,1024]{1,0:T(8,128)S(1)} %collective-permute-done.x_ref), channel_id=1, source_target_pairs={{0,16},{2,18},{4,20},{6,22},{8,24},{10,26},{12,28},{14,30},{16,0},... | collective-permute-start | bytes 393224 | tf_op jit(solution)/shard_map/ppermute | solution.py:142
  13.9 24.9 %copy-start = (f32[32,1024]{1,0:T(8,128)S(1)}, f32[32,1024]{1,0:T(8,128)}, u32[]{:S(2)}) copy-start(f32[32,1024]{1,0:T(8,128)} %running_ref.1) | copy-start | bytes 393220
  38.9 9.8 %collective-permute-start.2 = (f32[32,1024]{1,0:T(8,128)S(1)}, f32[32,1024]{1,0:T(8,128)S(1)}, u32[]{:S(2)}, u32[]{:S(2)}) collective-permute-start(f32[32,1024]{1,0:T(8,128)S(1)} %get-tuple-element.26), channel_id=1, source_target_pairs={{0,80},{2,32},{4,0},{6,96},{8,208},{10,160},{12,128},{14,224},{16,... | collective-permute-start | bytes 393224 | tf_op jit(solution)/shard_map/ppermute | solution.py:158
  48.6 5.0 %collective-permute-start.3 = (f32[32,1024]{1,0:T(8,128)S(1)}, f32[32,1024]{1,0:T(8,128)S(1)}, u32[]{:S(2)}, u32[]{:S(2)}) collective-permute-start(f32[32,1024]{1,0:T(8,128)S(1)} %collective-permute-done.2.x_ref), channel_id=1, source_target_pairs={{0,16},{2,18},{4,20},{6,22},{8,24},{10,26},{12,28},{14,30},{16,0},... | collective-permute-start | bytes 393224 | tf_op jit(solution)/shard_map/ppermute | solution.py:142
  73.0 7.4 %collective-permute-start.4 = (f32[32,1024]{1,0:T(8,128)S(1)}, f32[32,1024]{1,0:T(8,128)S(1)}, u32[]{:S(2)}, u32[]{:S(2)}) collective-permute-start(f32[32,1024]{1,0:T(8,128)S(1)} %get-tuple-element.28), channel_id=1, source_target_pairs={{0,80},{2,32},{4,0},{6,96},{8,208},{10,160},{12,128},{14,224},{16,... | collective-permute-start | bytes 393224 | tf_op jit(solution)/shard_map/ppermute | solution.py:158
  80.4 5.0 %collective-permute-start.5 = (f32[32,1024]{1,0:T(8,128)S(1)}, f32[32,1024]{1,0:T(8,128)S(1)}, u32[]{:S(2)}, u32[]{:S(2)}) collective-permute-start(f32[32,1024]{1,0:T(8,128)S(1)} %collective-permute-done.4.x_ref), channel_id=1, source_target_pairs={{0,16},{2,18},{4,20},{6,22},{8,24},{10,26},{12,28},{14,30},{16,0},... | collective-permute-start | bytes 393224 | tf_op jit(solution)/shard_map/ppermute | solution.py:142
  104.3 7.4 %collective-permute-start.6 = (f32[32,1024]{1,0:T(8,128)S(1)}, f32[32,1024]{1,0:T(8,128)S(1)}, u32[]{:S(2)}, u32[]{:S(2)}) collective-permute-start(f32[32,1024]{1,0:T(8,128)S(1)} %get-tuple-element.30), channel_id=1, source_target_pairs={{0,80},{2,32},{4,0},{6,96},{8,208},{10,160},{12,128},{14,224},{16,... | collective-permute-start | bytes 393224 | tf_op jit(solution)/shard_map/ppermute | solution.py:158
  111.7 5.2 %collective-permute-start.7 = (f32[32,1024]{1,0:T(8,128)S(1)}, f32[32,1024]{1,0:T(8,128)S(1)}, u32[]{:S(2)}, u32[]{:S(2)}) collective-permute-start(f32[32,1024]{1,0:T(8,128)S(1)} %collective-permute-done.6.x_ref), channel_id=1, source_target_pairs={{0,16},{2,18},{4,20},{6,22},{8,24},{10,26},{12,28},{14,30},{16,0},... | collective-permute-start | bytes 393224 | tf_op jit(solution)/shard_map/ppermute | solution.py:142
  137.1 8.8 %collective-permute-start.8 = (f32[32,1024]{1,0:T(8,128)S(1)}, f32[32,1024]{1,0:T(8,128)S(1)}, u32[]{:S(2)}, u32[]{:S(2)}) collective-permute-start(f32[32,1024]{1,0:T(8,128)S(1)} %get-tuple-element.32), channel_id=1, source_target_pairs={{0,80},{2,32},{4,0},{6,96},{8,208},{10,160},{12,128},{14,224},{16,... | collective-permute-start | bytes 393224 | tf_op jit(solution)/shard_map/ppermute | solution.py:158
  146.0 5.0 %collective-permute-start.9 = (f32[32,1024]{1,0:T(8,128)S(1)}, f32[32,1024]{1,0:T(8,128)S(1)}, u32[]{:S(2)}, u32[]{:S(2)}) collective-permute-start(f32[32,1024]{1,0:T(8,128)S(1)} %collective-permute-done.8.x_ref), channel_id=1, source_target_pairs={{0,16},{2,18},{4,20},{6,22},{8,24},{10,26},{12,28},{14,30},{16,0},... | collective-permute-start | bytes 393224 | tf_op jit(solution)/shard_map/ppermute | solution.py:142
  167.9 7.4 %collective-permute-start.10 = (f32[32,1024]{1,0:T(8,128)S(1)}, f32[32,1024]{1,0:T(8,128)S(1)}, u32[]{:S(2)}, u32[]{:S(2)}) collective-permute-start(f32[32,1024]{1,0:T(8,128)S(1)} %get-tuple-element.34), channel_id=1, source_target_pairs={{0,80},{2,32},{4,0},{6,96},{8,208},{10,160},{12,128},{14,224},{16,... | collective-permute-start | bytes 393224 | tf_op jit(solution)/shard_map/ppermute | solution.py:158
  175.3 5.0 %collective-permute-start.11 = (f32[32,1024]{1,0:T(8,128)S(1)}, f32[32,1024]{1,0:T(8,128)S(1)}, u32[]{:S(2)}, u32[]{:S(2)}) collective-permute-start(f32[32,1024]{1,0:T(8,128)S(1)} %collective-permute-done.10.x_ref), channel_id=1, source_target_pairs={{0,16},{2,18},{4,20},{6,22},{8,24},{10,26},{12,28},{14,30},{16,0},... | collective-permute-start | bytes 393224 | tf_op jit(solution)/shard_map/ppermute | solution.py:142

commit v5 on v4

v5 whole, which is shorter than its diff:
```python
import functools

import jax
import jax.numpy as jnp
from jax import lax
from jax.experimental import pallas as pl
from jax.experimental.pallas import tpu as pltpu
from jax.sharding import Mesh, PartitionSpec as P

TERMS = 6
STEPS = 1

ROW = ("xh", "zh", "zl")
COL = ("xl", "y")
SIZES = {"xh": 2, "zh": 4, "zl": 2, "xl": 2, "y": 4, "rep": 2}
PLACES = [
    (xh, zh, zl, xl, y)
    for xh in range(2)
    for zh in range(4)
    for zl in range(2)
    for xl in range(2)
    for y in range(4)
]
FAR = 2


def index(xh, zh, zl, xl, y):
    return (((xh * 4 + zh) * 2 + zl) * 2 + xl) * 4 + y


def owner_moves():
    def across(zh, y):
        return y if (y - zh) % 2 else (y + FAR) % 4

    return [
        (index(xh, zh, zl, xl, y), index(xl, across(zh, y), zl ^ int(y == zh), xh, zh))
        for xh, zh, zl, xl, y in PLACES
    ]


def partner_moves(which):
    return [
        (index(xh, zh, zl, xl, y), index(xh ^ (which // 2), zh, zl ^ (which % 2), xl, y))
        for xh, zh, zl, xl, y in PLACES
    ]


def split(value):
    high = value.astype(jnp.bfloat16)
    low = (value - high.astype(jnp.float32)).astype(jnp.bfloat16)
    return high, low


def prepare_kernel(which, a_ref, high_ref, low_ref, held, sems):
    blocks = held.shape[0]
    width = held.shape[2]
    swapped = lax.rem(lax.axis_index("y") + FAR, 4) == lax.axis_index("zh")
    half = lax.axis_index("zl") ^ swapped.astype(jnp.int32) ^ (which % 2)
    side = lax.axis_index("xh") ^ (which // 2)
    quarter = half * 2 + side

    def copy(block):
        column = pl.multiple_of(quarter * (blocks * width) + block * width, width)
        return pltpu.make_async_copy(a_ref.at[:, pl.ds(column, width)], held.at[block], sems.at[block])

    for block in range(blocks):
        copy(block).start()
    for block in range(blocks):
        copy(block).wait()
        high, low = split(held[block].T)
        rows = pl.ds(block * width, width)
        high_ref[rows, :] = high
        low_ref[rows, :] = low


def prepare(matrix, which):
    rows, columns = matrix.shape
    width = 256
    half = pltpu.VMEM((columns // 4, rows), jnp.bfloat16)
    return pl.pallas_call(
        functools.partial(prepare_kernel, which),
        out_shape=(half, half),
        in_specs=[pl.BlockSpec(memory_space=pltpu.HBM)],
        out_specs=(pl.BlockSpec(memory_space=pltpu.VMEM),) * 2,
        scratch_shapes=[
            pltpu.VMEM((columns // 4 // width, rows, width), jnp.float32),
            pltpu.SemaphoreType.DMA((columns // 4 // width,)),
        ],
        cost_estimate=pl.CostEstimate(flops=1_000_000_000, bytes_accessed=4 << 20, transcendentals=0),
        compiler_params=pltpu.CompilerParams(vmem_limit_bytes=8 << 20),
    )(pltpu.with_memory_space_constraint(matrix, pltpu.HBM))


def quarter_product(x_ref, high_ref, low_ref):
    x_high, x_low = split(x_ref[...])
    both = jnp.concatenate([x_high, x_low], axis=0)
    vectors = x_high.shape[0]
    for start in range(0, high_ref.shape[1], 256):
        columns = slice(start, start + 256)
        first = jnp.dot(both, high_ref[:, columns], preferred_element_type=jnp.float32)
        second = jnp.dot(x_high, low_ref[:, columns], preferred_element_type=jnp.float32)
        yield start, first[:vectors] + (first[vectors:] + second)


def first_kernel(x_ref, high_ref, low_ref, out_ref):
    for start, total in quarter_product(x_ref, high_ref, low_ref):
        out_ref[:, start : start + 256] = total


def next_kernel(x_ref, high_ref, low_ref, before_ref, out_ref):
    for start, total in quarter_product(x_ref, high_ref, low_ref):
        out_ref[:, start : start + 256] = before_ref[:, start : start + 256] + total


def spread_kernel(x_ref, high_ref, low_ref, before_ref, out_ref):
    width = out_ref.shape[2]
    for start, total in quarter_product(x_ref, high_ref, low_ref):
        total = before_ref[:, start : start + 256] + total
        side, within = divmod(start, width)
        for copy in range(4):
            out_ref[side * 4 + copy, :, within : within + 256] = total


def last_kernel(scale, x_ref, high_ref, low_ref, before_ref, running_ref, out_ref):
    width = running_ref.shape[1]
    mine = lax.axis_index("xl")
    first = lax.axis_index("y") == 0
    for start, total in quarter_product(x_ref, high_ref, low_ref):
        total = before_ref[:, start : start + 256] + total
        side, within = divmod(start, width)
        running = running_ref[:, within : within + 256]
        adds = jnp.logical_and(first, mine == side)
        total = total / scale + jnp.where(adds, running, jnp.zeros_like(running))
        for copy in range(8):
            out_ref[copy, :, start : start + 256] = total


def combine_kernel(scale, parts_ref, running_ref, summand_ref, total_ref):
    summand = parts_ref[0]
    for part in range(1, parts_ref.shape[0]):
        summand = summand + parts_ref[part]
    summand = summand / scale
    summand_ref[...] = summand
    total_ref[...] = running_ref[...] + summand


def call(kernel, out, flops, limit, *operands):
    vmem = pl.BlockSpec(memory_space=pltpu.VMEM)
    shapes = jax.tree.map(lambda shape: jax.ShapeDtypeStruct(shape, jnp.float32), out, is_leaf=lambda o: isinstance(o[0], int))
    return pl.pallas_call(
        kernel,
        out_shape=shapes,
        in_specs=[vmem] * len(operands),
        out_specs=jax.tree.map(lambda _: vmem, shapes),
        cost_estimate=pl.CostEstimate(flops=flops, bytes_accessed=4 << 20, transcendentals=0),
        compiler_params=pltpu.CompilerParams(vmem_limit_bytes=limit),
    )(*operands)


def product(piece, quarters, scale=None, running=None):
    vectors, width = piece.shape
    rows = quarters[0][0].shape[1]
    flops, limit = 100_000_000, 4 << 20
    others = [lax.ppermute(piece, ROW + COL, partner_moves(which)) for which in (1, 2, 3)]
    total = call(first_kernel, (vectors, rows), flops, limit, piece, *quarters[0])
    for which in (1, 2):
        total = call(next_kernel, (vectors, rows), flops, limit, others[which - 1], *quarters[which], total)
    if running is None:
        return call(spread_kernel, (8, vectors, width), flops, limit, others[2], *quarters[3], total)
    kernel = functools.partial(last_kernel, scale)
    return call(kernel, (8, vectors, rows), flops, limit, others[2], *quarters[3], total, running)


def move(piece):
    return lax.ppermute(piece, ROW + COL, owner_moves())


def exchange(value):
    return lax.all_to_all(value, COL, 0, 0, tiled=True)


def local(matrix, vectors):
    half = vectors.shape[1] // 2
    running = jnp.where(lax.axis_index("xl") == 0, vectors[:, :half], vectors[:, half:])
    piece = move(running)
    quarters = [prepare(matrix, which) for which in range(4)]
    for degree in range(1, TERMS):
        parts = exchange(product(piece, quarters))
        kernel = functools.partial(combine_kernel, float(degree * STEPS))
        summand, running = call(kernel, (running.shape,) * 2, 1_000_000, 2 << 20, parts, running)
        piece = move(summand)
    parts = exchange(product(piece, quarters, float(TERMS * STEPS), running))
    return functools.reduce(jnp.add, [parts[part] for part in range(8)])


def solution(mesh):
    fine = Mesh(mesh.devices.reshape(tuple(SIZES.values())), tuple(SIZES))
    placed = (P(ROW, COL), P("rep", ROW))
    return jax.shard_map(local, mesh=fine, in_specs=placed, out_specs=P("rep", ROW), check_vma=False)
```

time: 202 us -> 198 us (0.980)
  starting transfers between devices: 22.7 us -> 44.9 us
  blocking collectives: 111 us -> 90.1 us
  waiting for transfers between devices: 51.1 us -> 41.2 us
  Pallas kernels: 15.3 us -> 19.4 us
    ppermute x12 -> x24, starting transfers between devices: 22.7 us -> 44.9 us  [the longest x18 30 us: product(): lax.ppermute(piece, ROW + COL, partner_moves(which))]
    all_to_all x6, blocking collectives: 111 us -> 90.1 us  [exchange(): return lax.all_to_all(value, COL, 0, 0, tiled=True)]
    ppermute x12 -> x24, waiting for transfers between devices: 51.1 us -> 41.2 us  [the longest x6 27.5 us: move(): return lax.ppermute(piece, ROW + COL, owner_moves())]
    pallas_call x1 -> x4, Pallas kernels: 4.29 us -> 8 us  [prepare(): pl.pallas_call(functools.partial(prepare_kernel, which), out_shape=(half,...]
    pallas_call x18 -> x29, Pallas kernels: 11 us -> 11.4 us  [call(): pl.pallas_call(kernel, out_shape=shapes, in_specs=[vmem] * len(operands),...]
  transfers between devices with their start and end apart: 12 -> 24, of which waited for: 11 -> 15; matrix products, arithmetic and copies ran while one was open for 0% -> 0% of each run, Pallas kernels for 5% -> 8%
where the time goes in v5:
time: 198 us; the launch traced here: 197 us
  blocking collectives  90.1 us (46%)
  starting transfers between devices  44.9 us (23%)
  waiting for transfers between devices  41.2 us (21%)
  Pallas kernels  19.4 us (10%)
    all_to_all x6, blocking collectives, exchange(): return lax.all_to_all(value, COL, 0, 0, tiled=True)  90.1 us
    ppermute x18, starting transfers between devices, product(): lax.ppermute(piece, ROW + COL, partner_moves(which))  30 us
    ppermute x6, waiting for transfers between devices, move(): return lax.ppermute(piece, ROW + COL, owner_moves())  27.5 us
    ppermute x6, starting transfers between devices, move(): return lax.ppermute(piece, ROW + COL, owner_moves())  14.8 us
    ppermute x18, waiting for transfers between devices, product(): lax.ppermute(piece, ROW + COL, partner_moves(which))  13.7 us
    pallas_call x29, Pallas kernels, call(): pl.pallas_call(kernel, out_shape=shapes, in_specs=[vmem] * len(operands),...  11.4 us
    pallas_call x4, Pallas kernels, prepare(): pl.pallas_call(functools.partial(prepare_kernel, which), out_shape=(half,...  8 us
  transfers between devices with their start and end apart: 24, of which 15 were waited for; matrix products, arithmetic and copies ran while one was open for 0% of the time, Pallas kernels for 8%

profile of v5, /device:TPU:2, one launch (start us, length us, event | category | flops | bytes accessed | tf_op | source)
XLA Modules:
  0.0 197.3 jit_solution(10102801669296857452)
XLA Ops:
  0.9 7.7 %collective-permute-start = (f32[32,512]{1,0:T(8,128)S(1)}, f32[32,512]{1,0:T(8,128)S(1)}, u32[]{:S(2)}, u32[]{:S(2)}) collective-permute-start(f32[32,512]{1,0:T(8,128)S(1)} %slice_select_fusion.running_ref), channel_id=1, source_target_pairs={{0,80},{2,32},{4,0},{6,96},{8,208},{10,160},{12,128},{14,224},{16,... | collective-permute-start | bytes 196616 | tf_op jit(solution)/shard_map/ppermute | solution.py:175
  8.6 2.0 %shard_map.29 = (bf16[512,1024]{1,0:T(8,128)(2,1)S(1)}, bf16[512,1024]{1,0:T(8,128)(2,1)S(1)}) custom-call(f32[1024,2048]{1,0:T(8,128)} %a_ref.7), custom_call_target="tpu_custom_call" | custom-call | flops 1000000000 | bytes 4194304 | tf_op jit(solution)/shard_map/pallas_call | solution.py:80
  10.6 2.0 %shard_map.28 = (bf16[512,1024]{1,0:T(8,128)(2,1)S(1)}, bf16[512,1024]{1,0:T(8,128)(2,1)S(1)}) custom-call(f32[1024,2048]{1,0:T(8,128)} %a_ref.7), custom_call_target="tpu_custom_call" | custom-call | flops 1000000000 | bytes 4194304 | tf_op jit(solution)/shard_map/pallas_call | solution.py:80
  12.6 2.0 %shard_map.31 = (bf16[512,1024]{1,0:T(8,128)(2,1)S(1)}, bf16[512,1024]{1,0:T(8,128)(2,1)S(1)}) custom-call(f32[1024,2048]{1,0:T(8,128)} %a_ref.7), custom_call_target="tpu_custom_call" | custom-call | flops 1000000000 | bytes 4194304 | tf_op jit(solution)/shard_map/pallas_call | solution.py:80
  17.0 2.8 %collective-permute-start.1 = (f32[32,512]{1,0:T(8,128)S(1)}, f32[32,512]{1,0:T(8,128)S(1)}, u32[]{:S(2)}, u32[]{:S(2)}) collective-permute-start(f32[32,512]{1,0:T(8,128)S(1)} %collective-permute-done.x_ref), channel_id=1, source_target_pairs={{0,144},{2,146},{4,148},{6,150},{8,152},{10,154},{12,156},{14,158}... | collective-permute-start | bytes 196616 | tf_op jit(solution)/shard_map/ppermute | solution.py:164
  24.1 12.0 %all_to_all.30.parts_ref = f32[8,32,512]{2,1,0:T(8,128)S(1)} all-to-all(f32[8,32,512]{2,1,0:T(8,128)S(1)} %shard_map.35), channel_id=1, replica_groups=mesh['xh'=2,'zh'=4,'zl'=2,'xl'=2,'y'=4,'rep'=2] {'xl','y'}, dimensions={0} | all-to-all | bytes 1048576 | tf_op jit(solution)/shard_map/all_to_all | solution.py:179
  36.2 4.2 %collective-permute-start.4 = (f32[32,512]{1,0:T(8,128)S(1)}, f32[32,512]{1,0:T(8,128)S(1)}, u32[]{:S(2)}, u32[]{:S(2)}) collective-permute-start(f32[32,512]{1,0:T(8,128)S(1)} %get-tuple-element.31), channel_id=1, source_target_pairs={{0,80},{2,32},{4,0},{6,96},{8,208},{10,160},{12,128},{14,224},{16,... | collective-permute-start | bytes 196616 | tf_op jit(solution)/shard_map/ppermute | solution.py:175
  40.4 2.5 %collective-permute-done.4.x_ref = f32[32,512]{1,0:T(8,128)S(1)} collective-permute-done((f32[32,512]{1,0:T(8,128)S(1)}, f32[32,512]{1,0:T(8,128)S(1)}, u32[]{:S(2)}, u32[]{:S(2)}) %collective-permute-start.4) | collective-permute-done | bytes 65568 | tf_op jit(solution)/shard_map/ppermute | solution.py:175
  45.3 2.5 %collective-permute-start.5 = (f32[32,512]{1,0:T(8,128)S(1)}, f32[32,512]{1,0:T(8,128)S(1)}, u32[]{:S(2)}, u32[]{:S(2)}) collective-permute-start(f32[32,512]{1,0:T(8,128)S(1)} %collective-permute-done.4.x_ref), channel_id=1, source_target_pairs={{0,144},{2,146},{4,148},{6,150},{8,152},{10,154},{12,156},{14,158}... | collective-permute-start | bytes 196616 | tf_op jit(solution)/shard_map/ppermute | solution.py:164
  52.5 16.3 %all_to_all.31.parts_ref = f32[8,32,512]{2,1,0:T(8,128)S(1)} all-to-all(f32[8,32,512]{2,1,0:T(8,128)S(1)} %shard_map.40), channel_id=1, replica_groups=mesh['xh'=2,'zh'=4,'zl'=2,'xl'=2,'y'=4,'rep'=2] {'xl','y'}, dimensions={0} | all-to-all | bytes 1048576 | tf_op jit(solution)/shard_map/all_to_all | solution.py:179
  69.3 6.2 %collective-permute-done.8.x_ref = f32[32,512]{1,0:T(8,128)S(1)} collective-permute-done((f32[32,512]{1,0:T(8,128)S(1)}, f32[32,512]{1,0:T(8,128)S(1)}, u32[]{:S(2)}, u32[]{:S(2)}) %collective-permute-start.8) | collective-permute-done | bytes 65568 | tf_op jit(solution)/shard_map/ppermute | solution.py:175
  76.4 4.1 %collective-permute-start.9 = (f32[32,512]{1,0:T(8,128)S(1)}, f32[32,512]{1,0:T(8,128)S(1)}, u32[]{:S(2)}, u32[]{:S(2)}) collective-permute-start(f32[32,512]{1,0:T(8,128)S(1)} %collective-permute-done.8.x_ref), channel_id=1, source_target_pairs={{0,144},{2,146},{4,148},{6,150},{8,152},{10,154},{12,156},{14,158}... | collective-permute-start | bytes 196616 | tf_op jit(solution)/shard_map/ppermute | solution.py:164
  83.6 14.3 %all_to_all.32.parts_ref = f32[8,32,512]{2,1,0:T(8,128)S(1)} all-to-all(f32[8,32,512]{2,1,0:T(8,128)S(1)} %shard_map.45), channel_id=1, replica_groups=mesh['xh'=2,'zh'=4,'zl'=2,'xl'=2,'y'=4,'rep'=2] {'xl','y'}, dimensions={0} | all-to-all | bytes 1048576 | tf_op jit(solution)/shard_map/all_to_all | solution.py:179
  99.8 4.9 %collective-permute-done.12.x_ref = f32[32,512]{1,0:T(8,128)S(1)} collective-permute-done((f32[32,512]{1,0:T(8,128)S(1)}, f32[32,512]{1,0:T(8,128)S(1)}, u32[]{:S(2)}, u32[]{:S(2)}) %collective-permute-start.12) | collective-permute-done | bytes 65568 | tf_op jit(solution)/shard_map/ppermute | solution.py:175
  106.3 2.1 %collective-permute-start.14 = (f32[32,512]{1,0:T(8,128)S(1)}, f32[32,512]{1,0:T(8,128)S(1)}, u32[]{:S(2)}, u32[]{:S(2)}) collective-permute-start(f32[32,512]{1,0:T(8,128)S(1)} %collective-permute-done.12.x_ref), channel_id=1, source_target_pairs={{0,128},{2,130},{4,132},{6,134},{8,136},{10,138},{12,140},{14,142}... | collective-permute-start | bytes 196616 | tf_op jit(solution)/shard_map/ppermute | solution.py:164
  110.6 2.2 %collective-permute-done.14.x_ref = f32[32,512]{1,0:T(8,128)S(1)} collective-permute-done((f32[32,512]{1,0:T(8,128)S(1)}, f32[32,512]{1,0:T(8,128)S(1)}, u32[]{:S(2)}, u32[]{:S(2)}) %collective-permute-start.14) | collective-permute-done | bytes 65568 | tf_op jit(solution)/shard_map/ppermute | solution.py:164
  115.6 16.6 %all_to_all.33.parts_ref = f32[8,32,512]{2,1,0:T(8,128)S(1)} all-to-all(f32[8,32,512]{2,1,0:T(8,128)S(1)} %shard_map.50), channel_id=1, replica_groups=mesh['xh'=2,'zh'=4,'zl'=2,'xl'=2,'y'=4,'rep'=2] {'xl','y'}, dimensions={0} | all-to-all | bytes 1048576 | tf_op jit(solution)/shard_map/all_to_all | solution.py:179
  132.3 6.7 %collective-permute-done.16.x_ref = f32[32,512]{1,0:T(8,128)S(1)} collective-permute-done((f32[32,512]{1,0:T(8,128)S(1)}, f32[32,512]{1,0:T(8,128)S(1)}, u32[]{:S(2)}, u32[]{:S(2)}) %collective-permute-start.16) | collective-permute-done | bytes 65568 | tf_op jit(solution)/shard_map/ppermute | solution.py:175
  139.0 5.0 %collective-permute-start.17 = (f32[32,512]{1,0:T(8,128)S(1)}, f32[32,512]{1,0:T(8,128)S(1)}, u32[]{:S(2)}, u32[]{:S(2)}) collective-permute-start(f32[32,512]{1,0:T(8,128)S(1)} %collective-permute-done.16.x_ref), channel_id=1, source_target_pairs={{0,144},{2,146},{4,148},{6,150},{8,152},{10,154},{12,156},{14,158}... | collective-permute-start | bytes 196616 | tf_op jit(solution)/shard_map/ppermute | solution.py:164
  146.7 14.8 %all_to_all.34.parts_ref = f32[8,32,512]{2,1,0:T(8,128)S(1)} all-to-all(f32[8,32,512]{2,1,0:T(8,128)S(1)} %shard_map.55), channel_id=1, replica_groups=mesh['xh'=2,'zh'=4,'zl'=2,'xl'=2,'y'=4,'rep'=2] {'xl','y'}, dimensions={0} | all-to-all | bytes 1048576 | tf_op jit(solution)/shard_map/all_to_all | solution.py:179
  161.9 7.3 %collective-permute-done.20.x_ref = f32[32,512]{1,0:T(8,128)S(1)} collective-permute-done((f32[32,512]{1,0:T(8,128)S(1)}, f32[32,512]{1,0:T(8,128)S(1)}, u32[]{:S(2)}, u32[]{:S(2)}) %collective-permute-start.20) | collective-permute-done | bytes 65568 | tf_op jit(solution)/shard_map/ppermute | solution.py:175
  170.1 3.2 %collective-permute-start.22 = (f32[32,512]{1,0:T(8,128)S(1)}, f32[32,512]{1,0:T(8,128)S(1)}, u32[]{:S(2)}, u32[]{:S(2)}) collective-permute-start(f32[32,512]{1,0:T(8,128)S(1)} %collective-permute-done.20.x_ref), channel_id=1, source_target_pairs={{0,128},{2,130},{4,132},{6,134},{8,136},{10,138},{12,140},{14,142}... | collective-permute-start | bytes 196616 | tf_op jit(solution)/shard_map/ppermute | solution.py:164
  176.3 3.6 %collective-permute-done.21.x_ref = f32[32,512]{1,0:T(8,128)S(1)} collective-permute-done((f32[32,512]{1,0:T(8,128)S(1)}, f32[32,512]{1,0:T(8,128)S(1)}, u32[]{:S(2)}, u32[]{:S(2)}) %collective-permute-start.21) | collective-permute-done | bytes 65568 | tf_op jit(solution)/shard_map/ppermute | solution.py:164
  180.4 16.2 %all_to_all.35 = f32[8,32,1024]{2,1,0:T(8,128)S(1)} all-to-all(f32[8,32,1024]{2,1,0:T(8,128)S(1)} %shard_map.60), channel_id=1, replica_groups=mesh['xh'=2,'zh'=4,'zl'=2,'xl'=2,'y'=4,'rep'=2] {'xl','y'}, dimensions={0} | all-to-all | bytes 2097152 | tf_op jit(solution)/shard_map/all_to_all | solution.py:179
  (65 shorter events, 36.0 us)
Async XLA Ops:
  0.9 13.8 %collective-permute-start = (f32[32,512]{1,0:T(8,128)S(1)}, f32[32,512]{1,0:T(8,128)S(1)}, u32[]{:S(2)}, u32[]{:S(2)}) collective-permute-start(f32[32,512]{1,0:T(8,128)S(1)} %slice_select_fusion.running_ref), channel_id=1, source_target_pairs={{0,80},{2,32},{4,0},{6,96},{8,208},{10,160},{12,128},{14,224},{16,... | collective-permute-start | bytes 196616 | tf_op jit(solution)/shard_map/ppermute | solution.py:175
  14.7 7.5 %collective-permute-start.3 = (f32[32,512]{1,0:T(8,128)S(1)}, f32[32,512]{1,0:T(8,128)S(1)}, u32[]{:S(2)}, u32[]{:S(2)}) collective-permute-start(f32[32,512]{1,0:T(8,128)S(1)} %collective-permute-done.x_ref), channel_id=1, source_target_pairs={{0,16},{2,18},{4,20},{6,22},{8,24},{10,26},{12,28},{14,30},{16,0},... | collective-permute-start | bytes 196616 | tf_op jit(solution)/shard_map/ppermute | solution.py:164
  15.8 6.9 %collective-permute-start.2 = (f32[32,512]{1,0:T(8,128)S(1)}, f32[32,512]{1,0:T(8,128)S(1)}, u32[]{:S(2)}, u32[]{:S(2)}) collective-permute-start(f32[32,512]{1,0:T(8,128)S(1)} %collective-permute-done.x_ref), channel_id=1, source_target_pairs={{0,128},{2,130},{4,132},{6,134},{8,136},{10,138},{12,140},{14,142}... | collective-permute-start | bytes 196616 | tf_op jit(solution)/shard_map/ppermute | solution.py:164
  17.0 6.7 %collective-permute-start.1 = (f32[32,512]{1,0:T(8,128)S(1)}, f32[32,512]{1,0:T(8,128)S(1)}, u32[]{:S(2)}, u32[]{:S(2)}) collective-permute-start(f32[32,512]{1,0:T(8,128)S(1)} %collective-permute-done.x_ref), channel_id=1, source_target_pairs={{0,144},{2,146},{4,148},{6,150},{8,152},{10,154},{12,156},{14,158}... | collective-permute-start | bytes 196616 | tf_op jit(solution)/shard_map/ppermute | solution.py:164
  36.2 6.7 %collective-permute-start.4 = (f32[32,512]{1,0:T(8,128)S(1)}, f32[32,512]{1,0:T(8,128)S(1)}, u32[]{:S(2)}, u32[]{:S(2)}) collective-permute-start(f32[32,512]{1,0:T(8,128)S(1)} %get-tuple-element.31), channel_id=1, source_target_pairs={{0,80},{2,32},{4,0},{6,96},{8,208},{10,160},{12,128},{14,224},{16,... | collective-permute-start | bytes 196616 | tf_op jit(solution)/shard_map/ppermute | solution.py:175
  42.9 5.5 %collective-permute-start.7 = (f32[32,512]{1,0:T(8,128)S(1)}, f32[32,512]{1,0:T(8,128)S(1)}, u32[]{:S(2)}, u32[]{:S(2)}) collective-permute-start(f32[32,512]{1,0:T(8,128)S(1)} %collective-permute-done.4.x_ref), channel_id=1, source_target_pairs={{0,16},{2,18},{4,20},{6,22},{8,24},{10,26},{12,28},{14,30},{16,0},... | collective-permute-start | bytes 196616 | tf_op jit(solution)/shard_map/ppermute | solution.py:164
  43.9 5.8 %collective-permute-start.6 = (f32[32,512]{1,0:T(8,128)S(1)}, f32[32,512]{1,0:T(8,128)S(1)}, u32[]{:S(2)}, u32[]{:S(2)}) collective-permute-start(f32[32,512]{1,0:T(8,128)S(1)} %collective-permute-done.4.x_ref), channel_id=1, source_target_pairs={{0,128},{2,130},{4,132},{6,134},{8,136},{10,138},{12,140},{14,142}... | collective-permute-start | bytes 196616 | tf_op jit(solution)/shard_map/ppermute | solution.py:164
  45.3 6.7 %collective-permute-start.5 = (f32[32,512]{1,0:T(8,128)S(1)}, f32[32,512]{1,0:T(8,128)S(1)}, u32[]{:S(2)}, u32[]{:S(2)}) collective-permute-start(f32[32,512]{1,0:T(8,128)S(1)} %collective-permute-done.4.x_ref), channel_id=1, source_target_pairs={{0,144},{2,146},{4,148},{6,150},{8,152},{10,154},{12,156},{14,158}... | collective-permute-start | bytes 196616 | tf_op jit(solution)/shard_map/ppermute | solution.py:164
  68.8 6.7 %collective-permute-start.8 = (f32[32,512]{1,0:T(8,128)S(1)}, f32[32,512]{1,0:T(8,128)S(1)}, u32[]{:S(2)}, u32[]{:S(2)}) collective-permute-start(f32[32,512]{1,0:T(8,128)S(1)} %get-tuple-element.33), channel_id=1, source_target_pairs={{0,80},{2,32},{4,0},{6,96},{8,208},{10,160},{12,128},{14,224},{16,... | collective-permute-start | bytes 196616 | tf_op jit(solution)/shard_map/ppermute | solution.py:175
  75.6 5.5 %collective-permute-start.11 = (f32[32,512]{1,0:T(8,128)S(1)}, f32[32,512]{1,0:T(8,128)S(1)}, u32[]{:S(2)}, u32[]{:S(2)}) collective-permute-start(f32[32,512]{1,0:T(8,128)S(1)} %collective-permute-done.8.x_ref), channel_id=1, source_target_pairs={{0,16},{2,18},{4,20},{6,22},{8,24},{10,26},{12,28},{14,30},{16,0},... | collective-permute-start | bytes 196616 | tf_op jit(solution)/shard_map/ppermute | solution.py:164
  76.4 5.8 %collective-permute-start.10 = (f32[32,512]{1,0:T(8,128)S(1)}, f32[32,512]{1,0:T(8,128)S(1)}, u32[]{:S(2)}, u32[]{:S(2)}) collective-permute-start(f32[32,512]{1,0:T(8,128)S(1)} %collective-permute-done.8.x_ref), channel_id=1, source_target_pairs={{0,128},{2,130},{4,132},{6,134},{8,136},{10,138},{12,140},{14,142}... | collective-permute-start | bytes 196616 | tf_op jit(solution)/shard_map/ppermute | solution.py:164
  76.4 6.7 %collective-permute-start.9 = (f32[32,512]{1,0:T(8,128)S(1)}, f32[32,512]{1,0:T(8,128)S(1)}, u32[]{:S(2)}, u32[]{:S(2)}) collective-permute-start(f32[32,512]{1,0:T(8,128)S(1)} %collective-permute-done.8.x_ref), channel_id=1, source_target_pairs={{0,144},{2,146},{4,148},{6,150},{8,152},{10,154},{12,156},{14,158}... | collective-permute-start | bytes 196616 | tf_op jit(solution)/shard_map/ppermute | solution.py:164
  97.9 6.7 %collective-permute-start.12 = (f32[32,512]{1,0:T(8,128)S(1)}, f32[32,512]{1,0:T(8,128)S(1)}, u32[]{:S(2)}, u32[]{:S(2)}) collective-permute-start(f32[32,512]{1,0:T(8,128)S(1)} %get-tuple-element.35), channel_id=1, source_target_pairs={{0,80},{2,32},{4,0},{6,96},{8,208},{10,160},{12,128},{14,224},{16,... | collective-permute-start | bytes 196616 | tf_op jit(solution)/shard_map/ppermute | solution.py:175
  104.6 5.4 %collective-permute-start.15 = (f32[32,512]{1,0:T(8,128)S(1)}, f32[32,512]{1,0:T(8,128)S(1)}, u32[]{:S(2)}, u32[]{:S(2)}) collective-permute-start(f32[32,512]{1,0:T(8,128)S(1)} %collective-permute-done.12.x_ref), channel_id=1, source_target_pairs={{0,16},{2,18},{4,20},{6,22},{8,24},{10,26},{12,28},{14,30},{16,0},... | collective-permute-start | bytes 196616 | tf_op jit(solution)/shard_map/ppermute | solution.py:164
  106.3 6.5 %collective-permute-start.14 = (f32[32,512]{1,0:T(8,128)S(1)}, f32[32,512]{1,0:T(8,128)S(1)}, u32[]{:S(2)}, u32[]{:S(2)}) collective-permute-start(f32[32,512]{1,0:T(8,128)S(1)} %collective-permute-done.12.x_ref), channel_id=1, source_target_pairs={{0,128},{2,130},{4,132},{6,134},{8,136},{10,138},{12,140},{14,142}... | collective-permute-start | bytes 196616 | tf_op jit(solution)/shard_map/ppermute | solution.py:164
  108.4 6.7 %collective-permute-start.13 = (f32[32,512]{1,0:T(8,128)S(1)}, f32[32,512]{1,0:T(8,128)S(1)}, u32[]{:S(2)}, u32[]{:S(2)}) collective-permute-start(f32[32,512]{1,0:T(8,128)S(1)} %collective-permute-done.12.x_ref), channel_id=1, source_target_pairs={{0,144},{2,146},{4,148},{6,150},{8,152},{10,154},{12,156},{14,158}... | collective-permute-start | bytes 196616 | tf_op jit(solution)/shard_map/ppermute | solution.py:164
  132.2 6.7 %collective-permute-start.16 = (f32[32,512]{1,0:T(8,128)S(1)}, f32[32,512]{1,0:T(8,128)S(1)}, u32[]{:S(2)}, u32[]{:S(2)}) collective-permute-start(f32[32,512]{1,0:T(8,128)S(1)} %get-tuple-element.37), channel_id=1, source_target_pairs={{0,80},{2,32},{4,0},{6,96},{8,208},{10,160},{12,128},{14,224},{16,... | collective-permute-start | bytes 196616 | tf_op jit(solution)/shard_map/ppermute | solution.py:175
  139.0 5.5 %collective-permute-start.19 = (f32[32,512]{1,0:T(8,128)S(1)}, f32[32,512]{1,0:T(8,128)S(1)}, u32[]{:S(2)}, u32[]{:S(2)}) collective-permute-start(f32[32,512]{1,0:T(8,128)S(1)} %collective-permute-done.16.x_ref), channel_id=1, source_target_pairs={{0,16},{2,18},{4,20},{6,22},{8,24},{10,26},{12,28},{14,30},{16,0},... | collective-permute-start | bytes 196616 | tf_op jit(solution)/shard_map/ppermute | solution.py:164
  139.0 5.9 %collective-permute-start.18 = (f32[32,512]{1,0:T(8,128)S(1)}, f32[32,512]{1,0:T(8,128)S(1)}, u32[]{:S(2)}, u32[]{:S(2)}) collective-permute-start(f32[32,512]{1,0:T(8,128)S(1)} %collective-permute-done.16.x_ref), channel_id=1, source_target_pairs={{0,128},{2,130},{4,132},{6,134},{8,136},{10,138},{12,140},{14,142}... | collective-permute-start | bytes 196616 | tf_op jit(solution)/shard_map/ppermute | solution.py:164
  139.0 7.2 %collective-permute-start.17 = (f32[32,512]{1,0:T(8,128)S(1)}, f32[32,512]{1,0:T(8,128)S(1)}, u32[]{:S(2)}, u32[]{:S(2)}) collective-permute-start(f32[32,512]{1,0:T(8,128)S(1)} %collective-permute-done.16.x_ref), channel_id=1, source_target_pairs={{0,144},{2,146},{4,148},{6,150},{8,152},{10,154},{12,156},{14,158}... | collective-permute-start | bytes 196616 | tf_op jit(solution)/shard_map/ppermute | solution.py:164
  161.5 7.6 %collective-permute-start.20 = (f32[32,512]{1,0:T(8,128)S(1)}, f32[32,512]{1,0:T(8,128)S(1)}, u32[]{:S(2)}, u32[]{:S(2)}) collective-permute-start(f32[32,512]{1,0:T(8,128)S(1)} %get-tuple-element.39), channel_id=1, source_target_pairs={{0,80},{2,32},{4,0},{6,96},{8,208},{10,160},{12,128},{14,224},{16,... | collective-permute-start | bytes 196616 | tf_op jit(solution)/shard_map/ppermute | solution.py:175
  169.1 5.5 %collective-permute-start.23 = (f32[32,512]{1,0:T(8,128)S(1)}, f32[32,512]{1,0:T(8,128)S(1)}, u32[]{:S(2)}, u32[]{:S(2)}) collective-permute-start(f32[32,512]{1,0:T(8,128)S(1)} %collective-permute-done.20.x_ref), channel_id=1, source_target_pairs={{0,16},{2,18},{4,20},{6,22},{8,24},{10,26},{12,28},{14,30},{16,0},... | collective-permute-start | bytes 196616 | tf_op jit(solution)/shard_map/ppermute | solution.py:164
  170.1 5.8 %collective-permute-start.22 = (f32[32,512]{1,0:T(8,128)S(1)}, f32[32,512]{1,0:T(8,128)S(1)}, u32[]{:S(2)}, u32[]{:S(2)}) collective-permute-start(f32[32,512]{1,0:T(8,128)S(1)} %collective-permute-done.20.x_ref), channel_id=1, source_target_pairs={{0,128},{2,130},{4,132},{6,134},{8,136},{10,138},{12,140},{14,142}... | collective-permute-start | bytes 196616 | tf_op jit(solution)/shard_map/ppermute | solution.py:164
  173.2 6.7 %collective-permute-start.21 = (f32[32,512]{1,0:T(8,128)S(1)}, f32[32,512]{1,0:T(8,128)S(1)}, u32[]{:S(2)}, u32[]{:S(2)}) collective-permute-start(f32[32,512]{1,0:T(8,128)S(1)} %collective-permute-done.20.x_ref), channel_id=1, source_target_pairs={{0,144},{2,146},{4,148},{6,150},{8,152},{10,154},{12,156},{14,158}... | collective-permute-start | bytes 196616 | tf_op jit(solution)/shard_map/ppermute | solution.py:164

commit v6 on v4

v6 whole, which is shorter than its diff:
```python
import functools

import jax
import jax.numpy as jnp
from jax import lax
from jax.experimental import pallas as pl
from jax.experimental.pallas import tpu as pltpu
from jax.sharding import Mesh, PartitionSpec as P

TERMS = 6
STEPS = 1

ROW = ("xh", "zh", "zl")
COL = ("xl", "y")
SIZES = {"xh": 2, "zh": 4, "zl": 2, "xl": 2, "y": 4, "rep": 2}
PLACES = [
    (xh, zh, zl, xl, y)
    for xh in range(2)
    for zh in range(4)
    for zl in range(2)
    for xl in range(2)
    for y in range(4)
]
FAR = 2


def index(xh, zh, zl, xl, y):
    return (((xh * 4 + zh) * 2 + zl) * 2 + xl) * 4 + y


def owner_moves():
    def across(zh, y):
        return y if (y - zh) % 2 else (y + FAR) % 4

    return [
        (index(xh, zh, zl, xl, y), index(xl, across(zh, y), zl ^ int(y == zh), xh, zh))
        for xh, zh, zl, xl, y in PLACES
    ]


def partner_moves(which):
    return [
        (index(xh, zh, zl, xl, y), index(xh ^ (which // 2), zh, zl ^ (which % 2), xl, y))
        for xh, zh, zl, xl, y in PLACES
    ]


def split(value):
    high = value.astype(jnp.bfloat16)
    low = (value - high.astype(jnp.float32)).astype(jnp.bfloat16)
    return high, low


def prepare_kernel(a_ref, high_ref, low_ref, held, sems):
    blocks = held.shape[0]
    width = held.shape[2]
    swapped = lax.rem(lax.axis_index("y") + FAR, 4) == lax.axis_index("zh")
    own_half = lax.axis_index("zl") ^ swapped.astype(jnp.int32)
    own_side = lax.axis_index("xh")

    def copy(block):
        column = pl.multiple_of(block * width, width)
        return pltpu.make_async_copy(a_ref.at[:, pl.ds(column, width)], held.at[block], sems.at[block])

    for block in range(blocks):
        copy(block).start()

    def step(block, carry):
        copy(block).wait()
        high, low = split(held[block].T)
        half, side, part = block // 4, lax.rem(block // 2, 2), lax.rem(block, 2)
        place = ((half ^ own_half) + 2 * (side ^ own_side)) * 2 + part
        rows = pl.ds(pl.multiple_of(place * width, width), width)
        high_ref[rows, :] = high
        low_ref[rows, :] = low
        return carry

    lax.fori_loop(0, blocks, step, 0)


def prepare(matrix):
    rows, columns = matrix.shape
    width = columns // 8
    half = pltpu.VMEM((columns, rows), jnp.bfloat16)
    return pl.pallas_call(
        prepare_kernel,
        out_shape=(half, half),
        in_specs=[pl.BlockSpec(memory_space=pltpu.HBM)],
        out_specs=(pl.BlockSpec(memory_space=pltpu.VMEM),) * 2,
        scratch_shapes=[
            pltpu.VMEM((8, rows, width), jnp.float32),
            pltpu.SemaphoreType.DMA((8,)),
        ],
        cost_estimate=pl.CostEstimate(flops=4_000_000_000, bytes_accessed=8 << 20, transcendentals=0),
        compiler_params=pltpu.CompilerParams(vmem_limit_bytes=24 << 20),
    )(pltpu.with_memory_space_constraint(matrix, pltpu.HBM))


def tiles(pieces, high_ref, low_ref, before_ref=None):
    depth = high_ref.shape[0] // 4
    operands = []
    for quarter, piece in pieces:
        x_high, x_low = split(piece)
        rows = slice(quarter * depth, (quarter + 1) * depth)
        operands.append((rows, x_high, jnp.concatenate([x_high, x_low], axis=0)))
    for start in range(0, high_ref.shape[1], 256):
        columns = slice(start, start + 256)
        total = None
        for rows, x_high, both in operands:
            vectors = x_high.shape[0]
            first = jnp.dot(both, high_ref[rows, columns], preferred_element_type=jnp.float32)
            second = jnp.dot(x_high, low_ref[rows, columns], preferred_element_type=jnp.float32)
            value = first[:vectors] + (first[vectors:] + second)
            total = value if total is None else total + value
        if before_ref is not None:
            total = before_ref[:, columns] + total
        yield start, total


def block_pieces(quarters, x_ref):
    width = x_ref.shape[1] // 2
    side = lax.axis_index("xh")
    at = [pl.multiple_of(place * width, width) for place in (side, 1 - side)]
    return [(quarter, x_ref[:, pl.ds(place, width)]) for quarter, place in zip(quarters, at)]


def store(start, total, out_ref):
    out_ref[:, start : start + 256] = total


def spread(start, total, out_ref):
    side, within = divmod(start, out_ref.shape[2])
    for copy in range(4):
        out_ref[side * 4 + copy, :, within : within + 256] = total


def own_block_kernel(x_ref, high_ref, low_ref, vectors_ref, out_ref, running_ref):
    width = running_ref.shape[1]
    running_ref[...] = vectors_ref[:, pl.ds(pl.multiple_of(lax.axis_index("xl") * width, width), width)]
    for start, total in tiles(block_pieces((0, 2), x_ref), high_ref, low_ref):
        store(start, total, out_ref)


def other_block_kernel(x_ref, high_ref, low_ref, before_ref, out_ref):
    for start, total in tiles(block_pieces((1, 3), x_ref), high_ref, low_ref, before_ref):
        spread(start, total, out_ref)


def own_kernel(x_ref, high_ref, low_ref, out_ref):
    for start, total in tiles([(0, x_ref[...])], high_ref, low_ref):
        store(start, total, out_ref)


def next_kernel(which, x_ref, high_ref, low_ref, before_ref, out_ref):
    for start, total in tiles([(which, x_ref[...])], high_ref, low_ref, before_ref):
        store(start, total, out_ref)


def spread_kernel(x_ref, high_ref, low_ref, before_ref, out_ref):
    for start, total in tiles([(3, x_ref[...])], high_ref, low_ref, before_ref):
        spread(start, total, out_ref)


def last_kernel(scale, x_ref, high_ref, low_ref, before_ref, running_ref, out_ref):
    width = running_ref.shape[1]
    mine = lax.axis_index("xl")
    first = lax.axis_index("y") == 0
    for start, total in tiles([(3, x_ref[...])], high_ref, low_ref, before_ref):
        side, within = divmod(start, width)
        running = running_ref[:, within : within + 256]
        adds = jnp.logical_and(first, mine == side)
        total = total / scale + jnp.where(adds, running, jnp.zeros_like(running))
        for copy in range(8):
            out_ref[copy, :, start : start + 256] = total


def combine_kernel(scale, parts_ref, running_ref, summand_ref, total_ref):
    summand = parts_ref[0]
    for part in range(1, parts_ref.shape[0]):
        summand = summand + parts_ref[part]
    summand = summand / scale
    summand_ref[...] = summand
    total_ref[...] = running_ref[...] + summand


def call(kernel, out, flops, limit, *operands):
    vmem = pl.BlockSpec(memory_space=pltpu.VMEM)
    shapes = jax.tree.map(lambda shape: jax.ShapeDtypeStruct(shape, jnp.float32), out, is_leaf=lambda o: isinstance(o[0], int))
    return pl.pallas_call(
        kernel,
        out_shape=shapes,
        in_specs=[vmem] * len(operands),
        out_specs=jax.tree.map(lambda _: vmem, shapes),
        cost_estimate=pl.CostEstimate(flops=flops, bytes_accessed=4 << 20, transcendentals=0),
        compiler_params=pltpu.CompilerParams(vmem_limit_bytes=limit),
    )(*operands)


def permute(value, moves):
    return lax.ppermute(value, ROW + COL, moves)


def exchange(value):
    return lax.all_to_all(value, COL, 0, 0, tiled=True)


FLOPS, LIMIT = 100_000_000, 4 << 20


def block_product(block, halves, vectors):
    count, width = block.shape
    other = permute(block, partner_moves(1))
    out = ((count, width), (count, width // 2))
    total, running = call(own_block_kernel, out, 2 * FLOPS, LIMIT, block, *halves, vectors)
    return call(other_block_kernel, (8, count, width // 2), 2 * FLOPS, LIMIT, other, *halves, total), running


def product(piece, halves, scale=None, running=None):
    vectors, width = piece.shape
    rows = halves[0].shape[1]
    others = [permute(piece, partner_moves(which)) for which in (1, 2, 3)]
    total = call(own_kernel, (vectors, rows), FLOPS, LIMIT, piece, *halves)
    for which in (1, 2):
        kernel = functools.partial(next_kernel, which)
        total = call(kernel, (vectors, rows), FLOPS, LIMIT, others[which - 1], *halves, total)
    if running is None:
        return call(spread_kernel, (8, vectors, width), FLOPS, LIMIT, others[2], *halves, total)
    kernel = functools.partial(last_kernel, scale)
    return call(kernel, (8, vectors, rows), FLOPS, LIMIT, others[2], *halves, total, running)


def local(matrix, vectors):
    block = permute(vectors, owner_moves())
    halves = prepare(matrix)
    block, halves = lax.optimization_barrier((block, halves))
    partial_value, running = block_product(block, halves, vectors)
    parts = exchange(partial_value)
    for degree in range(1, TERMS):
        kernel = functools.partial(combine_kernel, float(degree * STEPS))
        summand, running = call(kernel, (running.shape,) * 2, 1_000_000, 2 << 20, parts, running)
        piece = permute(summand, owner_moves())
        if degree + 1 < TERMS:
            parts = exchange(product(piece, halves))
    parts = exchange(product(piece, halves, float(TERMS * STEPS), running))
    return functools.reduce(jnp.add, [parts[part] for part in range(8)])


def solution(mesh):
    fine = Mesh(mesh.devices.reshape(tuple(SIZES.values())), tuple(SIZES))
    placed = (P(ROW, COL), P("rep", ROW))
    return jax.shard_map(local, mesh=fine, in_specs=placed, out_specs=P("rep", ROW), check_vma=False)
```

time: 202 us -> 194 us (0.960)
  starting transfers between devices: 22.7 us -> 42.4 us
  blocking collectives: 111 us -> 95.9 us
  waiting for transfers between devices: 51.1 us -> 39 us
    ppermute x12 -> x22, starting transfers between devices: 22.7 us -> 42.4 us  [permute(): return lax.ppermute(value, ROW + COL, moves)]
    all_to_all x6, blocking collectives: 111 us -> 95.9 us  [exchange(): return lax.all_to_all(value, COL, 0, 0, tiled=True)]
    ppermute x12 -> x22, waiting for transfers between devices: 51.1 us -> 39 us  [permute(): return lax.ppermute(value, ROW + COL, moves)]
    pallas_call x18 -> x27, Pallas kernels: 11 us -> 11.2 us  [call(): pl.pallas_call(kernel, out_shape=shapes, in_specs=[vmem] * len(operands),...]
  transfers between devices with their start and end apart: 12 -> 22, of which waited for: 11 -> 15; matrix products, arithmetic and copies ran while one was open for 0% -> 0% of each run, Pallas kernels for 5% -> 6%
where the time goes in v6:
time: 194 us
  blocking collectives  95.9 us (49%)
  starting transfers between devices  42.4 us (22%)
  waiting for transfers between devices  39 us (20%)
  Pallas kernels  15.4 us (8%)
    all_to_all x6, blocking collectives, exchange(): return lax.all_to_all(value, COL, 0, 0, tiled=True)  95.9 us
    ppermute x22, starting transfers between devices, permute(): return lax.ppermute(value, ROW + COL, moves)  42.4 us
    ppermute x22, waiting for transfers between devices, permute(): return lax.ppermute(value, ROW + COL, moves)  39 us
    pallas_call x27, Pallas kernels, call(): pl.pallas_call(kernel, out_shape=shapes, in_specs=[vmem] * len(operands),...  11.2 us
    pallas_call x1, Pallas kernels, prepare(): pl.pallas_call(prepare_kernel, out_shape=(half, half), in_specs=[pl.Block...  4.29 us
  transfers between devices with their start and end apart: 22, of which 15 were waited for; matrix products, arithmetic and copies ran while one was open for 0% of the time, Pallas kernels for 6%

profile of v6, /device:TPU:2, one launch (start us, length us, event | category | flops | bytes accessed | tf_op | source)
XLA Modules:
  0.0 193.6 jit_solution(8750454106298104512)
XLA Ops:
  0.0 7.7 %collective-permute-start = (f32[32,1024]{1,0:T(8,128)}, f32[32,1024]{1,0:T(8,128)S(1)}, u32[]{:S(2)}, u32[]{:S(2)}) collective-permute-start(f32[32,1024]{1,0:T(8,128)} %vectors_ref.1), channel_id=1, source_target_pairs={{0,80},{2,32},{4,0},{6,96},{8,208},{10,160},{12,128},{14,224},{16,... | collective-permute-start | bytes 393224 | tf_op jit(solution)/shard_map/ppermute | solution.py:200
  7.7 4.3 %shard_map.28 = (bf16[2048,1024]{1,0:T(8,128)(2,1)S(1)}, bf16[2048,1024]{1,0:T(8,128)(2,1)S(1)}) custom-call(f32[1024,2048]{1,0:T(8,128)} %a_ref.1), custom_call_target="tpu_custom_call" | custom-call | flops 4000000000 | bytes 8388608 | tf_op jit(solution)/shard_map/pallas_call | solution.py:85
  13.9 3.1 %collective-permute-done.1.x_ref = f32[32,1024]{1,0:T(8,128)S(1)} collective-permute-done((f32[32,1024]{1,0:T(8,128)S(1)}, f32[32,1024]{1,0:T(8,128)S(1)}, u32[]{:S(2)}, u32[]{:S(2)}) %collective-permute-start.1) | collective-permute-done | bytes 131104 | tf_op jit(solution)/shard_map/ppermute | solution.py:200
  17.9 15.4 %all_to_all.30.parts_ref = f32[8,32,512]{2,1,0:T(8,128)S(1)} all-to-all(f32[8,32,512]{2,1,0:T(8,128)S(1)} %shard_map.30), channel_id=1, replica_groups=mesh['xh'=2,'zh'=4,'zl'=2,'xl'=2,'y'=4,'rep'=2] {'xl','y'}, dimensions={0} | all-to-all | bytes 1048576 | tf_op jit(solution)/shard_map/all_to_all | solution.py:204
  33.3 4.0 %collective-permute-start.2 = (f32[32,512]{1,0:T(8,128)S(1)}, f32[32,512]{1,0:T(8,128)S(1)}, u32[]{:S(2)}, u32[]{:S(2)}) collective-permute-start(f32[32,512]{1,0:T(8,128)S(1)} %get-tuple-element.29), channel_id=1, source_target_pairs={{0,80},{2,32},{4,0},{6,96},{8,208},{10,160},{12,128},{14,224},{16,... | collective-permute-start | bytes 196616 | tf_op jit(solution)/shard_map/ppermute | solution.py:200
  37.3 2.9 %collective-permute-done.2.x_ref = f32[32,512]{1,0:T(8,128)S(1)} collective-permute-done((f32[32,512]{1,0:T(8,128)S(1)}, f32[32,512]{1,0:T(8,128)S(1)}, u32[]{:S(2)}, u32[]{:S(2)}) %collective-permute-start.2) | collective-permute-done | bytes 65568 | tf_op jit(solution)/shard_map/ppermute | solution.py:200
  42.0 3.3 %collective-permute-start.3 = (f32[32,512]{1,0:T(8,128)S(1)}, f32[32,512]{1,0:T(8,128)S(1)}, u32[]{:S(2)}, u32[]{:S(2)}) collective-permute-start(f32[32,512]{1,0:T(8,128)S(1)} %collective-permute-done.2.x_ref), channel_id=1, source_target_pairs={{0,144},{2,146},{4,148},{6,150},{8,152},{10,154},{12,156},{14,158}... | collective-permute-start | bytes 196616 | tf_op jit(solution)/shard_map/ppermute | solution.py:200
  49.1 16.7 %all_to_all.31.parts_ref = f32[8,32,512]{2,1,0:T(8,128)S(1)} all-to-all(f32[8,32,512]{2,1,0:T(8,128)S(1)} %shard_map.35), channel_id=1, replica_groups=mesh['xh'=2,'zh'=4,'zl'=2,'xl'=2,'y'=4,'rep'=2] {'xl','y'}, dimensions={0} | all-to-all | bytes 1048576 | tf_op jit(solution)/shard_map/all_to_all | solution.py:204
  67.0 5.6 %collective-permute-done.6.x_ref = f32[32,512]{1,0:T(8,128)S(1)} collective-permute-done((f32[32,512]{1,0:T(8,128)S(1)}, f32[32,512]{1,0:T(8,128)S(1)}, u32[]{:S(2)}, u32[]{:S(2)}) %collective-permute-start.6) | collective-permute-done | bytes 65568 | tf_op jit(solution)/shard_map/ppermute | solution.py:200
  73.2 4.4 %collective-permute-start.7 = (f32[32,512]{1,0:T(8,128)S(1)}, f32[32,512]{1,0:T(8,128)S(1)}, u32[]{:S(2)}, u32[]{:S(2)}) collective-permute-start(f32[32,512]{1,0:T(8,128)S(1)} %collective-permute-done.6.x_ref), channel_id=1, source_target_pairs={{0,144},{2,146},{4,148},{6,150},{8,152},{10,154},{12,156},{14,158}... | collective-permute-start | bytes 196616 | tf_op jit(solution)/shard_map/ppermute | solution.py:200
  80.3 14.7 %all_to_all.32.parts_ref = f32[8,32,512]{2,1,0:T(8,128)S(1)} all-to-all(f32[8,32,512]{2,1,0:T(8,128)S(1)} %shard_map.40), channel_id=1, replica_groups=mesh['xh'=2,'zh'=4,'zl'=2,'xl'=2,'y'=4,'rep'=2] {'xl','y'}, dimensions={0} | all-to-all | bytes 1048576 | tf_op jit(solution)/shard_map/all_to_all | solution.py:204
  95.0 1.9 collective-permute-start.10
  96.9 4.9 %collective-permute-done.10.x_ref = f32[32,512]{1,0:T(8,128)S(1)} collective-permute-done((f32[32,512]{1,0:T(8,128)S(1)}, f32[32,512]{1,0:T(8,128)S(1)}, u32[]{:S(2)}, u32[]{:S(2)}) %collective-permute-start.10) | collective-permute-done | bytes 65568 | tf_op jit(solution)/shard_map/ppermute | solution.py:200
  101.8 2.0 %collective-permute-start.13 = (f32[32,512]{1,0:T(8,128)S(1)}, f32[32,512]{1,0:T(8,128)S(1)}, u32[]{:S(2)}, u32[]{:S(2)}) collective-permute-start(f32[32,512]{1,0:T(8,128)S(1)} %collective-permute-done.10.x_ref), channel_id=1, source_target_pairs={{0,16},{2,18},{4,20},{6,22},{8,24},{10,26},{12,28},{14,30},{16,0},... | collective-permute-start | bytes 196616 | tf_op jit(solution)/shard_map/ppermute | solution.py:200
  105.0 1.8 collective-permute-start.11
  112.2 14.9 %all_to_all.33.parts_ref = f32[8,32,512]{2,1,0:T(8,128)S(1)} all-to-all(f32[8,32,512]{2,1,0:T(8,128)S(1)} %shard_map.45), channel_id=1, replica_groups=mesh['xh'=2,'zh'=4,'zl'=2,'xl'=2,'y'=4,'rep'=2] {'xl','y'}, dimensions={0} | all-to-all | bytes 1048576 | tf_op jit(solution)/shard_map/all_to_all | solution.py:204
  128.3 5.5 %collective-permute-done.14.x_ref = f32[32,512]{1,0:T(8,128)S(1)} collective-permute-done((f32[32,512]{1,0:T(8,128)S(1)}, f32[32,512]{1,0:T(8,128)S(1)}, u32[]{:S(2)}, u32[]{:S(2)}) %collective-permute-start.14) | collective-permute-done | bytes 65568 | tf_op jit(solution)/shard_map/ppermute | solution.py:200
  135.1 3.8 %collective-permute-start.15 = (f32[32,512]{1,0:T(8,128)S(1)}, f32[32,512]{1,0:T(8,128)S(1)}, u32[]{:S(2)}, u32[]{:S(2)}) collective-permute-start(f32[32,512]{1,0:T(8,128)S(1)} %collective-permute-done.14.x_ref), channel_id=1, source_target_pairs={{0,144},{2,146},{4,148},{6,150},{8,152},{10,154},{12,156},{14,158}... | collective-permute-start | bytes 196616 | tf_op jit(solution)/shard_map/ppermute | solution.py:200
  142.2 16.6 %all_to_all.34.parts_ref = f32[8,32,512]{2,1,0:T(8,128)S(1)} all-to-all(f32[8,32,512]{2,1,0:T(8,128)S(1)} %shard_map.50), channel_id=1, replica_groups=mesh['xh'=2,'zh'=4,'zl'=2,'xl'=2,'y'=4,'rep'=2] {'xl','y'}, dimensions={0} | all-to-all | bytes 1048576 | tf_op jit(solution)/shard_map/all_to_all | solution.py:204
  159.0 6.7 %collective-permute-done.18.x_ref = f32[32,512]{1,0:T(8,128)S(1)} collective-permute-done((f32[32,512]{1,0:T(8,128)S(1)}, f32[32,512]{1,0:T(8,128)S(1)}, u32[]{:S(2)}, u32[]{:S(2)}) %collective-permute-start.18) | collective-permute-done | bytes 65568 | tf_op jit(solution)/shard_map/ppermute | solution.py:200
  165.6 2.4 %collective-permute-start.21 = (f32[32,512]{1,0:T(8,128)S(1)}, f32[32,512]{1,0:T(8,128)S(1)}, u32[]{:S(2)}, u32[]{:S(2)}) collective-permute-start(f32[32,512]{1,0:T(8,128)S(1)} %collective-permute-done.18.x_ref), channel_id=1, source_target_pairs={{0,16},{2,18},{4,20},{6,22},{8,24},{10,26},{12,28},{14,30},{16,0},... | collective-permute-start | bytes 196616 | tf_op jit(solution)/shard_map/ppermute | solution.py:200
  168.0 3.0 %collective-permute-start.19 = (f32[32,512]{1,0:T(8,128)S(1)}, f32[32,512]{1,0:T(8,128)S(1)}, u32[]{:S(2)}, u32[]{:S(2)}) collective-permute-start(f32[32,512]{1,0:T(8,128)S(1)} %collective-permute-done.18.x_ref), channel_id=1, source_target_pairs={{0,144},{2,146},{4,148},{6,150},{8,152},{10,154},{12,156},{14,158}... | collective-permute-start | bytes 196616 | tf_op jit(solution)/shard_map/ppermute | solution.py:200
  171.9 1.9 collective-permute-done.20.x_ref
  175.2 17.7 %all_to_all.35 = f32[8,32,1024]{2,1,0:T(8,128)S(1)} all-to-all(f32[8,32,1024]{2,1,0:T(8,128)S(1)} %shard_map.55), channel_id=1, replica_groups=mesh['xh'=2,'zh'=4,'zl'=2,'xl'=2,'y'=4,'rep'=2] {'xl','y'}, dimensions={0} | all-to-all | bytes 2097152 | tf_op jit(solution)/shard_map/all_to_all | solution.py:204
  (57 shorter events, 28.4 us)
Async XLA Ops:
  0.0 13.1 %copy-start = (f32[32,1024]{1,0:T(8,128)S(1)}, f32[32,1024]{1,0:T(8,128)}, u32[]{:S(2)}) copy-start(f32[32,1024]{1,0:T(8,128)} %vectors_ref.1) | copy-start | bytes 393220
  0.0 12.0 %collective-permute-start = (f32[32,1024]{1,0:T(8,128)}, f32[32,1024]{1,0:T(8,128)S(1)}, u32[]{:S(2)}, u32[]{:S(2)}) collective-permute-start(f32[32,1024]{1,0:T(8,128)} %vectors_ref.1), channel_id=1, source_target_pairs={{0,80},{2,32},{4,0},{6,96},{8,208},{10,160},{12,128},{14,224},{16,... | collective-permute-start | bytes 393224 | tf_op jit(solution)/shard_map/ppermute | solution.py:200
  12.0 5.1 %collective-permute-start.1 = (f32[32,1024]{1,0:T(8,128)S(1)}, f32[32,1024]{1,0:T(8,128)S(1)}, u32[]{:S(2)}, u32[]{:S(2)}) collective-permute-start(f32[32,1024]{1,0:T(8,128)S(1)} %collective-permute-done.x_ref), channel_id=1, source_target_pairs={{0,16},{2,18},{4,20},{6,22},{8,24},{10,26},{12,28},{14,30},{16,0},... | collective-permute-start | bytes 393224 | tf_op jit(solution)/shard_map/ppermute | solution.py:200
  33.3 7.0 %collective-permute-start.2 = (f32[32,512]{1,0:T(8,128)S(1)}, f32[32,512]{1,0:T(8,128)S(1)}, u32[]{:S(2)}, u32[]{:S(2)}) collective-permute-start(f32[32,512]{1,0:T(8,128)S(1)} %get-tuple-element.29), channel_id=1, source_target_pairs={{0,80},{2,32},{4,0},{6,96},{8,208},{10,160},{12,128},{14,224},{16,... | collective-permute-start | bytes 196616 | tf_op jit(solution)/shard_map/ppermute | solution.py:200
  40.2 5.5 %collective-permute-start.5 = (f32[32,512]{1,0:T(8,128)S(1)}, f32[32,512]{1,0:T(8,128)S(1)}, u32[]{:S(2)}, u32[]{:S(2)}) collective-permute-start(f32[32,512]{1,0:T(8,128)S(1)} %collective-permute-done.2.x_ref), channel_id=1, source_target_pairs={{0,16},{2,18},{4,20},{6,22},{8,24},{10,26},{12,28},{14,30},{16,0},... | collective-permute-start | bytes 196616 | tf_op jit(solution)/shard_map/ppermute | solution.py:200
  41.7 5.8 %collective-permute-start.4 = (f32[32,512]{1,0:T(8,128)S(1)}, f32[32,512]{1,0:T(8,128)S(1)}, u32[]{:S(2)}, u32[]{:S(2)}) collective-permute-start(f32[32,512]{1,0:T(8,128)S(1)} %collective-permute-done.2.x_ref), channel_id=1, source_target_pairs={{0,128},{2,130},{4,132},{6,134},{8,136},{10,138},{12,140},{14,142}... | collective-permute-start | bytes 196616 | tf_op jit(solution)/shard_map/ppermute | solution.py:200
  42.0 6.7 %collective-permute-start.3 = (f32[32,512]{1,0:T(8,128)S(1)}, f32[32,512]{1,0:T(8,128)S(1)}, u32[]{:S(2)}, u32[]{:S(2)}) collective-permute-start(f32[32,512]{1,0:T(8,128)S(1)} %collective-permute-done.2.x_ref), channel_id=1, source_target_pairs={{0,144},{2,146},{4,148},{6,150},{8,152},{10,154},{12,156},{14,158}... | collective-permute-start | bytes 196616 | tf_op jit(solution)/shard_map/ppermute | solution.py:200
  65.9 6.7 %collective-permute-start.6 = (f32[32,512]{1,0:T(8,128)S(1)}, f32[32,512]{1,0:T(8,128)S(1)}, u32[]{:S(2)}, u32[]{:S(2)}) collective-permute-start(f32[32,512]{1,0:T(8,128)S(1)} %get-tuple-element.31), channel_id=1, source_target_pairs={{0,80},{2,32},{4,0},{6,96},{8,208},{10,160},{12,128},{14,224},{16,... | collective-permute-start | bytes 196616 | tf_op jit(solution)/shard_map/ppermute | solution.py:200
  72.6 5.4 %collective-permute-start.9 = (f32[32,512]{1,0:T(8,128)S(1)}, f32[32,512]{1,0:T(8,128)S(1)}, u32[]{:S(2)}, u32[]{:S(2)}) collective-permute-start(f32[32,512]{1,0:T(8,128)S(1)} %collective-permute-done.6.x_ref), channel_id=1, source_target_pairs={{0,16},{2,18},{4,20},{6,22},{8,24},{10,26},{12,28},{14,30},{16,0},... | collective-permute-start | bytes 196616 | tf_op jit(solution)/shard_map/ppermute | solution.py:200
  73.2 5.8 %collective-permute-start.8 = (f32[32,512]{1,0:T(8,128)S(1)}, f32[32,512]{1,0:T(8,128)S(1)}, u32[]{:S(2)}, u32[]{:S(2)}) collective-permute-start(f32[32,512]{1,0:T(8,128)S(1)} %collective-permute-done.6.x_ref), channel_id=1, source_target_pairs={{0,128},{2,130},{4,132},{6,134},{8,136},{10,138},{12,140},{14,142}... | collective-permute-start | bytes 196616 | tf_op jit(solution)/shard_map/ppermute | solution.py:200
  73.2 6.7 %collective-permute-start.7 = (f32[32,512]{1,0:T(8,128)S(1)}, f32[32,512]{1,0:T(8,128)S(1)}, u32[]{:S(2)}, u32[]{:S(2)}) collective-permute-start(f32[32,512]{1,0:T(8,128)S(1)} %collective-permute-done.6.x_ref), channel_id=1, source_target_pairs={{0,144},{2,146},{4,148},{6,150},{8,152},{10,154},{12,156},{14,158}... | collective-permute-start | bytes 196616 | tf_op jit(solution)/shard_map/ppermute | solution.py:200
  95.0 6.7 %collective-permute-start.10 = (f32[32,512]{1,0:T(8,128)S(1)}, f32[32,512]{1,0:T(8,128)S(1)}, u32[]{:S(2)}, u32[]{:S(2)}) collective-permute-start(f32[32,512]{1,0:T(8,128)S(1)} %get-tuple-element.33), channel_id=1, source_target_pairs={{0,80},{2,32},{4,0},{6,96},{8,208},{10,160},{12,128},{14,224},{16,... | collective-permute-start | bytes 196616 | tf_op jit(solution)/shard_map/ppermute | solution.py:200
  101.8 5.5 %collective-permute-start.13 = (f32[32,512]{1,0:T(8,128)S(1)}, f32[32,512]{1,0:T(8,128)S(1)}, u32[]{:S(2)}, u32[]{:S(2)}) collective-permute-start(f32[32,512]{1,0:T(8,128)S(1)} %collective-permute-done.10.x_ref), channel_id=1, source_target_pairs={{0,16},{2,18},{4,20},{6,22},{8,24},{10,26},{12,28},{14,30},{16,0},... | collective-permute-start | bytes 196616 | tf_op jit(solution)/shard_map/ppermute | solution.py:200
  103.8 5.8 %collective-permute-start.12 = (f32[32,512]{1,0:T(8,128)S(1)}, f32[32,512]{1,0:T(8,128)S(1)}, u32[]{:S(2)}, u32[]{:S(2)}) collective-permute-start(f32[32,512]{1,0:T(8,128)S(1)} %collective-permute-done.10.x_ref), channel_id=1, source_target_pairs={{0,128},{2,130},{4,132},{6,134},{8,136},{10,138},{12,140},{14,142}... | collective-permute-start | bytes 196616 | tf_op jit(solution)/shard_map/ppermute | solution.py:200
  105.0 6.8 %collective-permute-start.11 = (f32[32,512]{1,0:T(8,128)S(1)}, f32[32,512]{1,0:T(8,128)S(1)}, u32[]{:S(2)}, u32[]{:S(2)}) collective-permute-start(f32[32,512]{1,0:T(8,128)S(1)} %collective-permute-done.10.x_ref), channel_id=1, source_target_pairs={{0,144},{2,146},{4,148},{6,150},{8,152},{10,154},{12,156},{14,158}... | collective-permute-start | bytes 196616 | tf_op jit(solution)/shard_map/ppermute | solution.py:200
  127.1 6.7 %collective-permute-start.14 = (f32[32,512]{1,0:T(8,128)S(1)}, f32[32,512]{1,0:T(8,128)S(1)}, u32[]{:S(2)}, u32[]{:S(2)}) collective-permute-start(f32[32,512]{1,0:T(8,128)S(1)} %get-tuple-element.35), channel_id=1, source_target_pairs={{0,80},{2,32},{4,0},{6,96},{8,208},{10,160},{12,128},{14,224},{16,... | collective-permute-start | bytes 196616 | tf_op jit(solution)/shard_map/ppermute | solution.py:200
  133.9 5.4 %collective-permute-start.17 = (f32[32,512]{1,0:T(8,128)S(1)}, f32[32,512]{1,0:T(8,128)S(1)}, u32[]{:S(2)}, u32[]{:S(2)}) collective-permute-start(f32[32,512]{1,0:T(8,128)S(1)} %collective-permute-done.14.x_ref), channel_id=1, source_target_pairs={{0,16},{2,18},{4,20},{6,22},{8,24},{10,26},{12,28},{14,30},{16,0},... | collective-permute-start | bytes 196616 | tf_op jit(solution)/shard_map/ppermute | solution.py:200
  133.9 5.9 %collective-permute-start.16 = (f32[32,512]{1,0:T(8,128)S(1)}, f32[32,512]{1,0:T(8,128)S(1)}, u32[]{:S(2)}, u32[]{:S(2)}) collective-permute-start(f32[32,512]{1,0:T(8,128)S(1)} %collective-permute-done.14.x_ref), channel_id=1, source_target_pairs={{0,128},{2,130},{4,132},{6,134},{8,136},{10,138},{12,140},{14,142}... | collective-permute-start | bytes 196616 | tf_op jit(solution)/shard_map/ppermute | solution.py:200
  135.1 6.7 %collective-permute-start.15 = (f32[32,512]{1,0:T(8,128)S(1)}, f32[32,512]{1,0:T(8,128)S(1)}, u32[]{:S(2)}, u32[]{:S(2)}) collective-permute-start(f32[32,512]{1,0:T(8,128)S(1)} %collective-permute-done.14.x_ref), channel_id=1, source_target_pairs={{0,144},{2,146},{4,148},{6,150},{8,152},{10,154},{12,156},{14,158}... | collective-permute-start | bytes 196616 | tf_op jit(solution)/shard_map/ppermute | solution.py:200
  158.9 6.8 %collective-permute-start.18 = (f32[32,512]{1,0:T(8,128)S(1)}, f32[32,512]{1,0:T(8,128)S(1)}, u32[]{:S(2)}, u32[]{:S(2)}) collective-permute-start(f32[32,512]{1,0:T(8,128)S(1)} %get-tuple-element.37), channel_id=1, source_target_pairs={{0,80},{2,32},{4,0},{6,96},{8,208},{10,160},{12,128},{14,224},{16,... | collective-permute-start | bytes 196616 | tf_op jit(solution)/shard_map/ppermute | solution.py:200
  165.6 5.8 %collective-permute-start.21 = (f32[32,512]{1,0:T(8,128)S(1)}, f32[32,512]{1,0:T(8,128)S(1)}, u32[]{:S(2)}, u32[]{:S(2)}) collective-permute-start(f32[32,512]{1,0:T(8,128)S(1)} %collective-permute-done.18.x_ref), channel_id=1, source_target_pairs={{0,16},{2,18},{4,20},{6,22},{8,24},{10,26},{12,28},{14,30},{16,0},... | collective-permute-start | bytes 196616 | tf_op jit(solution)/shard_map/ppermute | solution.py:200
  168.0 5.8 %collective-permute-start.20 = (f32[32,512]{1,0:T(8,128)S(1)}, f32[32,512]{1,0:T(8,128)S(1)}, u32[]{:S(2)}, u32[]{:S(2)}) collective-permute-start(f32[32,512]{1,0:T(8,128)S(1)} %collective-permute-done.18.x_ref), channel_id=1, source_target_pairs={{0,128},{2,130},{4,132},{6,134},{8,136},{10,138},{12,140},{14,142}... | collective-permute-start | bytes 196616 | tf_op jit(solution)/shard_map/ppermute | solution.py:200
  168.0 6.7 %collective-permute-start.19 = (f32[32,512]{1,0:T(8,128)S(1)}, f32[32,512]{1,0:T(8,128)S(1)}, u32[]{:S(2)}, u32[]{:S(2)}) collective-permute-start(f32[32,512]{1,0:T(8,128)S(1)} %collective-permute-done.18.x_ref), channel_id=1, source_target_pairs={{0,144},{2,146},{4,148},{6,150},{8,152},{10,154},{12,156},{14,158}... | collective-permute-start | bytes 196616 | tf_op jit(solution)/shard_map/ppermute | solution.py:200

commit v7 on v6

--- a/solution.py
+++ b/solution.py
@@ -22,6 +22,7 @@
     for y in range(4)
 ]
 FAR = 2
+HANDED = 8
 
 
 def index(xh, zh, zl, xl, y):
@@ -100,11 +101,12 @@
     depth = high_ref.shape[0] // 4
     operands = []
     for quarter, piece in pieces:
-        x_high, x_low = split(piece)
-        rows = slice(quarter * depth, (quarter + 1) * depth)
-        operands.append((rows, x_high, jnp.concatenate([x_high, x_low], axis=0)))
-    for start in range(0, high_ref.shape[1], 256):
-        columns = slice(start, start + 256)
+        x_high = piece.astype(jnp.bfloat16)
+        high = x_high.astype(jnp.float32)
+        both = jnp.concatenate([high, piece - high], axis=0).astype(jnp.bfloat16)
+        operands.append((slice(quarter * depth, (quarter + 1) * depth), x_high, both))
+
+    def tile(columns):
         total = None
         for rows, x_high, both in operands:
             vectors = x_high.shape[0]
@@ -112,9 +114,31 @@
             second = jnp.dot(x_high, low_ref[rows, columns], preferred_element_type=jnp.float32)
             value = first[:vectors] + (first[vectors:] + second)
             total = value if total is None else total + value
-        if before_ref is not None:
-            total = before_ref[:, columns] + total
-        yield start, total
+        return total if before_ref is None else before_ref[:, columns] + total
+
+    return tile
+
+
+def store(tile, out_ref):
+    def step(number, carry):
+        columns = pl.ds(pl.multiple_of(number * 256, 256), 256)
+        out_ref[:, columns] = tile(columns)
+        return carry
+
+    lax.fori_loop(0, out_ref.shape[1] // 256, step, 0)
+
+
+def spread(tile, out_ref):
+    width = out_ref.shape[2]
+
+    def step(side, carry):
+        for within in range(0, width, 256):
+            total = tile(pl.ds(pl.multiple_of(side * width + within, 256), 256))
+            for copy in range(4):
+                out_ref[side * 4 + copy, :, within : within + 256] = total
+        return carry
+
+    lax.fori_loop(0, 2, step, 0)
 
 
 def block_pieces(quarters, x_ref):
@@ -124,54 +148,45 @@
     return [(quarter, x_ref[:, pl.ds(place, width)]) for quarter, place in zip(quarters, at)]
 
 
-def store(start, total, out_ref):
-    out_ref[:, start : start + 256] = total
-
-
-def spread(start, total, out_ref):
-    side, within = divmod(start, out_ref.shape[2])
-    for copy in range(4):
-        out_ref[side * 4 + copy, :, within : within + 256] = total
-
-
 def own_block_kernel(x_ref, high_ref, low_ref, vectors_ref, out_ref, running_ref):
     width = running_ref.shape[1]
     running_ref[...] = vectors_ref[:, pl.ds(pl.multiple_of(lax.axis_index("xl") * width, width), width)]
-    for start, total in tiles(block_pieces((0, 2), x_ref), high_ref, low_ref):
-        store(start, total, out_ref)
+    store(tiles(block_pieces((0, 2), x_ref), high_ref, low_ref), out_ref)
 
 
 def other_block_kernel(x_ref, high_ref, low_ref, before_ref, out_ref):
-    for start, total in tiles(block_pieces((1, 3), x_ref), high_ref, low_ref, before_ref):
-        spread(start, total, out_ref)
+    spread(tiles(block_pieces((1, 3), x_ref), high_ref, low_ref, before_ref), out_ref)
 
 
 def own_kernel(x_ref, high_ref, low_ref, out_ref):
-    for start, total in tiles([(0, x_ref[...])], high_ref, low_ref):
-        store(start, total, out_ref)
+    store(tiles([(0, x_ref[...])], high_ref, low_ref), out_ref)
 
 
 def next_kernel(which, x_ref, high_ref, low_ref, before_ref, out_ref):
-    for start, total in tiles([(which, x_ref[...])], high_ref, low_ref, before_ref):
-        store(start, total, out_ref)
+    store(tiles([(which, x_ref[...])], high_ref, low_ref, before_ref), out_ref)
 
 
 def spread_kernel(x_ref, high_ref, low_ref, before_ref, out_ref):
-    for start, total in tiles([(3, x_ref[...])], high_ref, low_ref, before_ref):
-        spread(start, total, out_ref)
+    spread(tiles([(3, x_ref[...])], high_ref, low_ref, before_ref), out_ref)
 
 
 def last_kernel(scale, x_ref, high_ref, low_ref, before_ref, running_ref, out_ref):
     width = running_ref.shape[1]
     mine = lax.axis_index("xl")
     first = lax.axis_index("y") == 0
-    for start, total in tiles([(3, x_ref[...])], high_ref, low_ref, before_ref):
-        side, within = divmod(start, width)
-        running = running_ref[:, within : within + 256]
-        adds = jnp.logical_and(first, mine == side)
-        total = total / scale + jnp.where(adds, running, jnp.zeros_like(running))
-        for copy in range(8):
-            out_ref[copy, :, start : start + 256] = total
+    tile = tiles([(3, x_ref[...])], high_ref, low_ref, before_ref)
+
+    def step(side, carry):
+        for within in range(0, width, 256):
+            columns = pl.ds(pl.multiple_of(side * width + within, 256), 256)
+            running = running_ref[:, within : within + 256]
+            adds = jnp.logical_and(first, mine == side)
+            total = tile(columns) / scale + jnp.where(adds, running, jnp.zeros_like(running))
+            for copy in range(8):
+                out_ref[copy, :, columns] = total
+        return carry
+
+    lax.fori_loop(0, 2, step, 0)
 
 
 def combine_kernel(scale, parts_ref, running_ref, summand_ref, total_ref):
@@ -196,8 +211,9 @@
     )(*operands)
 
 
-def permute(value, moves):
-    return lax.ppermute(value, ROW + COL, moves)
+def permute(value, moves, rep):
+    pairs = [(source * 2 + rep, target * 2 + rep) for source, target in moves]
+    return lax.ppermute(value, ROW + COL + ("rep",), pairs)
 
 
 def exchange(value):
@@ -207,18 +223,18 @@
 FLOPS, LIMIT = 100_000_000, 4 << 20
 
 
-def block_product(block, halves, vectors):
+def block_product(block, halves, vectors, rep):
     count, width = block.shape
-    other = permute(block, partner_moves(1))
+    other = permute(block, partner_moves(1), rep)
     out = ((count, width), (count, width // 2))
     total, running = call(own_block_kernel, out, 2 * FLOPS, LIMIT, block, *halves, vectors)
     return call(other_block_kernel, (8, count, width // 2), 2 * FLOPS, LIMIT, other, *halves, total), running
 
 
-def product(piece, halves, scale=None, running=None):
+def product(piece, halves, rep, scale=None, running=None):
     vectors, width = piece.shape
     rows = halves[0].shape[1]
-    others = [permute(piece, partner_moves(which)) for which in (1, 2, 3)]
+    others = [permute(piece, partner_moves(which), rep) for which in (1, 2, 3)]
     total = call(own_kernel, (vectors, rows), FLOPS, LIMIT, piece, *halves)
     for which in (1, 2):
         kernel = functools.partial(next_kernel, which)
@@ -229,20 +245,39 @@
     return call(kernel, (8, vectors, rows), FLOPS, LIMIT, others[2], *halves, total, running)
 
 
-def local(matrix, vectors):
-    block = permute(vectors, owner_moves())
+def series(matrix, vectors, rep):
+    block = permute(vectors, owner_moves(), rep)
     halves = prepare(matrix)
     block, halves = lax.optimization_barrier((block, halves))
-    partial_value, running = block_product(block, halves, vectors)
+    partial_value, running = block_product(block, halves, vectors, rep)
     parts = exchange(partial_value)
     for degree in range(1, TERMS):
         kernel = functools.partial(combine_kernel, float(degree * STEPS))
         summand, running = call(kernel, (running.shape,) * 2, 1_000_000, 2 << 20, parts, running)
-        piece = permute(summand, owner_moves())
+        piece = permute(summand, owner_moves(), rep)
         if degree + 1 < TERMS:
-            parts = exchange(product(piece, halves))
-    parts = exchange(product(piece, halves, float(TERMS * STEPS), running))
+            parts = exchange(product(piece, halves, rep))
+    parts = exchange(product(piece, halves, rep, float(TERMS * STEPS), running))
     return functools.reduce(jnp.add, [parts[part] for part in range(8)])
+
+
+def local(matrix, vectors):
+    count = vectors.shape[0]
+    kept = count - HANDED
+    handed = lax.ppermute(vectors[kept:], "rep", [(0, 1)])
+
+    def most(matrix, vectors, handed):
+        result = series(matrix, jnp.concatenate([vectors, handed], axis=0), 1)
+        return result[:count], result[count:]
+
+    def fewer(matrix, vectors, handed):
+        result, handed = lax.optimization_barrier((series(matrix, vectors[:kept], 0), handed))
+        return jnp.concatenate([result, handed], axis=0), handed
+
+    takes = lax.axis_index("rep") == 1
+    result, handed = lax.cond(takes, most, fewer, matrix, vectors, handed)
+    back = lax.ppermute(handed, "rep", [(1, 0)])
+    return jnp.concatenate([result[:kept], jnp.where(takes, result[kept:], back)], axis=0)
 
 
 def solution(mesh):

time: 194 us -> 241 us (1.24); the launches traced: 194 us -> 238 us
  starting transfers between devices: 42.4 us -> 89.9 us
  Pallas kernels: 15.4 us -> 22.2 us
  blocking collectives: 95.9 us -> 89.7 us
  waiting for transfers between devices: 39 us -> 33.5 us
    ppermute x22 -> x24, starting transfers between devices: 42.4 us -> 89.9 us  [the longest x22 86.9 us: permute(): return lax.ppermute(value, ROW + COL + ('rep',), pairs)]
    pallas_call x27, Pallas kernels: 11.2 us -> 17.9 us  [call(): pl.pallas_call(kernel, out_shape=shapes, in_specs=[vmem] * len(operands),...]
    all_to_all x6, blocking collectives: 95.9 us -> 89.7 us  [exchange(): return lax.all_to_all(value, COL, 0, 0, tiled=True)]
    ppermute x22 -> x24, waiting for transfers between devices: 39 us -> 33.5 us  [the longest x22 30.9 us: permute(): return lax.ppermute(value, ROW + COL + ('rep',), pairs)]
  transfers between devices with their start and end apart: 22 -> 24, of which waited for: 15 -> 12; matrix products, arithmetic and copies ran while one was open for 0% -> 0% of each run, Pallas kernels for 6% -> 8%
where the time goes in v7:
time: 241 us; the launch traced here: 238 us
  starting transfers between devices  89.9 us (37%)
  blocking collectives  89.7 us (37%)
  waiting for transfers between devices  33.5 us (14%)
  Pallas kernels  22.2 us (9%)
    all_to_all x6, blocking collectives, exchange(): return lax.all_to_all(value, COL, 0, 0, tiled=True)  89.7 us
    ppermute x22, starting transfers between devices, permute(): return lax.ppermute(value, ROW + COL + ('rep',), pairs)  86.9 us
    ppermute x22, waiting for transfers between devices, permute(): return lax.ppermute(value, ROW + COL + ('rep',), pairs)  30.9 us
    pallas_call x27, Pallas kernels, call(): pl.pallas_call(kernel, out_shape=shapes, in_specs=[vmem] * len(operands),...  17.9 us
  transfers between devices with their start and end apart: 24, of which 12 were waited for; matrix products, arithmetic and copies ran while one was open for 0% of the time, Pallas kernels for 8%

profile of v7, /device:TPU:2, one launch (start us, length us, event | category | flops | bytes accessed | tf_op | source)
XLA Modules:
  0.0 238.2 jit_solution(11425769603192593730)
XLA Ops:
  3.3 231.0 %conditional.1 = (bf16[32,1024]{1,0:T(8,128)(2,1)S(1)}, f32[8,1024]{1,0:T(8,128)S(1)}, f32[24,1024]{1,0:T(8,128)S(1)}, f32[8,1024]{1,0:T(8,128)S(1)}) conditional(s32[]{:T(128)} %convert_element_type.3, (f32[32,1024]{1,0:T(8,128)}, f32[1024,2048]{1,0:T(8,128)}, f32[8,1024]{1,0:T(8,128)S(1)}) %tuple.18, (f32[32,1024]{1,0:T(8,128)}, ...), branch_computations={%region_0.0_spmd, %region_1.0_spmd} | conditional | flops 6405300224 | bytes 140936080 | solution.py:278
  4.2 9.6 %collective-permute-start = (f32[24,1024]{1,0:T(8,128)S(1)}, f32[24,1024]{1,0:T(8,128)S(1)}, u32[]{:S(2)}, u32[]{:S(2)}) collective-permute-start(f32[24,1024]{1,0:T(8,128)S(1)} %slice.50.vectors_ref), channel_id=1, source_target_pairs={{0,80},{2,32},{4,0},{6,96},{8,208},{10,160},{12,128},{14,224},{16,... | collective-permute-start | bytes 294920 | tf_op jit(solution)/shard_map/cond/branch_0_fun/ppermute | solution.py:216
  13.8 4.3 %branch_0_fun.28 = (bf16[2048,1024]{1,0:T(8,128)(2,1)S(1)}, bf16[2048,1024]{1,0:T(8,128)(2,1)S(1)}) custom-call(f32[1024,2048]{1,0:T(8,128)} %get-tuple-element.20.a_ref), custom_call_target="tpu_custom_call" | custom-call | flops 4000000000 | bytes 8388608 | tf_op jit(solution)/shard_map/cond/branch_0_fun/pallas_call | solution.py:86
  22.3 3.3 %collective-permute-done.1.x_ref = f32[24,1024]{1,0:T(8,128)S(1)} collective-permute-done((f32[24,1024]{1,0:T(8,128)S(1)}, f32[24,1024]{1,0:T(8,128)S(1)}, u32[]{:S(2)}, u32[]{:S(2)}) %collective-permute-start.1) | collective-permute-done | bytes 98336 | tf_op jit(solution)/shard_map/cond/branch_0_fun/ppermute | solution.py:216
  26.5 15.0 %all_to_all.48.parts_ref = f32[8,24,512]{2,1,0:T(8,128)S(1)} all-to-all(f32[8,24,512]{2,1,0:T(8,128)S(1)} %branch_0_fun.30), channel_id=1, replica_groups=mesh['xh'=2,'zh'=4,'zl'=2,'xl'=2,'y'=4,'rep'=2] {'xl','y'}, dimensions={0} | all-to-all | bytes 786432 | tf_op jit(solution)/shard_map/cond/branch_0_fun/all_to_all | solution.py:220
  41.5 7.6 %collective-permute-start.2 = (f32[24,512]{1,0:T(8,128)S(1)}, f32[24,512]{1,0:T(8,128)S(1)}, u32[]{:S(2)}, u32[]{:S(2)}) collective-permute-start(f32[24,512]{1,0:T(8,128)S(1)} %get-tuple-element.28), channel_id=1, source_target_pairs={{0,80},{2,32},{4,0},{6,96},{8,208},{10,160},{12,128},{14,224},{16,... | collective-permute-start | bytes 147464 | tf_op jit(solution)/shard_map/cond/branch_0_fun/ppermute | solution.py:216
  56.7 4.9 %collective-permute-start.3 = (f32[24,512]{1,0:T(8,128)S(1)}, f32[24,512]{1,0:T(8,128)S(1)}, u32[]{:S(2)}, u32[]{:S(2)}) collective-permute-start(f32[24,512]{1,0:T(8,128)S(1)} %collective-permute-done.2.x_ref), channel_id=1, source_target_pairs={{0,144},{2,146},{4,148},{6,150},{8,152},{10,154},{12,156},{14,158}... | collective-permute-start | bytes 147464 | tf_op jit(solution)/shard_map/cond/branch_0_fun/ppermute | solution.py:216
  65.7 15.8 %all_to_all.49.parts_ref = f32[8,24,512]{2,1,0:T(8,128)S(1)} all-to-all(f32[8,24,512]{2,1,0:T(8,128)S(1)} %branch_0_fun.35), channel_id=1, replica_groups=mesh['xh'=2,'zh'=4,'zl'=2,'xl'=2,'y'=4,'rep'=2] {'xl','y'}, dimensions={0} | all-to-all | bytes 786432 | tf_op jit(solution)/shard_map/cond/branch_0_fun/all_to_all | solution.py:220
  81.5 5.9 %collective-permute-start.6 = (f32[24,512]{1,0:T(8,128)S(1)}, f32[24,512]{1,0:T(8,128)S(1)}, u32[]{:S(2)}, u32[]{:S(2)}) collective-permute-start(f32[24,512]{1,0:T(8,128)S(1)} %get-tuple-element.30), channel_id=1, source_target_pairs={{0,80},{2,32},{4,0},{6,96},{8,208},{10,160},{12,128},{14,224},{16,... | collective-permute-start | bytes 147464 | tf_op jit(solution)/shard_map/cond/branch_0_fun/ppermute | solution.py:216
  87.4 3.4 %collective-permute-done.6.x_ref = f32[24,512]{1,0:T(8,128)S(1)} collective-permute-done((f32[24,512]{1,0:T(8,128)S(1)}, f32[24,512]{1,0:T(8,128)S(1)}, u32[]{:S(2)}, u32[]{:S(2)}) %collective-permute-start.6) | collective-permute-done | bytes 49184 | tf_op jit(solution)/shard_map/cond/branch_0_fun/ppermute | solution.py:216
  95.5 6.0 %collective-permute-start.7 = (f32[24,512]{1,0:T(8,128)S(1)}, f32[24,512]{1,0:T(8,128)S(1)}, u32[]{:S(2)}, u32[]{:S(2)}) collective-permute-start(f32[24,512]{1,0:T(8,128)S(1)} %collective-permute-done.6.x_ref), channel_id=1, source_target_pairs={{0,144},{2,146},{4,148},{6,150},{8,152},{10,154},{12,156},{14,158}... | collective-permute-start | bytes 147464 | tf_op jit(solution)/shard_map/cond/branch_0_fun/ppermute | solution.py:216
  104.7 14.5 %all_to_all.50.parts_ref = f32[8,24,512]{2,1,0:T(8,128)S(1)} all-to-all(f32[8,24,512]{2,1,0:T(8,128)S(1)} %branch_0_fun.40), channel_id=1, replica_groups=mesh['xh'=2,'zh'=4,'zl'=2,'xl'=2,'y'=4,'rep'=2] {'xl','y'}, dimensions={0} | all-to-all | bytes 786432 | tf_op jit(solution)/shard_map/cond/branch_0_fun/all_to_all | solution.py:220
  119.3 3.5 %collective-permute-start.10 = (f32[24,512]{1,0:T(8,128)S(1)}, f32[24,512]{1,0:T(8,128)S(1)}, u32[]{:S(2)}, u32[]{:S(2)}) collective-permute-start(f32[24,512]{1,0:T(8,128)S(1)} %get-tuple-element.32), channel_id=1, source_target_pairs={{0,80},{2,32},{4,0},{6,96},{8,208},{10,160},{12,128},{14,224},{16,... | collective-permute-start | bytes 147464 | tf_op jit(solution)/shard_map/cond/branch_0_fun/ppermute | solution.py:216
  122.8 5.2 %collective-permute-done.10.x_ref = f32[24,512]{1,0:T(8,128)S(1)} collective-permute-done((f32[24,512]{1,0:T(8,128)S(1)}, f32[24,512]{1,0:T(8,128)S(1)}, u32[]{:S(2)}, u32[]{:S(2)}) %collective-permute-start.10) | collective-permute-done | bytes 49184 | tf_op jit(solution)/shard_map/cond/branch_0_fun/ppermute | solution.py:216
  134.1 4.6 %collective-permute-start.11 = (f32[24,512]{1,0:T(8,128)S(1)}, f32[24,512]{1,0:T(8,128)S(1)}, u32[]{:S(2)}, u32[]{:S(2)}) collective-permute-start(f32[24,512]{1,0:T(8,128)S(1)} %collective-permute-done.10.x_ref), channel_id=1, source_target_pairs={{0,144},{2,146},{4,148},{6,150},{8,152},{10,154},{12,156},{14,158}... | collective-permute-start | bytes 147464 | tf_op jit(solution)/shard_map/cond/branch_0_fun/ppermute | solution.py:216
  143.1 14.4 %all_to_all.51.parts_ref = f32[8,24,512]{2,1,0:T(8,128)S(1)} all-to-all(f32[8,24,512]{2,1,0:T(8,128)S(1)} %branch_0_fun.45), channel_id=1, replica_groups=mesh['xh'=2,'zh'=4,'zl'=2,'xl'=2,'y'=4,'rep'=2] {'xl','y'}, dimensions={0} | all-to-all | bytes 786432 | tf_op jit(solution)/shard_map/cond/branch_0_fun/all_to_all | solution.py:220
  159.5 6.5 %collective-permute-done.14.x_ref = f32[24,512]{1,0:T(8,128)S(1)} collective-permute-done((f32[24,512]{1,0:T(8,128)S(1)}, f32[24,512]{1,0:T(8,128)S(1)}, u32[]{:S(2)}, u32[]{:S(2)}) %collective-permute-start.14) | collective-permute-done | bytes 49184 | tf_op jit(solution)/shard_map/cond/branch_0_fun/ppermute | solution.py:216
  165.9 3.6 %collective-permute-start.17 = (f32[24,512]{1,0:T(8,128)S(1)}, f32[24,512]{1,0:T(8,128)S(1)}, u32[]{:S(2)}, u32[]{:S(2)}) collective-permute-start(f32[24,512]{1,0:T(8,128)S(1)} %collective-permute-done.14.x_ref), channel_id=1, source_target_pairs={{0,16},{2,18},{4,20},{6,22},{8,24},{10,26},{12,28},{14,30},{16,0},... | collective-permute-start | bytes 147464 | tf_op jit(solution)/shard_map/cond/branch_0_fun/ppermute | solution.py:216
  171.5 5.2 %collective-permute-start.15 = (f32[24,512]{1,0:T(8,128)S(1)}, f32[24,512]{1,0:T(8,128)S(1)}, u32[]{:S(2)}, u32[]{:S(2)}) collective-permute-start(f32[24,512]{1,0:T(8,128)S(1)} %collective-permute-done.14.x_ref), channel_id=1, source_target_pairs={{0,144},{2,146},{4,148},{6,150},{8,152},{10,154},{12,156},{14,158}... | collective-permute-start | bytes 147464 | tf_op jit(solution)/shard_map/cond/branch_0_fun/ppermute | solution.py:216
  180.5 13.6 %all_to_all.52.parts_ref = f32[8,24,512]{2,1,0:T(8,128)S(1)} all-to-all(f32[8,24,512]{2,1,0:T(8,128)S(1)} %branch_0_fun.50), channel_id=1, replica_groups=mesh['xh'=2,'zh'=4,'zl'=2,'xl'=2,'y'=4,'rep'=2] {'xl','y'}, dimensions={0} | all-to-all | bytes 786432 | tf_op jit(solution)/shard_map/cond/branch_0_fun/all_to_all | solution.py:220
  196.0 6.5 %collective-permute-done.18.x_ref = f32[24,512]{1,0:T(8,128)S(1)} collective-permute-done((f32[24,512]{1,0:T(8,128)S(1)}, f32[24,512]{1,0:T(8,128)S(1)}, u32[]{:S(2)}, u32[]{:S(2)}) %collective-permute-start.18) | collective-permute-done | bytes 49184 | tf_op jit(solution)/shard_map/cond/branch_0_fun/ppermute | solution.py:216
  202.5 3.8 %collective-permute-start.21 = (f32[24,512]{1,0:T(8,128)S(1)}, f32[24,512]{1,0:T(8,128)S(1)}, u32[]{:S(2)}, u32[]{:S(2)}) collective-permute-start(f32[24,512]{1,0:T(8,128)S(1)} %collective-permute-done.18.x_ref), channel_id=1, source_target_pairs={{0,16},{2,18},{4,20},{6,22},{8,24},{10,26},{12,28},{14,30},{16,0},... | collective-permute-start | bytes 147464 | tf_op jit(solution)/shard_map/cond/branch_0_fun/ppermute | solution.py:216
  208.9 4.3 %collective-permute-start.19 = (f32[24,512]{1,0:T(8,128)S(1)}, f32[24,512]{1,0:T(8,128)S(1)}, u32[]{:S(2)}, u32[]{:S(2)}) collective-permute-start(f32[24,512]{1,0:T(8,128)S(1)} %collective-permute-done.18.x_ref), channel_id=1, source_target_pairs={{0,144},{2,146},{4,148},{6,150},{8,152},{10,154},{12,156},{14,158}... | collective-permute-start | bytes 147464 | tf_op jit(solution)/shard_map/cond/branch_0_fun/ppermute | solution.py:216
  217.9 16.4 %all_to_all.53 = f32[8,24,1024]{2,1,0:T(8,128)S(1)} all-to-all(f32[8,24,1024]{2,1,0:T(8,128)S(1)} %branch_0_fun.55), channel_id=1, replica_groups=mesh['xh'=2,'zh'=4,'zl'=2,'xl'=2,'y'=4,'rep'=2] {'xl','y'}, dimensions={0} | all-to-all | bytes 1572864 | tf_op jit(solution)/shard_map/cond/branch_0_fun/all_to_all | solution.py:220
  (66 shorter events, 59.9 us)
Async XLA Ops:
  0.8 2.6 %collective-permute-start.44 = (f32[8,1024]{1,0:T(8,128)S(1)}, f32[8,1024]{1,0:T(8,128)S(1)}, u32[]{:S(2)}, u32[]{:S(2)}) collective-permute-start(f32[8,1024]{1,0:T(8,128)S(1)} %slice.72), channel_id=1, source_target_pairs={{0,1},{2,3},{4,5},{6,7},{8,9},{10,11},{12,13},{14,15},{16,17},{18,... | collective-permute-start | bytes 98312 | tf_op jit(solution)/shard_map/ppermute | solution.py:267
  4.2 13.9 %collective-permute-start = (f32[24,1024]{1,0:T(8,128)S(1)}, f32[24,1024]{1,0:T(8,128)S(1)}, u32[]{:S(2)}, u32[]{:S(2)}) collective-permute-start(f32[24,1024]{1,0:T(8,128)S(1)} %slice.50.vectors_ref), channel_id=1, source_target_pairs={{0,80},{2,32},{4,0},{6,96},{8,208},{10,160},{12,128},{14,224},{16,... | collective-permute-start | bytes 294920 | tf_op jit(solution)/shard_map/cond/branch_0_fun/ppermute | solution.py:216
  18.1 7.4 %collective-permute-start.1 = (f32[24,1024]{1,0:T(8,128)S(1)}, f32[24,1024]{1,0:T(8,128)S(1)}, u32[]{:S(2)}, u32[]{:S(2)}) collective-permute-start(f32[24,1024]{1,0:T(8,128)S(1)} %collective-permute-done.x_ref), channel_id=1, source_target_pairs={{0,16},{2,18},{4,20},{6,22},{8,24},{10,26},{12,28},{14,30},{16,0},... | collective-permute-start | bytes 294920 | tf_op jit(solution)/shard_map/cond/branch_0_fun/ppermute | solution.py:216
  41.5 9.4 %collective-permute-start.2 = (f32[24,512]{1,0:T(8,128)S(1)}, f32[24,512]{1,0:T(8,128)S(1)}, u32[]{:S(2)}, u32[]{:S(2)}) collective-permute-start(f32[24,512]{1,0:T(8,128)S(1)} %get-tuple-element.28), channel_id=1, source_target_pairs={{0,80},{2,32},{4,0},{6,96},{8,208},{10,160},{12,128},{14,224},{16,... | collective-permute-start | bytes 147464 | tf_op jit(solution)/shard_map/cond/branch_0_fun/ppermute | solution.py:216
  50.9 11.6 %collective-permute-start.5 = (f32[24,512]{1,0:T(8,128)S(1)}, f32[24,512]{1,0:T(8,128)S(1)}, u32[]{:S(2)}, u32[]{:S(2)}) collective-permute-start(f32[24,512]{1,0:T(8,128)S(1)} %collective-permute-done.2.x_ref), channel_id=1, source_target_pairs={{0,16},{2,18},{4,20},{6,22},{8,24},{10,26},{12,28},{14,30},{16,0},... | collective-permute-start | bytes 147464 | tf_op jit(solution)/shard_map/cond/branch_0_fun/ppermute | solution.py:216
  53.9 9.4 %collective-permute-start.4 = (f32[24,512]{1,0:T(8,128)S(1)}, f32[24,512]{1,0:T(8,128)S(1)}, u32[]{:S(2)}, u32[]{:S(2)}) collective-permute-start(f32[24,512]{1,0:T(8,128)S(1)} %collective-permute-done.2.x_ref), channel_id=1, source_target_pairs={{0,128},{2,130},{4,132},{6,134},{8,136},{10,138},{12,140},{14,142}... | collective-permute-start | bytes 147464 | tf_op jit(solution)/shard_map/cond/branch_0_fun/ppermute | solution.py:216
  56.7 8.4 %collective-permute-start.3 = (f32[24,512]{1,0:T(8,128)S(1)}, f32[24,512]{1,0:T(8,128)S(1)}, u32[]{:S(2)}, u32[]{:S(2)}) collective-permute-start(f32[24,512]{1,0:T(8,128)S(1)} %collective-permute-done.2.x_ref), channel_id=1, source_target_pairs={{0,144},{2,146},{4,148},{6,150},{8,152},{10,154},{12,156},{14,158}... | collective-permute-start | bytes 147464 | tf_op jit(solution)/shard_map/cond/branch_0_fun/ppermute | solution.py:216
  81.5 9.3 %collective-permute-start.6 = (f32[24,512]{1,0:T(8,128)S(1)}, f32[24,512]{1,0:T(8,128)S(1)}, u32[]{:S(2)}, u32[]{:S(2)}) collective-permute-start(f32[24,512]{1,0:T(8,128)S(1)} %get-tuple-element.30), channel_id=1, source_target_pairs={{0,80},{2,32},{4,0},{6,96},{8,208},{10,160},{12,128},{14,224},{16,... | collective-permute-start | bytes 147464 | tf_op jit(solution)/shard_map/cond/branch_0_fun/ppermute | solution.py:216
  90.8 11.6 %collective-permute-start.9 = (f32[24,512]{1,0:T(8,128)S(1)}, f32[24,512]{1,0:T(8,128)S(1)}, u32[]{:S(2)}, u32[]{:S(2)}) collective-permute-start(f32[24,512]{1,0:T(8,128)S(1)} %collective-permute-done.6.x_ref), channel_id=1, source_target_pairs={{0,16},{2,18},{4,20},{6,22},{8,24},{10,26},{12,28},{14,30},{16,0},... | collective-permute-start | bytes 147464 | tf_op jit(solution)/shard_map/cond/branch_0_fun/ppermute | solution.py:216
  92.7 10.5 %collective-permute-start.8 = (f32[24,512]{1,0:T(8,128)S(1)}, f32[24,512]{1,0:T(8,128)S(1)}, u32[]{:S(2)}, u32[]{:S(2)}) collective-permute-start(f32[24,512]{1,0:T(8,128)S(1)} %collective-permute-done.6.x_ref), channel_id=1, source_target_pairs={{0,128},{2,130},{4,132},{6,134},{8,136},{10,138},{12,140},{14,142}... | collective-permute-start | bytes 147464 | tf_op jit(solution)/shard_map/cond/branch_0_fun/ppermute | solution.py:216
  95.5 8.6 %collective-permute-start.7 = (f32[24,512]{1,0:T(8,128)S(1)}, f32[24,512]{1,0:T(8,128)S(1)}, u32[]{:S(2)}, u32[]{:S(2)}) collective-permute-start(f32[24,512]{1,0:T(8,128)S(1)} %collective-permute-done.6.x_ref), channel_id=1, source_target_pairs={{0,144},{2,146},{4,148},{6,150},{8,152},{10,154},{12,156},{14,158}... | collective-permute-start | bytes 147464 | tf_op jit(solution)/shard_map/cond/branch_0_fun/ppermute | solution.py:216
  119.3 8.7 %collective-permute-start.10 = (f32[24,512]{1,0:T(8,128)S(1)}, f32[24,512]{1,0:T(8,128)S(1)}, u32[]{:S(2)}, u32[]{:S(2)}) collective-permute-start(f32[24,512]{1,0:T(8,128)S(1)} %get-tuple-element.32), channel_id=1, source_target_pairs={{0,80},{2,32},{4,0},{6,96},{8,208},{10,160},{12,128},{14,224},{16,... | collective-permute-start | bytes 147464 | tf_op jit(solution)/shard_map/cond/branch_0_fun/ppermute | solution.py:216
  128.0 11.6 %collective-permute-start.13 = (f32[24,512]{1,0:T(8,128)S(1)}, f32[24,512]{1,0:T(8,128)S(1)}, u32[]{:S(2)}, u32[]{:S(2)}) collective-permute-start(f32[24,512]{1,0:T(8,128)S(1)} %collective-permute-done.10.x_ref), channel_id=1, source_target_pairs={{0,16},{2,18},{4,20},{6,22},{8,24},{10,26},{12,28},{14,30},{16,0},... | collective-permute-start | bytes 147464 | tf_op jit(solution)/shard_map/cond/branch_0_fun/ppermute | solution.py:216
  131.1 9.3 %collective-permute-start.12 = (f32[24,512]{1,0:T(8,128)S(1)}, f32[24,512]{1,0:T(8,128)S(1)}, u32[]{:S(2)}, u32[]{:S(2)}) collective-permute-start(f32[24,512]{1,0:T(8,128)S(1)} %collective-permute-done.10.x_ref), channel_id=1, source_target_pairs={{0,128},{2,130},{4,132},{6,134},{8,136},{10,138},{12,140},{14,142}... | collective-permute-start | bytes 147464 | tf_op jit(solution)/shard_map/cond/branch_0_fun/ppermute | solution.py:216
  134.1 8.4 %collective-permute-start.11 = (f32[24,512]{1,0:T(8,128)S(1)}, f32[24,512]{1,0:T(8,128)S(1)}, u32[]{:S(2)}, u32[]{:S(2)}) collective-permute-start(f32[24,512]{1,0:T(8,128)S(1)} %collective-permute-done.10.x_ref), channel_id=1, source_target_pairs={{0,144},{2,146},{4,148},{6,150},{8,152},{10,154},{12,156},{14,158}... | collective-permute-start | bytes 147464 | tf_op jit(solution)/shard_map/cond/branch_0_fun/ppermute | solution.py:216
  157.6 8.4 %collective-permute-start.14 = (f32[24,512]{1,0:T(8,128)S(1)}, f32[24,512]{1,0:T(8,128)S(1)}, u32[]{:S(2)}, u32[]{:S(2)}) collective-permute-start(f32[24,512]{1,0:T(8,128)S(1)} %get-tuple-element.34), channel_id=1, source_target_pairs={{0,80},{2,32},{4,0},{6,96},{8,208},{10,160},{12,128},{14,224},{16,... | collective-permute-start | bytes 147464 | tf_op jit(solution)/shard_map/cond/branch_0_fun/ppermute | solution.py:216
  165.9 11.6 %collective-permute-start.17 = (f32[24,512]{1,0:T(8,128)S(1)}, f32[24,512]{1,0:T(8,128)S(1)}, u32[]{:S(2)}, u32[]{:S(2)}) collective-permute-start(f32[24,512]{1,0:T(8,128)S(1)} %collective-permute-done.14.x_ref), channel_id=1, source_target_pairs={{0,16},{2,18},{4,20},{6,22},{8,24},{10,26},{12,28},{14,30},{16,0},... | collective-permute-start | bytes 147464 | tf_op jit(solution)/shard_map/cond/branch_0_fun/ppermute | solution.py:216
  169.6 8.8 %collective-permute-start.16 = (f32[24,512]{1,0:T(8,128)S(1)}, f32[24,512]{1,0:T(8,128)S(1)}, u32[]{:S(2)}, u32[]{:S(2)}) collective-permute-start(f32[24,512]{1,0:T(8,128)S(1)} %collective-permute-done.14.x_ref), channel_id=1, source_target_pairs={{0,128},{2,130},{4,132},{6,134},{8,136},{10,138},{12,140},{14,142}... | collective-permute-start | bytes 147464 | tf_op jit(solution)/shard_map/cond/branch_0_fun/ppermute | solution.py:216
  171.5 8.4 %collective-permute-start.15 = (f32[24,512]{1,0:T(8,128)S(1)}, f32[24,512]{1,0:T(8,128)S(1)}, u32[]{:S(2)}, u32[]{:S(2)}) collective-permute-start(f32[24,512]{1,0:T(8,128)S(1)} %collective-permute-done.14.x_ref), channel_id=1, source_target_pairs={{0,144},{2,146},{4,148},{6,150},{8,152},{10,154},{12,156},{14,158}... | collective-permute-start | bytes 147464 | tf_op jit(solution)/shard_map/cond/branch_0_fun/ppermute | solution.py:216
  194.1 8.4 %collective-permute-start.18 = (f32[24,512]{1,0:T(8,128)S(1)}, f32[24,512]{1,0:T(8,128)S(1)}, u32[]{:S(2)}, u32[]{:S(2)}) collective-permute-start(f32[24,512]{1,0:T(8,128)S(1)} %get-tuple-element.36), channel_id=1, source_target_pairs={{0,80},{2,32},{4,0},{6,96},{8,208},{10,160},{12,128},{14,224},{16,... | collective-permute-start | bytes 147464 | tf_op jit(solution)/shard_map/cond/branch_0_fun/ppermute | solution.py:216
  202.5 11.6 %collective-permute-start.21 = (f32[24,512]{1,0:T(8,128)S(1)}, f32[24,512]{1,0:T(8,128)S(1)}, u32[]{:S(2)}, u32[]{:S(2)}) collective-permute-start(f32[24,512]{1,0:T(8,128)S(1)} %collective-permute-done.18.x_ref), channel_id=1, source_target_pairs={{0,16},{2,18},{4,20},{6,22},{8,24},{10,26},{12,28},{14,30},{16,0},... | collective-permute-start | bytes 147464 | tf_op jit(solution)/shard_map/cond/branch_0_fun/ppermute | solution.py:216
  206.3 8.6 %collective-permute-start.20 = (f32[24,512]{1,0:T(8,128)S(1)}, f32[24,512]{1,0:T(8,128)S(1)}, u32[]{:S(2)}, u32[]{:S(2)}) collective-permute-start(f32[24,512]{1,0:T(8,128)S(1)} %collective-permute-done.18.x_ref), channel_id=1, source_target_pairs={{0,128},{2,130},{4,132},{6,134},{8,136},{10,138},{12,140},{14,142}... | collective-permute-start | bytes 147464 | tf_op jit(solution)/shard_map/cond/branch_0_fun/ppermute | solution.py:216
  208.9 8.4 %collective-permute-start.19 = (f32[24,512]{1,0:T(8,128)S(1)}, f32[24,512]{1,0:T(8,128)S(1)}, u32[]{:S(2)}, u32[]{:S(2)}) collective-permute-start(f32[24,512]{1,0:T(8,128)S(1)} %collective-permute-done.18.x_ref), channel_id=1, source_target_pairs={{0,144},{2,146},{4,148},{6,150},{8,152},{10,154},{12,156},{14,158}... | collective-permute-start | bytes 147464 | tf_op jit(solution)/shard_map/cond/branch_0_fun/ppermute | solution.py:216
  234.4 3.1 %collective-permute-start.45 = (f32[8,1024]{1,0:T(8,128)S(1)}, f32[8,1024]{1,0:T(8,128)S(1)}, u32[]{:S(2)}, u32[]{:S(2)}) collective-permute-start(f32[8,1024]{1,0:T(8,128)S(1)} %get-tuple-element.66), channel_id=1, source_target_pairs={{1,0},{3,2},{5,4},{7,6},{9,8},{11,10},{13,12},{15,14},{17,16},{19,... | collective-permute-start | bytes 98312 | tf_op jit(solution)/shard_map/ppermute | solution.py:279

commit v8 on v7

--- a/solution.py
+++ b/solution.py
@@ -211,9 +211,8 @@
     )(*operands)
 
 
-def permute(value, moves, rep):
-    pairs = [(source * 2 + rep, target * 2 + rep) for source, target in moves]
-    return lax.ppermute(value, ROW + COL + ("rep",), pairs)
+def permute(value, moves):
+    return lax.ppermute(value, ROW + COL, moves)
 
 
 def exchange(value):
@@ -223,18 +222,18 @@
 FLOPS, LIMIT = 100_000_000, 4 << 20
 
 
-def block_product(block, halves, vectors, rep):
+def block_product(block, halves, vectors):
     count, width = block.shape
-    other = permute(block, partner_moves(1), rep)
+    other = permute(block, partner_moves(1))
     out = ((count, width), (count, width // 2))
     total, running = call(own_block_kernel, out, 2 * FLOPS, LIMIT, block, *halves, vectors)
     return call(other_block_kernel, (8, count, width // 2), 2 * FLOPS, LIMIT, other, *halves, total), running
 
 
-def product(piece, halves, rep, scale=None, running=None):
+def product(piece, halves, scale=None, running=None):
     vectors, width = piece.shape
     rows = halves[0].shape[1]
-    others = [permute(piece, partner_moves(which), rep) for which in (1, 2, 3)]
+    others = [permute(piece, partner_moves(which)) for which in (1, 2, 3)]
     total = call(own_kernel, (vectors, rows), FLOPS, LIMIT, piece, *halves)
     for which in (1, 2):
         kernel = functools.partial(next_kernel, which)
@@ -245,19 +244,19 @@
     return call(kernel, (8, vectors, rows), FLOPS, LIMIT, others[2], *halves, total, running)
 
 
-def series(matrix, vectors, rep):
-    block = permute(vectors, owner_moves(), rep)
+def series(matrix, vectors):
+    block = permute(vectors, owner_moves())
     halves = prepare(matrix)
     block, halves = lax.optimization_barrier((block, halves))
-    partial_value, running = block_product(block, halves, vectors, rep)
+    partial_value, running = block_product(block, halves, vectors)
     parts = exchange(partial_value)
     for degree in range(1, TERMS):
         kernel = functools.partial(combine_kernel, float(degree * STEPS))
         summand, running = call(kernel, (running.shape,) * 2, 1_000_000, 2 << 20, parts, running)
-        piece = permute(summand, owner_moves(), rep)
+        piece = permute(summand, owner_moves())
         if degree + 1 < TERMS:
-            parts = exchange(product(piece, halves, rep))
-    parts = exchange(product(piece, halves, rep, float(TERMS * STEPS), running))
+            parts = exchange(product(piece, halves))
+    parts = exchange(product(piece, halves, float(TERMS * STEPS), running))
     return functools.reduce(jnp.add, [parts[part] for part in range(8)])
 
 
@@ -267,11 +266,11 @@
     handed = lax.ppermute(vectors[kept:], "rep", [(0, 1)])
 
     def most(matrix, vectors, handed):
-        result = series(matrix, jnp.concatenate([vectors, handed], axis=0), 1)
+        result = series(matrix, jnp.concatenate([vectors, handed], axis=0))
         return result[:count], result[count:]
 
     def fewer(matrix, vectors, handed):
-        result, handed = lax.optimization_barrier((series(matrix, vectors[:kept], 0), handed))
+        result, handed = lax.optimization_barrier((series(matrix, vectors[:kept]), handed))
         return jnp.concatenate([result, handed], axis=0), handed
 
     takes = lax.axis_index("rep") == 1

time: 241 us -> 202 us (0.84)
  starting transfers between devices: 89.9 us -> 48.8 us
    ppermute x22, starting transfers between devices: 86.9 us -> 45.7 us  [permute(): return lax.ppermute(value, ROW + COL, moves)]
    all_to_all x6, blocking collectives: 89.7 us -> 92.1 us  [exchange(): return lax.all_to_all(value, COL, 0, 0, tiled=True)]
  transfers between devices with their start and end apart: 24 -> 24, of which waited for: 12 -> 16; matrix products, arithmetic and copies ran while one was open for 0% -> 0% of each run, Pallas kernels for 8% -> 9%
where the time goes in v8:
time: 202 us; the launch traced here: 200 us
  blocking collectives  92.1 us (46%)
  starting transfers between devices  48.8 us (24%)
  waiting for transfers between devices  33.5 us (17%)
  Pallas kernels  22.1 us (11%)
    all_to_all x6, blocking collectives, exchange(): return lax.all_to_all(value, COL, 0, 0, tiled=True)  92.1 us
    ppermute x22, starting transfers between devices, permute(): return lax.ppermute(value, ROW + COL, moves)  45.7 us
    ppermute x22, waiting for transfers between devices, permute(): return lax.ppermute(value, ROW + COL, moves)  30.8 us
    pallas_call x27, Pallas kernels, call(): pl.pallas_call(kernel, out_shape=shapes, in_specs=[vmem] * len(operands),...  17.9 us
    pallas_call x1, Pallas kernels, prepare(): pl.pallas_call(prepare_kernel, out_shape=(half, half), in_specs=[pl.Block...  4.29 us
  transfers between devices with their start and end apart: 24, of which 16 were waited for; matrix products, arithmetic and copies ran while one was open for 0% of the time, Pallas kernels for 9%

profile of v8, /device:TPU:2, one launch (start us, length us, event | category | flops | bytes accessed | tf_op | source)
XLA Modules:
  0.0 199.7 jit_solution(17538668655518685208)
XLA Ops:
  3.3 192.6 %conditional.1 = (bf16[32,1024]{1,0:T(8,128)(2,1)S(1)}, f32[8,1024]{1,0:T(8,128)S(1)}, f32[24,1024]{1,0:T(8,128)S(1)}, f32[8,1024]{1,0:T(8,128)S(1)}) conditional(s32[]{:T(128)} %convert_element_type.3, (f32[32,1024]{1,0:T(8,128)}, f32[1024,2048]{1,0:T(8,128)}, f32[8,1024]{1,0:T(8,128)S(1)}) %tuple.18, (f32[32,1024]{1,0:T(8,128)}, ...), branch_computations={%region_0.0_spmd, %region_1.0_spmd} | conditional | flops 6405300224 | bytes 140936080 | solution.py:277
  4.2 7.7 %collective-permute-start = (f32[24,1024]{1,0:T(8,128)S(1)}, f32[24,1024]{1,0:T(8,128)S(1)}, u32[]{:S(2)}, u32[]{:S(2)}) collective-permute-start(f32[24,1024]{1,0:T(8,128)S(1)} %slice.50.vectors_ref), channel_id=1, source_target_pairs={{0,80},{2,32},{4,0},{6,96},{8,208},{10,160},{12,128},{14,224},{16,... | collective-permute-start | bytes 294920 | tf_op jit(solution)/shard_map/cond/branch_0_fun/ppermute | solution.py:215
  11.9 4.3 %branch_0_fun.28 = (bf16[2048,1024]{1,0:T(8,128)(2,1)S(1)}, bf16[2048,1024]{1,0:T(8,128)(2,1)S(1)}) custom-call(f32[1024,2048]{1,0:T(8,128)} %get-tuple-element.20.a_ref), custom_call_target="tpu_custom_call" | custom-call | flops 4000000000 | bytes 8388608 | tf_op jit(solution)/shard_map/cond/branch_0_fun/pallas_call | solution.py:86
  18.5 3.4 %collective-permute-done.1.x_ref = f32[24,1024]{1,0:T(8,128)S(1)} collective-permute-done((f32[24,1024]{1,0:T(8,128)S(1)}, f32[24,1024]{1,0:T(8,128)S(1)}, u32[]{:S(2)}, u32[]{:S(2)}) %collective-permute-start.1) | collective-permute-done | bytes 98336 | tf_op jit(solution)/shard_map/cond/branch_0_fun/ppermute | solution.py:215
  22.9 14.9 %all_to_all.48.parts_ref = f32[8,24,512]{2,1,0:T(8,128)S(1)} all-to-all(f32[8,24,512]{2,1,0:T(8,128)S(1)} %branch_0_fun.30), channel_id=1, replica_groups=mesh['xh'=2,'zh'=4,'zl'=2,'xl'=2,'y'=4,'rep'=2] {'xl','y'}, dimensions={0} | all-to-all | bytes 786432 | tf_op jit(solution)/shard_map/cond/branch_0_fun/all_to_all | solution.py:219
  37.8 5.8 %collective-permute-start.2 = (f32[24,512]{1,0:T(8,128)S(1)}, f32[24,512]{1,0:T(8,128)S(1)}, u32[]{:S(2)}, u32[]{:S(2)}) collective-permute-start(f32[24,512]{1,0:T(8,128)S(1)} %get-tuple-element.28), channel_id=1, source_target_pairs={{0,80},{2,32},{4,0},{6,96},{8,208},{10,160},{12,128},{14,224},{16,... | collective-permute-start | bytes 147464 | tf_op jit(solution)/shard_map/cond/branch_0_fun/ppermute | solution.py:215
  43.5 1.8 collective-permute-done.2.x_ref
  47.3 3.0 %collective-permute-start.3 = (f32[24,512]{1,0:T(8,128)S(1)}, f32[24,512]{1,0:T(8,128)S(1)}, u32[]{:S(2)}, u32[]{:S(2)}) collective-permute-start(f32[24,512]{1,0:T(8,128)S(1)} %collective-permute-done.2.x_ref), channel_id=1, source_target_pairs={{0,144},{2,146},{4,148},{6,150},{8,152},{10,154},{12,156},{14,158}... | collective-permute-start | bytes 147464 | tf_op jit(solution)/shard_map/cond/branch_0_fun/ppermute | solution.py:215
  54.4 15.9 %all_to_all.49.parts_ref = f32[8,24,512]{2,1,0:T(8,128)S(1)} all-to-all(f32[8,24,512]{2,1,0:T(8,128)S(1)} %branch_0_fun.35), channel_id=1, replica_groups=mesh['xh'=2,'zh'=4,'zl'=2,'xl'=2,'y'=4,'rep'=2] {'xl','y'}, dimensions={0} | all-to-all | bytes 786432 | tf_op jit(solution)/shard_map/cond/branch_0_fun/all_to_all | solution.py:219
  70.3 4.1 %collective-permute-start.6 = (f32[24,512]{1,0:T(8,128)S(1)}, f32[24,512]{1,0:T(8,128)S(1)}, u32[]{:S(2)}, u32[]{:S(2)}) collective-permute-start(f32[24,512]{1,0:T(8,128)S(1)} %get-tuple-element.30), channel_id=1, source_target_pairs={{0,80},{2,32},{4,0},{6,96},{8,208},{10,160},{12,128},{14,224},{16,... | collective-permute-start | bytes 147464 | tf_op jit(solution)/shard_map/cond/branch_0_fun/ppermute | solution.py:215
  74.4 3.4 %collective-permute-done.6.x_ref = f32[24,512]{1,0:T(8,128)S(1)} collective-permute-done((f32[24,512]{1,0:T(8,128)S(1)}, f32[24,512]{1,0:T(8,128)S(1)}, u32[]{:S(2)}, u32[]{:S(2)}) %collective-permute-start.6) | collective-permute-done | bytes 49184 | tf_op jit(solution)/shard_map/cond/branch_0_fun/ppermute | solution.py:215
  78.7 4.1 %collective-permute-start.7 = (f32[24,512]{1,0:T(8,128)S(1)}, f32[24,512]{1,0:T(8,128)S(1)}, u32[]{:S(2)}, u32[]{:S(2)}) collective-permute-start(f32[24,512]{1,0:T(8,128)S(1)} %collective-permute-done.6.x_ref), channel_id=1, source_target_pairs={{0,144},{2,146},{4,148},{6,150},{8,152},{10,154},{12,156},{14,158}... | collective-permute-start | bytes 147464 | tf_op jit(solution)/shard_map/cond/branch_0_fun/ppermute | solution.py:215
  85.9 14.7 %all_to_all.50.parts_ref = f32[8,24,512]{2,1,0:T(8,128)S(1)} all-to-all(f32[8,24,512]{2,1,0:T(8,128)S(1)} %branch_0_fun.40), channel_id=1, replica_groups=mesh['xh'=2,'zh'=4,'zl'=2,'xl'=2,'y'=4,'rep'=2] {'xl','y'}, dimensions={0} | all-to-all | bytes 786432 | tf_op jit(solution)/shard_map/cond/branch_0_fun/all_to_all | solution.py:219
  100.6 1.8 collective-permute-start.10
  102.4 5.0 %collective-permute-done.10.x_ref = f32[24,512]{1,0:T(8,128)S(1)} collective-permute-done((f32[24,512]{1,0:T(8,128)S(1)}, f32[24,512]{1,0:T(8,128)S(1)}, u32[]{:S(2)}, u32[]{:S(2)}) %collective-permute-start.10) | collective-permute-done | bytes 49184 | tf_op jit(solution)/shard_map/cond/branch_0_fun/ppermute | solution.py:215
  109.7 2.8 %collective-permute-start.11 = (f32[24,512]{1,0:T(8,128)S(1)}, f32[24,512]{1,0:T(8,128)S(1)}, u32[]{:S(2)}, u32[]{:S(2)}) collective-permute-start(f32[24,512]{1,0:T(8,128)S(1)} %collective-permute-done.10.x_ref), channel_id=1, source_target_pairs={{0,144},{2,146},{4,148},{6,150},{8,152},{10,154},{12,156},{14,158}... | collective-permute-start | bytes 147464 | tf_op jit(solution)/shard_map/cond/branch_0_fun/ppermute | solution.py:215
  116.8 14.5 %all_to_all.51.parts_ref = f32[8,24,512]{2,1,0:T(8,128)S(1)} all-to-all(f32[8,24,512]{2,1,0:T(8,128)S(1)} %branch_0_fun.45), channel_id=1, replica_groups=mesh['xh'=2,'zh'=4,'zl'=2,'xl'=2,'y'=4,'rep'=2] {'xl','y'}, dimensions={0} | all-to-all | bytes 786432 | tf_op jit(solution)/shard_map/cond/branch_0_fun/all_to_all | solution.py:219
  131.6 6.6 %collective-permute-done.14.x_ref = f32[24,512]{1,0:T(8,128)S(1)} collective-permute-done((f32[24,512]{1,0:T(8,128)S(1)}, f32[24,512]{1,0:T(8,128)S(1)}, u32[]{:S(2)}, u32[]{:S(2)}) %collective-permute-start.14) | collective-permute-done | bytes 49184 | tf_op jit(solution)/shard_map/cond/branch_0_fun/ppermute | solution.py:215
  139.7 3.5 %collective-permute-start.15 = (f32[24,512]{1,0:T(8,128)S(1)}, f32[24,512]{1,0:T(8,128)S(1)}, u32[]{:S(2)}, u32[]{:S(2)}) collective-permute-start(f32[24,512]{1,0:T(8,128)S(1)} %collective-permute-done.14.x_ref), channel_id=1, source_target_pairs={{0,144},{2,146},{4,148},{6,150},{8,152},{10,154},{12,156},{14,158}... | collective-permute-start | bytes 147464 | tf_op jit(solution)/shard_map/cond/branch_0_fun/ppermute | solution.py:215
  146.8 14.1 %all_to_all.52.parts_ref = f32[8,24,512]{2,1,0:T(8,128)S(1)} all-to-all(f32[8,24,512]{2,1,0:T(8,128)S(1)} %branch_0_fun.50), channel_id=1, replica_groups=mesh['xh'=2,'zh'=4,'zl'=2,'xl'=2,'y'=4,'rep'=2] {'xl','y'}, dimensions={0} | all-to-all | bytes 786432 | tf_op jit(solution)/shard_map/cond/branch_0_fun/all_to_all | solution.py:219
  161.0 6.5 %collective-permute-done.18.x_ref = f32[24,512]{1,0:T(8,128)S(1)} collective-permute-done((f32[24,512]{1,0:T(8,128)S(1)}, f32[24,512]{1,0:T(8,128)S(1)}, u32[]{:S(2)}, u32[]{:S(2)}) %collective-permute-start.18) | collective-permute-done | bytes 49184 | tf_op jit(solution)/shard_map/cond/branch_0_fun/ppermute | solution.py:215
  170.1 2.4 %collective-permute-start.19 = (f32[24,512]{1,0:T(8,128)S(1)}, f32[24,512]{1,0:T(8,128)S(1)}, u32[]{:S(2)}, u32[]{:S(2)}) collective-permute-start(f32[24,512]{1,0:T(8,128)S(1)} %collective-permute-done.18.x_ref), channel_id=1, source_target_pairs={{0,144},{2,146},{4,148},{6,150},{8,152},{10,154},{12,156},{14,158}... | collective-permute-start | bytes 147464 | tf_op jit(solution)/shard_map/cond/branch_0_fun/ppermute | solution.py:215
  177.2 18.1 %all_to_all.53 = f32[8,24,1024]{2,1,0:T(8,128)S(1)} all-to-all(f32[8,24,1024]{2,1,0:T(8,128)S(1)} %branch_0_fun.55), channel_id=1, replica_groups=mesh['xh'=2,'zh'=4,'zl'=2,'xl'=2,'y'=4,'rep'=2] {'xl','y'}, dimensions={0} | all-to-all | bytes 1572864 | tf_op jit(solution)/shard_map/cond/branch_0_fun/all_to_all | solution.py:219
  197.3 1.8 collective-permute-done.45
  (66 shorter events, 39.0 us)
Async XLA Ops:
  0.8 2.6 %collective-permute-start.44 = (f32[8,1024]{1,0:T(8,128)S(1)}, f32[8,1024]{1,0:T(8,128)S(1)}, u32[]{:S(2)}, u32[]{:S(2)}) collective-permute-start(f32[8,1024]{1,0:T(8,128)S(1)} %slice.72), channel_id=1, source_target_pairs={{0,1},{2,3},{4,5},{6,7},{8,9},{10,11},{12,13},{14,15},{16,17},{18,... | collective-permute-start | bytes 98312 | tf_op jit(solution)/shard_map/ppermute | solution.py:266
  4.2 12.0 %collective-permute-start = (f32[24,1024]{1,0:T(8,128)S(1)}, f32[24,1024]{1,0:T(8,128)S(1)}, u32[]{:S(2)}, u32[]{:S(2)}) collective-permute-start(f32[24,1024]{1,0:T(8,128)S(1)} %slice.50.vectors_ref), channel_id=1, source_target_pairs={{0,80},{2,32},{4,0},{6,96},{8,208},{10,160},{12,128},{14,224},{16,... | collective-permute-start | bytes 294920 | tf_op jit(solution)/shard_map/cond/branch_0_fun/ppermute | solution.py:215
  16.2 5.7 %collective-permute-start.1 = (f32[24,1024]{1,0:T(8,128)S(1)}, f32[24,1024]{1,0:T(8,128)S(1)}, u32[]{:S(2)}, u32[]{:S(2)}) collective-permute-start(f32[24,1024]{1,0:T(8,128)S(1)} %collective-permute-done.x_ref), channel_id=1, source_target_pairs={{0,16},{2,18},{4,20},{6,22},{8,24},{10,26},{12,28},{14,30},{16,0},... | collective-permute-start | bytes 294920 | tf_op jit(solution)/shard_map/cond/branch_0_fun/ppermute | solution.py:215
  37.8 7.5 %collective-permute-start.2 = (f32[24,512]{1,0:T(8,128)S(1)}, f32[24,512]{1,0:T(8,128)S(1)}, u32[]{:S(2)}, u32[]{:S(2)}) collective-permute-start(f32[24,512]{1,0:T(8,128)S(1)} %get-tuple-element.28), channel_id=1, source_target_pairs={{0,80},{2,32},{4,0},{6,96},{8,208},{10,160},{12,128},{14,224},{16,... | collective-permute-start | bytes 147464 | tf_op jit(solution)/shard_map/cond/branch_0_fun/ppermute | solution.py:215
  45.3 5.8 %collective-permute-start.5 = (f32[24,512]{1,0:T(8,128)S(1)}, f32[24,512]{1,0:T(8,128)S(1)}, u32[]{:S(2)}, u32[]{:S(2)}) collective-permute-start(f32[24,512]{1,0:T(8,128)S(1)} %collective-permute-done.2.x_ref), channel_id=1, source_target_pairs={{0,16},{2,18},{4,20},{6,22},{8,24},{10,26},{12,28},{14,30},{16,0},... | collective-permute-start | bytes 147464 | tf_op jit(solution)/shard_map/cond/branch_0_fun/ppermute | solution.py:215
  46.4 6.2 %collective-permute-start.4 = (f32[24,512]{1,0:T(8,128)S(1)}, f32[24,512]{1,0:T(8,128)S(1)}, u32[]{:S(2)}, u32[]{:S(2)}) collective-permute-start(f32[24,512]{1,0:T(8,128)S(1)} %collective-permute-done.2.x_ref), channel_id=1, source_target_pairs={{0,128},{2,130},{4,132},{6,134},{8,136},{10,138},{12,140},{14,142}... | collective-permute-start | bytes 147464 | tf_op jit(solution)/shard_map/cond/branch_0_fun/ppermute | solution.py:215
  47.3 6.5 %collective-permute-start.3 = (f32[24,512]{1,0:T(8,128)S(1)}, f32[24,512]{1,0:T(8,128)S(1)}, u32[]{:S(2)}, u32[]{:S(2)}) collective-permute-start(f32[24,512]{1,0:T(8,128)S(1)} %collective-permute-done.2.x_ref), channel_id=1, source_target_pairs={{0,144},{2,146},{4,148},{6,150},{8,152},{10,154},{12,156},{14,158}... | collective-permute-start | bytes 147464 | tf_op jit(solution)/shard_map/cond/branch_0_fun/ppermute | solution.py:215
  70.3 7.4 %collective-permute-start.6 = (f32[24,512]{1,0:T(8,128)S(1)}, f32[24,512]{1,0:T(8,128)S(1)}, u32[]{:S(2)}, u32[]{:S(2)}) collective-permute-start(f32[24,512]{1,0:T(8,128)S(1)} %get-tuple-element.30), channel_id=1, source_target_pairs={{0,80},{2,32},{4,0},{6,96},{8,208},{10,160},{12,128},{14,224},{16,... | collective-permute-start | bytes 147464 | tf_op jit(solution)/shard_map/cond/branch_0_fun/ppermute | solution.py:215
  77.7 5.8 %collective-permute-start.9 = (f32[24,512]{1,0:T(8,128)S(1)}, f32[24,512]{1,0:T(8,128)S(1)}, u32[]{:S(2)}, u32[]{:S(2)}) collective-permute-start(f32[24,512]{1,0:T(8,128)S(1)} %collective-permute-done.6.x_ref), channel_id=1, source_target_pairs={{0,16},{2,18},{4,20},{6,22},{8,24},{10,26},{12,28},{14,30},{16,0},... | collective-permute-start | bytes 147464 | tf_op jit(solution)/shard_map/cond/branch_0_fun/ppermute | solution.py:215
  77.7 6.7 %collective-permute-start.8 = (f32[24,512]{1,0:T(8,128)S(1)}, f32[24,512]{1,0:T(8,128)S(1)}, u32[]{:S(2)}, u32[]{:S(2)}) collective-permute-start(f32[24,512]{1,0:T(8,128)S(1)} %collective-permute-done.6.x_ref), channel_id=1, source_target_pairs={{0,128},{2,130},{4,132},{6,134},{8,136},{10,138},{12,140},{14,142}... | collective-permute-start | bytes 147464 | tf_op jit(solution)/shard_map/cond/branch_0_fun/ppermute | solution.py:215
  78.7 6.6 %collective-permute-start.7 = (f32[24,512]{1,0:T(8,128)S(1)}, f32[24,512]{1,0:T(8,128)S(1)}, u32[]{:S(2)}, u32[]{:S(2)}) collective-permute-start(f32[24,512]{1,0:T(8,128)S(1)} %collective-permute-done.6.x_ref), channel_id=1, source_target_pairs={{0,144},{2,146},{4,148},{6,150},{8,152},{10,154},{12,156},{14,158}... | collective-permute-start | bytes 147464 | tf_op jit(solution)/shard_map/cond/branch_0_fun/ppermute | solution.py:215
  100.6 6.9 %collective-permute-start.10 = (f32[24,512]{1,0:T(8,128)S(1)}, f32[24,512]{1,0:T(8,128)S(1)}, u32[]{:S(2)}, u32[]{:S(2)}) collective-permute-start(f32[24,512]{1,0:T(8,128)S(1)} %get-tuple-element.32), channel_id=1, source_target_pairs={{0,80},{2,32},{4,0},{6,96},{8,208},{10,160},{12,128},{14,224},{16,... | collective-permute-start | bytes 147464 | tf_op jit(solution)/shard_map/cond/branch_0_fun/ppermute | solution.py:215
  107.5 5.8 %collective-permute-start.13 = (f32[24,512]{1,0:T(8,128)S(1)}, f32[24,512]{1,0:T(8,128)S(1)}, u32[]{:S(2)}, u32[]{:S(2)}) collective-permute-start(f32[24,512]{1,0:T(8,128)S(1)} %collective-permute-done.10.x_ref), channel_id=1, source_target_pairs={{0,16},{2,18},{4,20},{6,22},{8,24},{10,26},{12,28},{14,30},{16,0},... | collective-permute-start | bytes 147464 | tf_op jit(solution)/shard_map/cond/branch_0_fun/ppermute | solution.py:215
  108.5 5.8 %collective-permute-start.12 = (f32[24,512]{1,0:T(8,128)S(1)}, f32[24,512]{1,0:T(8,128)S(1)}, u32[]{:S(2)}, u32[]{:S(2)}) collective-permute-start(f32[24,512]{1,0:T(8,128)S(1)} %collective-permute-done.10.x_ref), channel_id=1, source_target_pairs={{0,128},{2,130},{4,132},{6,134},{8,136},{10,138},{12,140},{14,142}... | collective-permute-start | bytes 147464 | tf_op jit(solution)/shard_map/cond/branch_0_fun/ppermute | solution.py:215
  109.7 6.5 %collective-permute-start.11 = (f32[24,512]{1,0:T(8,128)S(1)}, f32[24,512]{1,0:T(8,128)S(1)}, u32[]{:S(2)}, u32[]{:S(2)}) collective-permute-start(f32[24,512]{1,0:T(8,128)S(1)} %collective-permute-done.10.x_ref), channel_id=1, source_target_pairs={{0,144},{2,146},{4,148},{6,150},{8,152},{10,154},{12,156},{14,158}... | collective-permute-start | bytes 147464 | tf_op jit(solution)/shard_map/cond/branch_0_fun/ppermute | solution.py:215
  131.3 6.9 %collective-permute-start.14 = (f32[24,512]{1,0:T(8,128)S(1)}, f32[24,512]{1,0:T(8,128)S(1)}, u32[]{:S(2)}, u32[]{:S(2)}) collective-permute-start(f32[24,512]{1,0:T(8,128)S(1)} %get-tuple-element.34), channel_id=1, source_target_pairs={{0,80},{2,32},{4,0},{6,96},{8,208},{10,160},{12,128},{14,224},{16,... | collective-permute-start | bytes 147464 | tf_op jit(solution)/shard_map/cond/branch_0_fun/ppermute | solution.py:215
  138.2 5.8 %collective-permute-start.17 = (f32[24,512]{1,0:T(8,128)S(1)}, f32[24,512]{1,0:T(8,128)S(1)}, u32[]{:S(2)}, u32[]{:S(2)}) collective-permute-start(f32[24,512]{1,0:T(8,128)S(1)} %collective-permute-done.14.x_ref), channel_id=1, source_target_pairs={{0,16},{2,18},{4,20},{6,22},{8,24},{10,26},{12,28},{14,30},{16,0},... | collective-permute-start | bytes 147464 | tf_op jit(solution)/shard_map/cond/branch_0_fun/ppermute | solution.py:215
  139.7 5.6 %collective-permute-start.16 = (f32[24,512]{1,0:T(8,128)S(1)}, f32[24,512]{1,0:T(8,128)S(1)}, u32[]{:S(2)}, u32[]{:S(2)}) collective-permute-start(f32[24,512]{1,0:T(8,128)S(1)} %collective-permute-done.14.x_ref), channel_id=1, source_target_pairs={{0,128},{2,130},{4,132},{6,134},{8,136},{10,138},{12,140},{14,142}... | collective-permute-start | bytes 147464 | tf_op jit(solution)/shard_map/cond/branch_0_fun/ppermute | solution.py:215
  139.7 6.5 %collective-permute-start.15 = (f32[24,512]{1,0:T(8,128)S(1)}, f32[24,512]{1,0:T(8,128)S(1)}, u32[]{:S(2)}, u32[]{:S(2)}) collective-permute-start(f32[24,512]{1,0:T(8,128)S(1)} %collective-permute-done.14.x_ref), channel_id=1, source_target_pairs={{0,144},{2,146},{4,148},{6,150},{8,152},{10,154},{12,156},{14,158}... | collective-permute-start | bytes 147464 | tf_op jit(solution)/shard_map/cond/branch_0_fun/ppermute | solution.py:215
  160.9 6.6 %collective-permute-start.18 = (f32[24,512]{1,0:T(8,128)S(1)}, f32[24,512]{1,0:T(8,128)S(1)}, u32[]{:S(2)}, u32[]{:S(2)}) collective-permute-start(f32[24,512]{1,0:T(8,128)S(1)} %get-tuple-element.36), channel_id=1, source_target_pairs={{0,80},{2,32},{4,0},{6,96},{8,208},{10,160},{12,128},{14,224},{16,... | collective-permute-start | bytes 147464 | tf_op jit(solution)/shard_map/cond/branch_0_fun/ppermute | solution.py:215
  167.5 5.8 %collective-permute-start.21 = (f32[24,512]{1,0:T(8,128)S(1)}, f32[24,512]{1,0:T(8,128)S(1)}, u32[]{:S(2)}, u32[]{:S(2)}) collective-permute-start(f32[24,512]{1,0:T(8,128)S(1)} %collective-permute-done.18.x_ref), channel_id=1, source_target_pairs={{0,16},{2,18},{4,20},{6,22},{8,24},{10,26},{12,28},{14,30},{16,0},... | collective-permute-start | bytes 147464 | tf_op jit(solution)/shard_map/cond/branch_0_fun/ppermute | solution.py:215
  169.0 5.6 %collective-permute-start.20 = (f32[24,512]{1,0:T(8,128)S(1)}, f32[24,512]{1,0:T(8,128)S(1)}, u32[]{:S(2)}, u32[]{:S(2)}) collective-permute-start(f32[24,512]{1,0:T(8,128)S(1)} %collective-permute-done.18.x_ref), channel_id=1, source_target_pairs={{0,128},{2,130},{4,132},{6,134},{8,136},{10,138},{12,140},{14,142}... | collective-permute-start | bytes 147464 | tf_op jit(solution)/shard_map/cond/branch_0_fun/ppermute | solution.py:215
  170.1 6.5 %collective-permute-start.19 = (f32[24,512]{1,0:T(8,128)S(1)}, f32[24,512]{1,0:T(8,128)S(1)}, u32[]{:S(2)}, u32[]{:S(2)}) collective-permute-start(f32[24,512]{1,0:T(8,128)S(1)} %collective-permute-done.18.x_ref), channel_id=1, source_target_pairs={{0,144},{2,146},{4,148},{6,150},{8,152},{10,154},{12,156},{14,158}... | collective-permute-start | bytes 147464 | tf_op jit(solution)/shard_map/cond/branch_0_fun/ppermute | solution.py:215
  196.0 3.1 %collective-permute-start.45 = (f32[8,1024]{1,0:T(8,128)S(1)}, f32[8,1024]{1,0:T(8,128)S(1)}, u32[]{:S(2)}, u32[]{:S(2)}) collective-permute-start(f32[8,1024]{1,0:T(8,128)S(1)} %get-tuple-element.66), channel_id=1, source_target_pairs={{1,0},{3,2},{5,4},{7,6},{9,8},{11,10},{13,12},{15,14},{17,16},{19,... | collective-permute-start | bytes 98312 | tf_op jit(solution)/shard_map/ppermute | solution.py:278
